TPU v7x, 8 devices: a whole 2x2x1 slice. The times are simulated.
8 devices in a mesh: data: 2 (over z, y), dap: 4 (over x, core).
Axes of the slice: x: 2, y: 2, z: 1, core: 2. Of those that a mesh axis runs over, the one named last changes fastest.
Arguments:
- pair_z: float32 [24, 256, 256, 64], P('data', 'dap'), parts along dimension 0
- pair_mask: int32 [24, 256, 256], P('data', 'dap'), parts along dimension 0
- out_norm_gain: float32 [64], replicated
- out_norm_bias: float32 [64], replicated
- out_w_a: bfloat16 [64, 64], replicated
- out_w_agate: bfloat16 [64, 64], replicated
- out_w_b: bfloat16 [64, 64], replicated
- out_w_bgate: bfloat16 [64, 64], replicated
- out_w_gate: bfloat16 [64, 64], replicated
- out_x_gain: float32 [64], replicated
- out_x_bias: float32 [64], replicated
- out_w_proj: bfloat16 [64, 64], replicated
- in_norm_gain: float32 [64], replicated
- in_norm_bias: float32 [64], replicated
- in_w_a: bfloat16 [64, 64], replicated
- in_w_agate: bfloat16 [64, 64], replicated
- in_w_b: bfloat16 [64, 64], replicated
- in_w_bgate: bfloat16 [64, 64], replicated
- in_w_gate: bfloat16 [64, 64], replicated
- in_x_gain: float32 [64], replicated
- in_x_bias: float32 [64], replicated
- in_w_proj: bfloat16 [64, 64], replicated
- att_norm_gain: float32 [64], replicated
- att_norm_bias: float32 [64], replicated
- att_w_q: bfloat16 [64, 64], replicated
- att_w_k: bfloat16 [64, 64], replicated
- att_w_v: bfloat16 [64, 64], replicated
- att_w_bias: bfloat16 [64, 4], replicated
- att_w_gate: bfloat16 [64, 64], replicated
- att_w_proj: bfloat16 [64, 64], replicated
Outputs:
- output: float32 [24, 256, 256, 64], P('data', 'dap'), parts along dimension 0
There are 2 independent parts. A program takes and returns all parts, laid end to end along the dimension named above; an argument that names none is the same for every part.
All inputs are finite; a program needn't handle non-finite values.
Results may differ from a plain program's by a relative error of at most 0.00913572.
Values are sent between devices in bfloat16 or wider.
A program may use at most 1 GiB of HBM per device.

v0:
```python
import functools

import jax
import jax.numpy as jnp
from jax import lax
from jax.experimental import pallas as pl
from jax.experimental.pallas import tpu as pltpu
from jax.sharding import PartitionSpec as P


LN_EPS = 1e-5
F32, BF16 = jnp.float32, jnp.bfloat16
ROWS, CH, COLS = 64, 64, 256
TILE = 16
MIB = 1 << 20
OUT, IN, ATT = range(3)


def channel_stats(vals):
    ch_mean = jnp.mean(vals, axis=0, keepdims=True)
    ch_var = jnp.mean(jnp.square(vals - ch_mean), axis=0, keepdims=True)
    return ch_mean, lax.rsqrt(ch_var + LN_EPS)


def channel_norm(vals, norm, stats=None):
    gain, shift = norm
    ch_mean, scale = channel_stats(vals) if stats is None else stats
    return (vals - ch_mean) * scale * gain + shift


def sigmoid(vals):
    return 0.5 * jnp.tanh(0.5 * vals) + 0.5


def swap_major(vals):
    return jnp.swapaxes(vals, 0, 1)


def pair_of(ref, place):
    return ref.at[2 * place], ref.at[2 * place + 1]


def norm_of(ref, place):
    return [part[:] for part in pair_of(ref, place)]


def contract(lhs, rhs, axis_id):
    return lax.dot_general(lhs, rhs, (((axis_id,), (axis_id,)), ((), ())), preferred_element_type=F32)


def mm(lhs, rhs):
    return jnp.dot(lhs, rhs, preferred_element_type=F32)


def opened(gate, product):
    return (jnp.tanh(gate) + 1.0) * product


def row_at(base, i):
    return pl.ds(base + i, 1)


def ab_row(proj, tile_a, tile_b, slot):
    for n, tile in enumerate((tile_a, tile_b)):
        linear, gate = jnp.split(proj[2 * CH * n:2 * CH * n + 2 * CH], 2)
        tile[slot] = opened(gate, linear).astype(BF16)


def x_norm_tile(x_s, tile_x, base, xg, xb):
    parts = [(sub, half) for sub in range(2) for half in range(2)]

    def load(c, part):
        return x_s[c, pl.ds(pl.multiple_of(base + 8 * part[0], 8), 8), 128 * part[1]:128 * part[1] + 128]

    means = [sum(load(c, p) for c in range(CH)) * (1.0 / CH) for p in parts]
    scales = [lax.rsqrt(sum(jnp.square(load(c, p) - means[n]) for c in range(CH)) * (1.0 / CH) + LN_EPS)
              for n, p in enumerate(parts)]
    for c in range(CH):
        rows = []
        for sub in range(2):
            rows.append(jnp.concatenate(
                [(load(c, (sub, half)) - means[2 * sub + half]) * scales[2 * sub + half] * xg[c] + xb[c]
                 for half in range(2)], axis=1))
        tile_x[c] = jnp.concatenate(rows).astype(BF16)


LAG = 3


def staggered(count, *stages):
    held = [{} for _ in stages]
    for tick in range(count + LAG * (len(stages) - 1)):
        for k, stage in enumerate(stages):
            i = tick - LAG * k
            if 0 <= i < count:
                held[k][i] = stage(i, held[k - 1].pop(i) if k else None)


def u_kernel(last, layout, sc, *refs):
    z_refs = refs[:len(layout)]
    n_far = 2 * CHUNKS + 1 if last else 1
    (mask0, mask1, mask2, mask3, norms, xgs, w_ab, w_sq, w_bias, z2_own, z2_par, bias_out, far2, *far3) = refs[len(layout):][:13 + n_far]
    (z_s, a_s, b_s, x_s, mask, stats, tile_a, tile_b, tile_x, tile_c, tile_d, tile_z, in_sem, z_sem, x_sem) = refs[len(layout) + 13 + n_far:]
    me, sample = sc[0], sc[1]
    lanes = pl.ds(pl.multiple_of(LANES * (me // 2), LANES), LANES)
    out_norm = norm_of(norms, OUT)
    in_norm = norm_of(norms, IN)
    att_norm = norm_of(norms, ATT)
    n_tiles = COLS // TILE

    for ref, (r, start) in zip(z_refs, layout):
        src = ref if r else ref.at[sample]
        rows = pl.ds(pl.multiple_of(ROWS * (me ^ r) + start, 8), src.shape[0])
        pltpu.make_async_copy(src, z_s.at[rows], in_sem.at[r]).start()
    for r, part in enumerate((mask0, mask1, mask2, mask3)):
        mask[pl.ds(pl.multiple_of(ROWS * (me ^ r), ROWS), ROWS), :] = part[:].astype(F32)

    def gate_and_product(place, normed, product):
        gate, proj = pair_of(w_sq, place)
        return mm(gate[:], normed), mm(proj[:], product)

    def mask_row(base, i):
        return mask[row_at(base, i), :]

    def measure(base, i, vals=None):
        found = channel_stats(z_s[base + i] if vals is None else vals)
        for n in range(2):
            stats[n if vals is None else n + 2, row_at(base, i), :] = found[n]
        return found

    def recall(base, i, first):
        return [stats[first + n, row_at(base, i), :] for n in range(2)]

    def flush(base):
        a_s[:, pl.ds(base, TILE), :] = swap_major(tile_a[:])
        b_s[:, pl.ds(base, TILE), :] = swap_major(tile_b[:])

    def export(t, start, outgoing, sem):
        r = (t * TILE // ROWS) ^ me
        q = t % (ROWS // TILE)
        rows = pl.ds(pl.multiple_of(TILE * q, TILE), TILE)
        half = pl.ds(pl.multiple_of(ROWS + TILE * (q % 2), TILE), TILE)
        side = pl.ds(pl.multiple_of(LANES * (q // 2), LANES), LANES)
        act = (lambda cp: cp.start()) if start else (lambda cp: cp.wait())
        wide, z_tile = tile_c.at[t % 2], tile_z.at[t % 2]
        narrow = tile_c.at[t % 2, :, :, lanes]
        jobs = [(r == 2, narrow, far2.at[half, :, side])] if outgoing else [
            (r == 0, z_tile, z2_own.at[rows]), (r == 1, z_tile, z2_par.at[rows]), (r == 2, wide, far2.at[rows])]
        if last:
            for n in range(CHUNKS):
                jobs += [((r == 3) & (q == n), narrow, far3[2 * n + 1]) if outgoing else ((r == 3) & (q == n), wide, far3[2 * n])]
            if not outgoing:
                rest = pl.ds(pl.multiple_of(jnp.maximum(q - CHUNKS, 0) * TILE, TILE), TILE)
                jobs += [((r == 3) & (q >= CHUNKS), z_tile, far3[-1].at[rest])]
        else:
            jobs += [(r == 3, narrow, far3[0].at[half, :, side]) if outgoing else (r == 3, wide, far3[0].at[rows])]
        for when, src, dst in jobs:
            @pl.when(when)
            def _():
                act(pltpu.make_async_copy(src, dst, sem.at[t % 2]))

    @pl.loop(0, n_tiles)
    def _(v):
        r = v * TILE // ROWS

        @pl.when(v * TILE % ROWS == 0)
        def _():
            pltpu.make_async_copy(z_refs[0].at[sample], z_s.at[pl.ds(0, ROWS)], in_sem.at[r]).wait()

        base = pl.multiple_of(ROWS * (me ^ r) + v * TILE % ROWS, TILE)
        staggered(
            TILE,
            lambda i, _: mm(w_ab[OUT], (mask_row(base, i) * channel_norm(z_s[base + i], out_norm, measure(base, i))).astype(BF16)),
            lambda i, proj: ab_row(proj, tile_a, tile_b, i))
        flush(base)

    @pl.loop(0, CH, unroll=16)
    def _(c):
        x_s[c] = contract(a_s[c], b_s[c], 1)

    @pl.loop(0, n_tiles)
    def _(t):
        base = pl.multiple_of(TILE * t, TILE)

        @pl.when(t >= 2)
        def _():
            export(t - 2, False, True, x_sem)

        x_norm_tile(x_s, tile_x, base, *pair_of(xgs, OUT))
        tile_c[t % 2] = swap_major(tile_x[:])

        def gate_and_update(i, _):
            normed = channel_norm(z_s[base + i], out_norm, recall(base, i, 0)).astype(BF16)
            return gate_and_product(OUT, normed, tile_c[t % 2, i])

        def next_norm(i, parts):
            z_one = z_s[base + i] + opened(*parts)
            tile_z[0, i] = z_one
            return (mask_row(base, i) * channel_norm(z_one, in_norm, measure(base, i, z_one))).astype(BF16)

        staggered(TILE, gate_and_update, next_norm, lambda i, normed: mm(w_ab[IN], normed),
                  lambda i, proj: ab_row(proj, tile_a, tile_b, i))
        flush(base)
        z_s[pl.ds(base, TILE)] = tile_z[0]
        export(t, True, True, x_sem)

    for t in (n_tiles - 2, n_tiles - 1):
        export(t, False, True, x_sem)

    @pl.loop(0, CH, unroll=16)
    def _(c):
        x_s[c] = contract(a_s[c], b_s[c], 0)

    @pl.loop(0, n_tiles)
    def _(t):
        base = pl.multiple_of(TILE * t, TILE)

        @pl.when(t >= 2)
        def _():
            export(t - 2, False, False, z_sem)

        x_norm_tile(x_s, tile_x, base, *pair_of(xgs, IN))
        tile_c[t % 2] = swap_major(tile_x[:])

        def gate_and_update(i, _):
            normed = channel_norm(z_s[base + i], in_norm, recall(base, i, 2)).astype(BF16)
            return gate_and_product(IN, normed, tile_c[t % 2, i])

        def next_norm(i, parts):
            z_two = z_s[base + i] + opened(*parts)
            tile_z[t % 2, i] = z_two
            return channel_norm(z_two, att_norm).astype(BF16)

        def bias_row(i, normed):
            tile_d[i] = mm(w_bias[:], normed)

        staggered(TILE, gate_and_update, next_norm, bias_row)
        rows = pl.ds(pl.multiple_of(t * TILE % ROWS, TILE), TILE)
        bias_out[t * TILE // ROWS, :, rows, :] = swap_major(tile_d[:])[:4].astype(BF16)
        export(t, True, False, z_sem)

    bias_to = ((far2, 0, 0), (far2, 1, 1), (far2, 3, 2)) if last else ((far2, 0, 0), (far3[0], 1, 0))

    def bias_copy(n):
        dst, block, place = bias_to[n]
        return pltpu.make_async_copy(bias_out.at[me ^ block], dst.at[pl.ds(FAR_BIAS + 4 * place, 4)], in_sem.at[n])

    for n in range(len(bias_to)):
        bias_copy(n).start()
    for t in (n_tiles - 2, n_tiles - 1):
        export(t, False, False, z_sem)
    for n in range(len(bias_to)):
        bias_copy(n).wait()


LANES = 128
VM = pl.BlockSpec(memory_space=pltpu.VMEM)
HB = pl.BlockSpec(memory_space=pltpu.HBM)
SDS = jax.ShapeDtypeStruct
AT_FIRST = lambda i, *_: (i, 0, 0, 0)
SM = pl.BlockSpec(memory_space=pltpu.SMEM)
PARAMS = pltpu.CompilerParams(vmem_limit_bytes=40 * MIB, dimension_semantics=("arbitrary",))
AB_TILE = pltpu.VMEM((TILE, CH, COLS), BF16)
DMA2 = pltpu.SemaphoreType.DMA((2,))
FAR_BIAS = ROWS + ROWS // 2
FAR = SDS((FAR_BIAS + 4, CH, COLS), BF16)
TILE_FULL = SDS((TILE, CH, COLS), BF16)
TILE_HALF = SDS((TILE, CH, LANES), BF16)
CHUNKS = 2
AWAY = SDS((ROWS - CHUNKS * TILE, CH, COLS), F32)
FAR_LAST = SDS((FAR_BIAS + 12, CH, COLS), BF16)
ROW_WIDE = SDS((ROWS, CH, COLS), F32)
SAMPLE_BF = pltpu.VMEM((CH, COLS, COLS), BF16)


def u_call(last, layout, sc, z_parts, masks, norms, xgs, w_ab, w_sq, w_bias):
    return pl.pallas_call(
        functools.partial(u_kernel, last, layout),
        out_shape=(ROW_WIDE, ROW_WIDE, SDS((4, 4, ROWS, COLS), BF16), *((FAR_LAST, *(TILE_FULL, TILE_HALF) * CHUNKS, AWAY) if last else (FAR, FAR))),
        in_specs=[SM] + [HB] * len(layout) + [VM] * 9,
        out_specs=(HB, HB, VM) + (HB,) * (2 * CHUNKS + 2 if last else 2),
        scratch_shapes=[
            pltpu.VMEM((COLS, CH, COLS), F32), SAMPLE_BF, SAMPLE_BF,
            pltpu.VMEM((CH, COLS, COLS), F32), pltpu.VMEM((COLS, COLS), F32), pltpu.VMEM((4, COLS, COLS), F32), AB_TILE, AB_TILE, pltpu.VMEM((CH, TILE, COLS), BF16), pltpu.VMEM((2, TILE, CH, COLS), BF16),
            pltpu.VMEM((TILE, 8, COLS), F32), pltpu.VMEM((2, TILE, CH, COLS), F32),
            pltpu.SemaphoreType.DMA((4,)), DMA2, DMA2,
        ],
        compiler_params=pltpu.CompilerParams(vmem_limit_bytes=62 * MIB),
        name="pair_updates",
    )(sc, *z_parts, *masks, norms, xgs, w_ab, w_sq, w_bias)


def l1_kernel(ids, z_in, mask_in, norms, w_ab, a_out, b_out, mask, tile_a, tile_b):
    out_norm = norm_of(norms, OUT)
    mask[:] = mask_in[0].astype(F32)

    @pl.loop(0, ROWS // TILE)
    def _(t):
        base = pl.multiple_of(TILE * t, TILE)
        staggered(
            TILE,
            lambda i, _: mm(w_ab[OUT], (mask[row_at(base, i), :] * channel_norm(z_in[0, base + i], out_norm)).astype(BF16)),
            lambda i, proj: ab_row(proj, tile_a, tile_b, i))
        a_out[0, :, pl.ds(base, TILE), :] = swap_major(tile_a[:])
        b_out[0, :, pl.ds(base, TILE), :] = swap_major(tile_b[:])


def l1_call(ids, zt, mask, norms, w_ab):
    n = ids.shape[0]
    ab = SDS((n, CH, ROWS, COLS), BF16)
    ab_spec = pl.BlockSpec((1, CH, ROWS, COLS), AT_FIRST)
    return pl.pallas_call(
        l1_kernel,
        out_shape=(ab, ab),
        grid_spec=pltpu.PrefetchScalarGridSpec(
            num_scalar_prefetch=1, grid=(n,),
            in_specs=[pl.BlockSpec((1, ROWS, CH, COLS), lambda i, ids: (ids[i], 0, 0, 0)),
                      pl.BlockSpec((1, ROWS, COLS), lambda i, ids: (ids[i], 0, 0)), VM, VM],
            out_specs=(ab_spec, ab_spec),
            scratch_shapes=[pltpu.VMEM((ROWS, COLS), F32), AB_TILE, AB_TILE]),
        compiler_params=PARAMS,
        name="near_projections",
    )(ids, zt, mask, norms, w_ab)


def l2_kernel(sc, a_in, b_own, b_par, xgs, x_out, x_s, tile_x):
    odd = sc[0] % 2 == 1

    @pl.loop(0, CH, unroll=2)
    def _(c):
        for n in range(2):
            own, par = b_own[n, c].astype(F32), b_par[1 - n, c].astype(F32)
            pair = jnp.concatenate([jnp.where(odd, par, own), jnp.where(odd, own, par)]).astype(BF16)
            x_s[c, :, LANES * n:LANES * n + LANES] = contract(a_in[n, c], pair, 1)

    @pl.loop(0, ROWS // TILE)
    def _(t):
        base = pl.multiple_of(TILE * t, TILE)
        x_norm_tile(x_s, tile_x, base, *pair_of(xgs, OUT))
        both = swap_major(tile_x[:])
        for n in range(2):
            x_out[n, pl.ds(base, TILE)] = both[:, :, LANES * n:LANES * n + LANES]


def l2_call(sc, a_all, b_own, b_par, xgs):
    n = a_all.shape[0]
    ab_spec = pl.BlockSpec((2, CH, ROWS, COLS), AT_FIRST)
    return pl.pallas_call(
        l2_kernel,
        grid=(n // 2,),
        out_shape=SDS((n, ROWS, CH, LANES), BF16),
        in_specs=[SM, ab_spec, ab_spec, ab_spec, VM],
        out_specs=pl.BlockSpec((2, ROWS, CH, LANES), AT_FIRST),
        scratch_shapes=[pltpu.VMEM((CH, ROWS, COLS), F32), pltpu.VMEM((CH, TILE, COLS), BF16)],
        compiler_params=PARAMS,
        name="near_product",
    )(sc, a_all, b_own, b_par, xgs)


def r_kernel(blocks, sc, z_in, x_near, x_far, xi, *refs):
    bias_far, refs = (refs[0], refs[1:]) if blocks else (None, refs)
    norms, w_sq, w_bias, z_out, *refs = refs
    swap, refs = (refs[0], refs[1:]) if blocks else (None, refs)
    tile_d, tile_z, z_buf, sem = refs
    step, steps = pl.program_id(0), pl.num_programs(0)
    first = sc[0] < 2
    out_norm, in_norm, att_norm = [norm_of(norms, place) for place in (OUT, IN, ATT)]

    def z_copy(n):
        return pltpu.make_async_copy(z_buf.at[n % 2], z_out.at[pl.ds(pl.multiple_of(n * TILE, TILE), TILE)], sem.at[n % 2])

    @pl.when(step >= 2)
    def _():
        z_copy(step - 2).wait()

    def gate_and_product(place, normed, product):
        gate, proj = pair_of(w_sq, place)
        return mm(gate[:], normed), mm(proj[:], product)

    def outgoing(i, _):
        near, far = x_near[0, i].astype(F32), x_far[i].astype(F32)
        xn = jnp.concatenate([jnp.where(first, near, far), jnp.where(first, far, near)], axis=1).astype(BF16)
        return gate_and_product(OUT, channel_norm(z_in[0, i], out_norm).astype(BF16), xn)

    def norm_one(i, parts):
        z_one = z_in[0, i] + opened(*parts)
        tile_z[i] = z_one
        return channel_norm(z_one, in_norm).astype(BF16)

    def incoming(i, normed):
        return gate_and_product(IN, normed, xi[i])

    def norm_two(i, parts):
        z_two = tile_z[i] + opened(*parts)
        z_buf[step % 2, i] = z_two
        return channel_norm(z_two, att_norm).astype(BF16) if blocks else None

    def bias_row(i, normed):
        tile_d[i] = mm(w_bias[:], normed)

    staggered(TILE, outgoing, norm_one, incoming, norm_two, *([bias_row] if blocks else []))
    z_copy(step).start()
    if blocks:
        swap[0, :, pl.ds(pl.multiple_of(step * TILE, TILE), TILE), :] = swap_major(tile_d[:])[:4].astype(BF16)

        @pl.when(step == 0)
        def _():
            for n in range(blocks):
                swap[n + 1] = bias_far[4 * n:4 * n + 4]

    @pl.when(step == steps - 1)
    def _():
        @pl.when(steps > 1)
        def _():
            z_copy(step - 1).wait()

        z_copy(step).wait()


def r_call(blocks, start, sc, zt, x_near, x_far, xi, norms, w_sq, w_bias):
    steps = ROWS // TILE if blocks else 1
    far_map = (lambda i, sc: (ROWS // TILE + i % 2, 0, i // 2)) if blocks else (lambda i, sc: (i, 0, 0))
    return pl.pallas_call(
        functools.partial(r_kernel, blocks),
        out_shape=[pltpu.HBM((steps * TILE, CH, COLS), F32)] + [pltpu.HBM((blocks + 1, 4, ROWS, COLS), BF16)] * (blocks > 0),
        grid_spec=pltpu.PrefetchScalarGridSpec(
            num_scalar_prefetch=1, grid=(steps,),
            in_specs=[pl.BlockSpec((1, TILE, CH, COLS), lambda i, sc: (sc[1], start + i, 0, 0)),
                      pl.BlockSpec((1, TILE, CH, LANES), lambda i, sc: (sc[2], start + i, 0, 0)),
                      pl.BlockSpec((TILE, CH, LANES), far_map), pl.BlockSpec((TILE, CH, COLS), lambda i, sc: (i, 0, 0)),
                      *[pl.BlockSpec((4 * blocks, CH, COLS), lambda i, sc: (FAR_BIAS // (4 * blocks), 0, 0))] * (blocks > 0),
                      VM, VM, VM],
            out_specs=[HB] + [pl.BlockSpec((blocks + 1, 4, ROWS, COLS), lambda i, sc: (0, 0, 0, 0))] * (blocks > 0),
            scratch_shapes=[pltpu.VMEM((TILE, 8, COLS), F32), pltpu.VMEM((TILE, CH, COLS), F32),
                            pltpu.VMEM((2, TILE, CH, COLS), F32), DMA2]),
        compiler_params=PARAMS,
        name="row_updates",
    )(sc, zt, x_near, x_far, xi, *[xi] * (blocks > 0), norms, w_sq, w_bias)


HEADS, HEAD = 4, 16
MASK_FILL = -1e9
CHUNK = 32
SLOTS = 2
STEPS = 6
AWAY_FIRST = 24


def attention_kernel(parts, fresh, away, sc, *refs):
    n = len(parts)
    z_refs, bias_refs, (mask_in, norms, w_all, w_proj, *rest) = refs[:n], refs[n:5 * n], refs[5 * n:]
    mask_away, rest = (rest[0], rest[1:]) if away else (None, rest)
    out, *rest = rest if fresh else rest[1:]
    out_away, rest = (rest[:2], rest[2:]) if away else ((), rest)
    (z_in, z_out, mask_i, mask, bias_in, bias_t, q_s, k_s, v_s, g_s, vn_s, gn_s, keep_s, s_buf, e_buf, p_s,
     top_s, inv_s, o_s, m_sem, z_sem, o_sem, b_sem) = rest
    n_rows = sum(size for _, size, _ in parts)
    att_norm = norm_of(norms, 0)

    def rows_of(j):
        return pl.ds(ROWS * j, parts[j][1])

    def own(ref, j):
        return ref.at[sc[j], pl.ds(*parts[j][:2])]

    def z_copy(j):
        return pltpu.make_async_copy(z_refs[j], z_in.at[rows_of(j)], z_sem.at[j])

    def m_copy(j):
        src = mask_away.at[0] if away and j == n - 1 else own(mask_in, j)
        return pltpu.make_async_copy(src, mask_i.at[rows_of(j)], m_sem.at[j])

    def b_copy(j, r):
        rows = pl.ds(pl.multiple_of(ROWS * (sc[n + j] ^ r), ROWS), ROWS)
        return pltpu.make_async_copy(bias_refs[4 * j + r].at[parts[j][2][r]], bias_in.at[j, :, rows], b_sem.at[j])

    def o_copies(j):
        if away and j == n - 1:
            return [pltpu.make_async_copy(z_out.at[pl.ds(ROWS * j + start, ref.shape[0])], ref, o_sem.at[j])
                    for ref, start in zip(out_away, (0, AWAY_FIRST))]
        return [pltpu.make_async_copy(z_out.at[rows_of(j)], own(out, j), o_sem.at[j])]

    starts = [f(j) for j in range(n) for f in (m_copy, *(functools.partial(b_copy, r=r) for r in range(4)))]
    for copy in starts + [z_copy(j) for j in range(n)]:
        copy.start()
    for copy in starts:
        copy.wait()
    mask[:] = mask_i[:].astype(F32)
    q_s[:] = jnp.zeros_like(q_s)

    @pl.loop(0, n * HEADS, unroll=4)
    def _(h):
        bias_t[h // HEADS, h % HEADS] = bias_in[h // HEADS, h % HEADS].astype(F32).T

    z_copy(0).wait()

    def project(row, slot):
        row = jnp.minimum(row, n_rows - 1)
        normed = channel_norm(z_in[row], att_norm).astype(BF16)
        proj = mm(w_all[:], normed)
        k_s[slot] = proj[CH:2 * CH].T.astype(BF16)
        q = proj[:CH].astype(BF16)
        for h in range(HEADS):
            q_s[slot, h, HEAD * h:HEAD * h + HEAD] = q[HEAD * h:HEAD * h + HEAD]
        vn_s[slot] = proj[2 * CH:3 * CH].astype(BF16)
        gn_s[slot] = sigmoid(proj[3 * CH:])

    def keep_mask(row, slot):
        row = jnp.minimum(row, n_rows - 1)
        keep_s[slot] = jnp.broadcast_to(mask[pl.ds(row, 1), :], (LANES, COLS)).T

    def tall(line):
        return jnp.concatenate([line] * (CHUNK // 8))

    def fold(part, op):
        out = part[:8]
        for n in range(1, part.shape[0] // 8):
            out = op(out, part[8 * n:8 * n + 8])
        return out

    def scores(slot, h):
        return mm(k_s[slot], q_s[slot, h])

    def weigh(slot, h, probs):
        heads = slice(HEAD * h, HEAD * h + HEAD)
        o_s[slot, heads] = mm(v_s[slot, heads], probs)

    def step(row, slot, h, logits, defer):
        buf, prev = h % 2, (h + 1) % 2
        sample = jnp.clip(row, 0, n_rows - 1) // ROWS
        top, total, probs = None, None, []
        for c in range(COLS // CHUNK):
            rows = slice(CHUNK * c, CHUNK * c + CHUNK)
            probs.append((e_buf[buf, rows] * tall(inv_s[buf])).astype(BF16))
            exps = jnp.exp(s_buf[prev, rows] - tall(top_s[prev]))
            e_buf[prev, rows] = exps
            part = fold(exps, jnp.add)
            total = part if total is None else total + part
            keep = keep_s[slot, rows]
            keep = jnp.concatenate([keep, keep], axis=1) > 0
            vals = jnp.where(keep, logits[rows] + bias_t[sample, h, rows], MASK_FILL)
            s_buf[buf, rows] = vals
            part = fold(vals, jnp.maximum)
            top = part if top is None else jnp.maximum(top, part)
        top_s[buf] = jnp.broadcast_to(jnp.max(top, axis=0, keepdims=True), (8, COLS))
        inv_s[prev] = jnp.broadcast_to(1.0 / jnp.sum(total, axis=0, keepdims=True), (8, COLS))
        if defer:
            p_s[:] = jnp.concatenate(probs)
        else:
            weigh(1 - slot if h < 2 else slot, (h - 2) % HEADS, jnp.concatenate(probs))

    def finish(row, slot):
        gated = (g_s[slot] * o_s[slot]).astype(BF16)
        z_out[jnp.maximum(row, 0)] = z_in[jnp.clip(row, 0, n_rows - 1)] + mm(w_proj[:], gated)

    project(0, 0)
    keep_mask(0, 0)
    n_steps = (n_rows + 2 + STEPS - 1) // STEPS

    @pl.loop(0, n_steps)
    def _(it):
        first = STEPS * it - 1
        lg = scores(1, 0)
        weigh(0, 1, p_s[:])
        for k in range(STEPS):
            row, slot, last = first + k, 1 - k % 2, k == STEPS - 1
            for h in range(HEADS):
                nxt = scores(slot, h + 1) if h < HEADS - 1 else (None if last else scores(1 - slot, 0))
                if h == 2:
                    project(row + 2, slot)
                step(row, slot, h, lg, last and h == HEADS - 1)
                lg = nxt
                if h == 3:
                    finish(row - 1, 1 - slot)
                    v_s[1 - slot] = vn_s[1 - slot]
                    g_s[1 - slot] = gn_s[1 - slot]
            keep_mask(row + 2, slot)
        for j in range(1, n):
            @pl.when(it == (ROWS * j - 1) // STEPS - 1)
            def _():
                z_copy(j).wait()

            @pl.when(it == (ROWS * j + 1) // STEPS)
            def _():
                for copy in o_copies(j - 1):
                    copy.start()

    for copy in o_copies(n - 1):
        copy.start()
    for j in range(n):
        for copy in o_copies(j):
            copy.wait()


def attend(static, sc, z_parts, biases, mask, norms, w_all, w_proj, out, mask_away=None):
    n, fresh, away = len(z_parts), out is None, mask_away is not None
    z_parts, biases = jax.tree.map(lambda v: pltpu.with_memory_space_constraint(v, pltpu.HBM), (list(z_parts), list(biases)))
    args = (sc, *z_parts, *biases, mask, norms, w_all, w_proj, *[mask_away] * away, *[out] * (not fresh))
    whole = SDS((mask.shape[0], ROWS, CH, COLS), F32)
    aways = [SDS((k, CH, COLS), F32) for k in (AWAY_FIRST, AWAY.shape[0] - AWAY_FIRST)] * away
    rows = sum(z.shape[0] for z in z_parts)
    pair, wide, square, line = [pltpu.VMEM((SLOTS, *shape), dtype) for shape, dtype in (
        ((CH, COLS), BF16), ((CH, COLS), F32), ((COLS, COLS), F32), ((8, COLS), F32))]
    each = [pltpu.VMEM((n, HEADS, COLS, COLS), dtype) for dtype in (BF16, F32)]
    sems = pltpu.SemaphoreType.DMA((n,))
    return pl.pallas_call(
        functools.partial(attention_kernel, static, fresh, away),
        out_shape=(whole, *aways),
        in_specs=[SM] + [HB] * (5 * n + 1) + [VM] * 3 + [HB] * (away + (not fresh)),
        out_specs=(HB,) * (1 + len(aways)),
        scratch_shapes=[
            pltpu.VMEM((rows, CH, COLS), F32), pltpu.VMEM((rows + STEPS, CH, COLS), F32), pltpu.VMEM((rows, COLS), jnp.int32),
            pltpu.VMEM((rows, COLS), F32), *each, pltpu.VMEM((SLOTS, HEADS, CH, COLS), BF16),
            pltpu.VMEM((SLOTS, COLS, CH), BF16), pair, wide, pair, wide, pltpu.VMEM((SLOTS, COLS, LANES), F32),
            square, square, pltpu.VMEM((COLS, COLS), BF16), line, line, wide, sems, sems, sems, sems,
        ],
        compiler_params=pltpu.CompilerParams(vmem_limit_bytes=48 * MIB),
        input_output_aliases={} if fresh else {len(args) - 1: 0},
        name="triangle_attention",
    )(*args)


FIRST = 8


def exchange(values, r):
    return lax.ppermute(values, 'dap', [(i, i ^ r) for i in range(4)])


def update_weights(params):
    norm_gain, norm_bias, w_a, w_agate, w_b, w_bgate, w_gate, x_gain, x_bias, w_proj = params
    half = jnp.bfloat16(0.5)
    wide = lambda v: jnp.broadcast_to(v[:, None], (CH, COLS))
    deep = lambda v: jnp.broadcast_to(v[:, None, None], (CH, 8, 128))
    return ([wide(norm_gain), wide(norm_bias)], [deep(x_gain), deep(x_bias)],
            half * jnp.concatenate([w_a.T, w_agate.T, w_b.T, w_bgate.T]), [half * w_gate.T, half * w_proj.T])


def solution(mesh):
    def local_block(pair_z, pair_mask, *weights):
        me = lax.axis_index('dap')
        zt = jnp.transpose(pair_z, (0, 1, 3, 2))
        n_own = zt.shape[0] // 4
        mask_bf = pair_mask.astype(BF16)
        arrived, layouts, before = [], [], ()
        for t in range(n_own):
            pieces = [(2, 0, FIRST), (2, FIRST, ROWS)] if t == 0 else [(2, 0, ROWS)]
            pieces += [(3, 0, ROWS), (1, 0, ROWS)]
            got = []
            for r, start, stop in pieces:
                where = (n_own * (me ^ r) + t, start, 0, 0)
                send = lax.dynamic_slice(lax.optimization_barrier((zt, *before))[0], where, (1, stop - start, CH, COLS))[0]
                if t == 0 or r == 1:
                    before = (send,)
                got.append(exchange(send, r))
                if t == 0 and stop == ROWS and r == 2:
                    mask_bf, weights = lax.optimization_barrier((mask_bf, weights, send))[:2]
                    masks = [lax.dynamic_slice_in_dim(mask_bf, n_own * (me ^ k), n_own) for k in range(4)]
                    before = (*before, *masks)
                    masks = [exchange(m, k) if k else m for k, m in enumerate(masks)]
            arrived.append([zt, *got])
            layouts.append(((0, 0), *((r, start) for r, start, _ in pieces)))

        out_n, out_x, out_ab, out_sq = update_weights(weights[:10])
        in_n, in_x, in_ab, in_sq = update_weights(weights[10:20])
        att_gain, att_shift, w_q, w_k, w_v, w_bias, w_gate, w_proj = weights[20:]
        att_n = [jnp.broadcast_to(v[:, None], (CH, COLS)) for v in (att_gain, att_shift)]
        norms = jnp.stack(out_n + in_n + att_n)
        xgs = jnp.stack(out_x + in_x)
        w_ab = jnp.stack([out_ab, in_ab])
        w_sq = jnp.stack(out_sq + in_sq)
        w_bias8 = jnp.concatenate([w_bias.T, jnp.zeros((4, CH), BF16)])
        w_all = jnp.concatenate([w_q.T * jnp.bfloat16(HEAD ** -0.5), w_k.T, w_v.T, w_gate.T])
        w_out = w_proj.T
        att_norms = norms[4:]

        token = [None]

        def ordered(call, sc, *args):
            sc = jnp.stack([jnp.asarray(v, jnp.int32) for v in sc])
            if token[0] is not None:
                sc = lax.optimization_barrier((sc, token[0]))[0]
            res = call(sc, *args)
            token[0] = jax.tree.leaves(res)[-1]
            return res

        def attention(jobs, out, mask_away=None):
            samples, orders, z_parts, biases, starts = zip(*jobs)
            static = tuple((start, z.shape[0], tuple(place for _, place in blocks))
                           for start, z, blocks in zip(starts, z_parts, biases))
            arrays = [array for blocks in biases for array, _ in blocks]
            return ordered(functools.partial(attend, static), samples + orders, z_parts, arrays, pair_mask, att_norms,
                           w_all, w_out, out, mask_away)

        far = [(t, r) for t in range(n_own) for r in (2, 3)]
        a_far, b_far = ordered(l1_call, [n_own * (me ^ r) + t for t, r in far], zt, pair_mask, norms, w_ab)
        b_par = exchange(b_far, 1)
        x_near = ordered(l2_call, [me], a_far, b_far, b_par, xgs)

        out = None
        held = []
        for t in range(n_own):
            last = t == n_own - 1
            z_own, z_par, bias, far2, *far3 = ordered(functools.partial(u_call, last, layouts[t]), [me, n_own * me + t],
                                                      arrived[t], [m[t] for m in masks], norms, xgs, w_ab, w_sq, w_bias8)
            here = lambda array: [(array, r) for r in range(4)]
            near = (n_own * (me ^ 1) + t, 0, exchange(z_par, 1), here(exchange(bias, 1)), 0)
            own = (n_own * me + t, 0, z_own, here(bias), 0)
            two = exchange(far2, 2)
            three = [exchange(v, 3) for v in far3[:2 * CHUNKS]]
            held.append((two, three))
            if last:
                out, *away = attention([own, (0, 0, far3[-1], here(bias), 0)], out,
                                       masks[3][t][None, CHUNKS * TILE:].astype(jnp.int32))
                away = [exchange(v, 3) for v in away]
            else:
                out, = attention([own, near], out)

        def rows_of(t, r, blocks, x_far, xi, start=0):
            return ordered(functools.partial(r_call, blocks, start), [me, n_own * (me ^ r) + t, far.index((t, r))],
                           zt, x_near, x_far, xi, norms, w_sq, w_bias8)

        for t in range(n_own - 1):
            two, (three,) = held[t]
            z_two, mine_two = rows_of(t, 2, 1, two, two)
            z_three, mine_three = rows_of(t, 3, 1, three, three)
            par_two, par_three = exchange(mine_two, 1), exchange(mine_three, 1)
            jobs = [(n_own * (me ^ r) + t, me, z, [(mine, 0), (par, 0), (mine, 1), (par, 1)], 0)
                    for r, z, mine, par in ((2, z_two, mine_two, par_three), (3, z_three, mine_three, par_two))]
            out, = attention(([] if t else [near]) + jobs, out)
        two, three = held[t + 1]
        z_two, mine = rows_of(t + 1, 2, 3, two, two)
        par = exchange(mine, 1)
        jobs = [(n_own * (me ^ 2) + t + 1, me, z_two, [(mine, k) for k in (0, 3, 1, 2)], 0)]
        for n in range(CHUNKS):
            z_three, = rows_of(t + 1, 3, 0, three[2 * n + 1], three[2 * n], n)
            jobs += [(n_own * (me ^ 3) + t + 1, me, z_three, [(par, k) for k in (3, 0, 2, 1)], n * TILE)]
            out, = attention(jobs, out)
            jobs = []
        for v, start in zip(away, (CHUNKS * TILE, CHUNKS * TILE + AWAY_FIRST)):
            out = lax.dynamic_update_slice(out, v[None], (n_own * (me ^ 3) + n_own - 1, start, 0, 0))
        return jnp.transpose(out, (0, 1, 3, 2))

    pair_spec = P('data', 'dap')
    return jax.shard_map(local_block, mesh=mesh, in_specs=(pair_spec, pair_spec) + (P(),) * 28,
                         out_specs=pair_spec, check_vma=False)
```

profile of v0, /device:TPU:0, one launch (start us, length us, event | category | flops | bytes accessed | tf_op | source)
XLA Modules:
  0.0 1308.6 jit_solution(4644707113579389523)
XLA Ops:
  0.0 1.2 dynamic-slice_bitcast_fusion.9
  1.3 4.4 dynamic-slice_bitcast_fusion.8
  7.4 28.7 %near_projections.1 = (bf16[6,64,64,256]{3,2,1,0:T(8,128)(2,1)S(1)}, bf16[6,64,64,256]{3,2,1,0:T(8,128)(2,1)}) custom-call(s32[6]{0:T(128)S(1)} %stack.182.ids, f32[12,64,64,256]{3,2,1,0:T(8,128)} %bitcast.121, s32[12,64,256]{2,1,0:T(8,128)S(1)} %copy-done.2, f32[6,64,256]{2,1,0:T(8,128)S(1)} %broadcast_dynamic-update-slice_fusion.norms.refs_9_.refs_8_.refs_1_.refs_0_, ...), custom_call_target="tpu_custom_call" | custom-call | tf_op jit(solution)/shard_map/near_projections/pallas_call | solution.py:312
  36.1 4.6 copy-done.6
  40.6 0.8 collective-permute-start
  41.5 4.6 dynamic-slice_bitcast_fusion.7
  46.2 4.7 dynamic-slice_bitcast_fusion.6
  51.0 2.6 collective-permute-start.3
  53.9 1.5 collective-permute-start.7
  57.0 0.8 dynamic-slice_bitcast_fusion.10
  57.8 167.5 %collective-permute-done.7 = bf16[3,64,256]{2,1,0:T(8,128)(2,1)S(1)} collective-permute-done((bf16[3,64,256]{2,1,0:T(8,128)(2,1)S(1)}, bf16[3,64,256]{2,1,0:T(8,128)(2,1)S(1)}, u32[]{:S(2)}, u32[]{:S(2)}) %collective-permute-start.7) | collective-permute-done | bytes 98336 | tf_op jit(solution)/shard_map/ppermute | solution.py:627
  225.3 2.3 collective-permute-start.6
  228.2 2.4 collective-permute-done.6
  231.3 0.7 collective-permute-done.5
  232.0 1.7 collective-permute-start.1
  235.7 33.0 %near_product.1.x_near = bf16[6,64,64,128]{3,2,1,0:T(8,128)(2,1)S(1)} custom-call(s32[1]{0:T(128)} %bitcast.1.sc, bf16[6,64,64,256]{3,2,1,0:T(8,128)(2,1)} %copy-done.6, bf16[6,64,64,256]{3,2,1,0:T(8,128)(2,1)} %get-tuple-element.106.b_own, bf16[6,64,64,256]{3,2,1,0:T(8,128)(2,1)} %collective-permute-done.b_par, ...), custom_call_target="tpu_custom_call" | custom-call | tf_op jit(solution)/shard_map/near_product/pallas_call | solution.py:348
  268.7 2.6 copy-done
  271.3 0.8 copy-done.27
  272.1 87.6 %pair_updates.3 = (f32[64,64,256]{2,1,0:T(8,128)}, f32[64,64,256]{2,1,0:T(8,128)}, bf16[4,4,64,256]{3,2,1,0:T(8,128)(2,1)}, bf16[100,64,256]{2,1,0:T(8,128)(2,1)}, bf16[100,64,256]{2,1,0:T(8,128)(2,1)}) custom-call(s32[2]{0:T(128)} %pad_add_fusion.12.sc, f32[12,64,64,256]{3,2,1,0:T(8,128)} %bitcast.124, f32[8,64,256]{2,1,0:T(8,128)} %copy-done.27, ...), custom_call_target="tpu_custom_call" | custom-call | tf_op jit(solution)/shard_map/pair_updates/pallas_call | solution.py:277
  359.8 9.8 dynamic-slice_bitcast_fusion.3
  369.6 1.8 collective-permute-start.11
  373.4 6.1 collective-permute-done.9.refs_6_.refs_7_.refs_8_.refs_9_
  379.5 0.8 copy-done.19
  380.3 65.2 %triangle_attention.7.refs_14_ = f32[12,64,64,256]{3,2,1,0:T(8,128)} custom-call(s32[4]{0:T(128)S(1)} %get-tuple-element.123.sc, f32[64,64,256]{2,1,0:T(8,128)} %get-tuple-element.124.refs_0_, f32[64,64,256]{2,1,0:T(8,128)} %collective-permute-done.8.refs_1_, bf16[4,4,64,256]{3,2,1,0:T(8,128)(2,1)} %get-tuple-element.126.refs_2_.refs_3_.refs_4_.refs_5_, ...), custom_call_target="tpu_custom_call" | custom-call | tf_op jit(solution)/shard_map/triangle_attention/pallas_call | solution.py:606
  445.5 17.9 %collective-permute-done.10.refs_1_ = f32[64,64,256]{2,1,0:T(8,128)} collective-permute-done((f32[64,64,256]{2,1,0:T(8,128)}, f32[64,64,256]{2,1,0:T(8,128)}, u32[]{:S(2)}, u32[]{:S(2)}) %collective-permute-start.10) | collective-permute-done | bytes 4194336 | tf_op jit(solution)/shard_map/ppermute | solution.py:627
  463.4 88.8 %collective-permute-done.11.refs_2_ = f32[64,64,256]{2,1,0:T(8,128)} collective-permute-done((f32[64,64,256]{2,1,0:T(8,128)}, f32[64,64,256]{2,1,0:T(8,128)}, u32[]{:S(2)}, u32[]{:S(2)}) %collective-permute-start.11) | collective-permute-done | bytes 4194336 | tf_op jit(solution)/shard_map/ppermute | solution.py:627
  552.2 87.6 %pair_updates.4 = (f32[64,64,256]{2,1,0:T(8,128)}, f32[64,64,256]{2,1,0:T(8,128)}, bf16[4,4,64,256]{3,2,1,0:T(8,128)(2,1)}, bf16[100,64,256]{2,1,0:T(8,128)(2,1)}, bf16[100,64,256]{2,1,0:T(8,128)(2,1)}) custom-call(s32[2]{0:T(128)} %pad_add_fusion.11.sc, f32[12,64,64,256]{3,2,1,0:T(8,128)} %bitcast.126, f32[64,64,256]{2,1,0:T(8,128)} %collective-permute-done.10.refs_1_, ...), custom_call_target="tpu_custom_call" | custom-call | tf_op jit(solution)/shard_map/pair_updates/pallas_call | solution.py:277
  640.1 9.8 dynamic-slice_bitcast_fusion
  650.0 1.6 collective-permute-start.16
  652.1 7.5 collective-permute-done.14.refs_6_.refs_7_.refs_8_.refs_9_
  659.9 1.5 collective-permute-start.19
  661.4 0.7 pad_add_fusion.10.sc
  662.0 65.4 %triangle_attention.8.refs_15_ = f32[12,64,64,256]{3,2,1,0:T(8,128)} custom-call(s32[4]{0:T(128)S(1)} %get-tuple-element.135.sc, f32[64,64,256]{2,1,0:T(8,128)} %get-tuple-element.136.refs_0_, f32[64,64,256]{2,1,0:T(8,128)} %collective-permute-done.13.refs_1_, ...), custom_call_target="tpu_custom_call", output_to_operand_aliasing={{}: (15, {})} | custom-call | tf_op jit(solution)/shard_map/triangle_attention/pallas_call | solution.py:606
  727.4 16.3 %collective-permute-done.15.refs_1_ = f32[64,64,256]{2,1,0:T(8,128)} collective-permute-done((f32[64,64,256]{2,1,0:T(8,128)}, f32[64,64,256]{2,1,0:T(8,128)}, u32[]{:S(2)}, u32[]{:S(2)}) %collective-permute-start.15) | collective-permute-done | bytes 4194336 | tf_op jit(solution)/shard_map/ppermute | solution.py:627
  743.7 88.4 %collective-permute-done.16.refs_2_ = f32[64,64,256]{2,1,0:T(8,128)} collective-permute-done((f32[64,64,256]{2,1,0:T(8,128)}, f32[64,64,256]{2,1,0:T(8,128)}, u32[]{:S(2)}, u32[]{:S(2)}) %collective-permute-start.16) | collective-permute-done | bytes 4194336 | tf_op jit(solution)/shard_map/ppermute | solution.py:627
  832.1 87.2 %pair_updates.5 = (f32[64,64,256]{2,1,0:T(8,128)}, f32[64,64,256]{2,1,0:T(8,128)}, bf16[4,4,64,256]{3,2,1,0:T(8,128)(2,1)}, bf16[108,64,256]{2,1,0:T(8,128)(2,1)...) custom-call(s32[2]{0:T(128)} %pad_add_fusion.10.sc, ...), custom_call_target="tpu_custom_call" | custom-call | tf_op jit(solution)/shard_map/pair_updates/pallas_call | solution.py:277
  919.3 1.8 collective-permute-start.20
  921.2 1.4 collective-permute-start.25
  923.4 51.3 %triangle_attention.9 = (f32[12,64,64,256]{3,2,1,0:T(8,128)}, f32[24,64,256]{2,1,0:T(8,128)}, f32[8,64,256]{2,1,0:T(8,128)S(1)}) custom-call(s32[4]{0:T(128)S(1)} %get-tuple-element.142.sc, f32[64,64,256]{2,1,0:T(8,128)} %get-tuple-element.143.refs_0_, f32[32,64,256]{2,1,0:T(8,128)} %get-tuple-element.141.refs_1_, ...), custom_call_target="tpu_custom_call", output_to_operand_aliasing={{0}: (16, {})} | custom-call | tf_op jit(solution)/shard_map/triangle_attention/pallas_call | solution.py:606
  974.7 2.9 copy-done.1
  977.7 10.9 row_updates.7
  988.6 10.9 row_updates.8
  999.7 1.6 collective-permute-done.22.refs_8_.refs_10_
  1001.4 1.4 collective-permute-done.23.refs_12_.refs_14_
  1003.0 1.8 collective-permute-done.21.refs_3_.refs_4_.refs_5_.refs_6_
  1004.7 0.8 copy-done.18
  1005.5 1.5 collective-permute-start.34
  1008.4 95.2 %triangle_attention.10.refs_14_ = f32[12,64,64,256]{3,2,1,0:T(8,128)} custom-call(s32[6]{0:T(128)S(1)} %copy-done.11, f32[64,64,256]{2,1,0:T(8,128)} %collective-permute-done.20.refs_0_, f32[64,64,256]{2,1,0:T(8,128)} %get-tuple-element.153.refs_1_, f32[64,64,256]{2,1,0:T(8,128)} %get-tuple-element.154.refs_2_, ...), custom_call_target="tpu_custom_call", output_to_operand_aliasing={{}: (20, {})} | custom-call | tf_op jit(solution)/shard_map/triangle_attention/pallas_call | solution.py:606
  1103.7 10.7 row_updates.9
  1114.4 10.7 row_updates.10
  1125.9 0.9 collective-permute-done.26.refs_3_.refs_5_
  1127.5 0.7 copy-done.26
  1128.2 65.2 %triangle_attention.11.refs_14_ = f32[12,64,64,256]{3,2,1,0:T(8,128)} custom-call(s32[4]{0:T(128)S(1)} %add_add_fusion.1.sc, f32[64,64,256]{2,1,0:T(8,128)} %get-tuple-element.162.refs_0_, f32[64,64,256]{2,1,0:T(8,128)} %get-tuple-element.163.refs_1_, bf16[2,4,64,256]{3,2,1,0:T(8,128)(2,1)} %get-tuple-element.158.refs_2_.refs_4_, ...), custom_call_target="tpu_custom_call", output_to_operand_aliasing={{}: (15, {})} | custom-call | tf_op jit(solution)/shard_map/triangle_attention/pallas_call | solution.py:606
  1193.5 10.9 row_updates.11
  1204.5 1.1 collective-permute-start.33
  1205.6 33.6 %collective-permute-done.29.x_far = bf16[16,64,128]{2,1,0:T(8,128)(2,1)S(1)} collective-permute-done((bf16[16,64,128]{2,1,0:T(8,128)(2,1)S(1)}, bf16[16,64,128]{2,1,0:T(8,128)(2,1)S(1)}, u32[]{:S(2)}, u32[]{:S(2)}) %collective-permute-start.29) | collective-permute-done | bytes 262176 | tf_op jit(solution)/shard_map/ppermute | solution.py:627
  1239.3 1.3 collective-permute-start.32
  1241.3 4.1 row_updates.12.refs_1_
  1245.4 0.8 copy-done.15
  1246.2 42.5 %triangle_attention.12.refs_9_ = f32[12,64,64,256]{3,2,1,0:T(8,128)} custom-call(s32[4]{0:T(128)S(1)} %add_add_fusion.sc, f32[64,64,256]{2,1,0:T(8,128)} %get-tuple-element.171.refs_0_, f32[16,64,256]{2,1,0:T(8,128)} %row_updates.12.refs_1_, ...), custom_call_target="tpu_custom_call", output_to_operand_aliasing={{}: (15, {})} | custom-call | tf_op jit(solution)/shard_map/triangle_attention/pallas_call | solution.py:606
  1288.7 4.2 row_updates.13.refs_0_
  1292.9 11.6 triangle_attention.13
  1304.6 2.7 bitcast_dynamic-update-slice_fusion
  1307.3 0.8 bitcast_dynamic-update-slice_fusion.1
  (222 shorter events, 15.0 us)
Async XLA Ops:
  6.9 29.2 %copy-start.8 = (bf16[2,256,64]{2,1,0:T(8,128)(2,1)}, bf16[2,256,64]{2,1,0:T(8,128)(2,1)S(1)}, u32[]{:S(2)}) copy-start(bf16[2,256,64]{2,1,0:T(8,128)(2,1)S(1)} %pad_maximum_fusion.1.w_ab.refs_11_.refs_10_) | copy-start | bytes 196612
  7.3 28.8 %copy-start.3 = (f32[6,64,256]{2,1,0:T(8,128)}, f32[6,64,256]{2,1,0:T(8,128)S(1)}, u32[]{:S(2)}) copy-start(f32[6,64,256]{2,1,0:T(8,128)S(1)} %broadcast_dynamic-update-slice_fusion.norms.refs_9_.refs_8_.refs_1_.refs_0_) | copy-start | bytes 1179652
  40.6 195.0 %collective-permute-start = (bf16[6,64,64,256]{3,2,1,0:T(8,128)(2,1)}, bf16[6,64,64,256]{3,2,1,0:T(8,128)(2,1)}, u32[]{:S(2)}, u32[]{:S(2)}) collective-permute-start(bf16[6,64,64,256]{3,2,1,0:T(8,128)(2,1)} %get-tuple-element.106.b_own), channel_id=1, source_target_pairs={{0,1},{1,0},{2,3},{3,2},{4,5},{5,4},{6,7},{7,6}} | collective-permute-start | bytes 37748744 | tf_op jit(solution)/shard_map/ppermute | solution.py:627
  46.2 10.3 copy-start.53
  46.2 10.5 copy-start.54
  46.2 10.6 copy-start.55
  51.0 220.3 %collective-permute-start.4 = (f32[64,64,256]{2,1,0:T(8,128)}, f32[64,64,256]{2,1,0:T(8,128)}, u32[]{:S(2)}, u32[]{:S(2)}) collective-permute-start(f32[64,64,256]{2,1,0:T(8,128)} %dynamic-slice_bitcast_fusion.6), channel_id=1, source_target_pairs={{0,1},{1,0},{2,3},{3,2},{4,5},{5,4},{6,7},{7,6}} | collective-permute-start | bytes 12582920 | tf_op jit(solution)/shard_map/ppermute | solution.py:627
  51.0 220.3 %collective-permute-start.3 = (f32[64,64,256]{2,1,0:T(8,128)}, f32[64,64,256]{2,1,0:T(8,128)}, u32[]{:S(2)}, u32[]{:S(2)}) collective-permute-start(f32[64,64,256]{2,1,0:T(8,128)} %dynamic-slice_bitcast_fusion.7), channel_id=1, source_target_pairs={{0,3},{1,2},{2,1},{3,0},{4,7},{5,6},{6,5},{7,4}} | collective-permute-start | bytes 12582920 | tf_op jit(solution)/shard_map/ppermute | solution.py:627
  53.5 217.7 %collective-permute-start.2 = (f32[56,64,256]{2,1,0:T(8,128)}, f32[56,64,256]{2,1,0:T(8,128)}, u32[]{:S(2)}, u32[]{:S(2)}) collective-permute-start(f32[56,64,256]{2,1,0:T(8,128)} %dynamic-slice_bitcast_fusion.8), channel_id=1, source_target_pairs={{0,2},{1,3},{2,0},{3,1},{4,6},{5,7},{6,4},{7,5}} | collective-permute-start | bytes 11010056 | tf_op jit(solution)/shard_map/ppermute | solution.py:627
  53.9 171.4 %collective-permute-start.7 = (bf16[3,64,256]{2,1,0:T(8,128)(2,1)S(1)}, bf16[3,64,256]{2,1,0:T(8,128)(2,1)S(1)}, u32[]{:S(2)}, u32[]{:S(2)}) collective-permute-start(bf16[3,64,256]{2,1,0:T(8,128)(2,1)S(1)} %get-tuple-element.186), channel_id=1, source_target_pairs={{0,3},{1,2},{2,1},{3,0},{4,7},{5,6},{6,5},{7,4}} | collective-permute-start | bytes 294920 | tf_op jit(solution)/shard_map/ppermute | solution.py:627
  57.0 211.7 %copy-start.5 = (f32[4,64,8,128]{3,2,1,0:T(8,128)}, f32[4,64,8,128]{3,2,1,0:T(8,128)S(1)}, u32[]{:S(2)}) copy-start(f32[4,64,8,128]{3,2,1,0:T(8,128)S(1)} %pad_maximum_fusion.xgs.refs_10_.refs_9_) | copy-start | bytes 3145732
  225.3 5.4 collective-permute-start.6
  230.7 1.3 collective-permute-start.5
  232.0 39.3 %collective-permute-start.1 = (f32[8,64,256]{2,1,0:T(8,128)S(1)}, f32[8,64,256]{2,1,0:T(8,128)S(1)}, u32[]{:S(2)}, u32[]{:S(2)}) collective-permute-start(f32[8,64,256]{2,1,0:T(8,128)S(1)} %dynamic-slice_bitcast_fusion.9), channel_id=1, source_target_pairs={{0,2},{1,3},{2,0},{3,1},{4,6},{5,7},{6,4},{7,5}} | collective-permute-start | bytes 1572872 | tf_op jit(solution)/shard_map/ppermute | solution.py:627
  359.7 12.1 copy-start.40
  359.7 12.2 copy-start.41
  359.7 12.3 copy-start.42
  359.7 12.3 copy-start.43
  359.7 12.4 copy-start.44
  359.8 12.6 copy-start.17
  359.8 19.8 %collective-permute-start.8 = (f32[64,64,256]{2,1,0:T(8,128)}, f32[64,64,256]{2,1,0:T(8,128)}, u32[]{:S(2)}, u32[]{:S(2)}) collective-permute-start(f32[64,64,256]{2,1,0:T(8,128)} %get-tuple-element.125), channel_id=1, source_target_pairs={{0,1},{1,0},{2,3},{3,2},{4,5},{5,4},{6,7},{7,6}} | collective-permute-start | bytes 12582920 | tf_op jit(solution)/shard_map/ppermute | solution.py:627
  369.6 93.8 %collective-permute-start.10 = (f32[64,64,256]{2,1,0:T(8,128)}, f32[64,64,256]{2,1,0:T(8,128)}, u32[]{:S(2)}, u32[]{:S(2)}) collective-permute-start(f32[64,64,256]{2,1,0:T(8,128)} %get-tuple-element.182), channel_id=1, source_target_pairs={{0,2},{1,3},{2,0},{3,1},{4,6},{5,7},{6,4},{7,5}} | collective-permute-start | bytes 12582920 | tf_op jit(solution)/shard_map/ppermute | solution.py:627
  369.6 182.6 %collective-permute-start.11 = (f32[64,64,256]{2,1,0:T(8,128)}, f32[64,64,256]{2,1,0:T(8,128)}, u32[]{:S(2)}, u32[]{:S(2)}) collective-permute-start(f32[64,64,256]{2,1,0:T(8,128)} %get-tuple-element.181), channel_id=1, source_target_pairs={{0,3},{1,2},{2,1},{3,0},{4,7},{5,6},{6,5},{7,4}} | collective-permute-start | bytes 12582920 | tf_op jit(solution)/shard_map/ppermute | solution.py:627
  371.4 180.8 %collective-permute-start.12 = (f32[64,64,256]{2,1,0:T(8,128)}, f32[64,64,256]{2,1,0:T(8,128)}, u32[]{:S(2)}, u32[]{:S(2)}) collective-permute-start(f32[64,64,256]{2,1,0:T(8,128)} %get-tuple-element.180), channel_id=1, source_target_pairs={{0,1},{1,0},{2,3},{3,2},{4,5},{5,4},{6,7},{7,6}} | collective-permute-start | bytes 12582920 | tf_op jit(solution)/shard_map/ppermute | solution.py:627
  372.4 7.2 collective-permute-start.9
  639.8 20.1 %collective-permute-start.13 = (f32[64,64,256]{2,1,0:T(8,128)}, f32[64,64,256]{2,1,0:T(8,128)}, u32[]{:S(2)}, u32[]{:S(2)}) collective-permute-start(f32[64,64,256]{2,1,0:T(8,128)} %get-tuple-element.137), channel_id=1, source_target_pairs={{0,1},{1,0},{2,3},{3,2},{4,5},{5,4},{6,7},{7,6}} | collective-permute-start | bytes 12582920 | tf_op jit(solution)/shard_map/ppermute | solution.py:627
  640.1 12.0 copy-start.16
  650.0 93.8 %collective-permute-start.15 = (f32[64,64,256]{2,1,0:T(8,128)}, f32[64,64,256]{2,1,0:T(8,128)}, u32[]{:S(2)}, u32[]{:S(2)}) collective-permute-start(f32[64,64,256]{2,1,0:T(8,128)} %get-tuple-element.179), channel_id=1, source_target_pairs={{0,2},{1,3},{2,0},{3,1},{4,6},{5,7},{6,4},{7,5}} | collective-permute-start | bytes 12582920 | tf_op jit(solution)/shard_map/ppermute | solution.py:627
  650.0 182.1 %collective-permute-start.16 = (f32[64,64,256]{2,1,0:T(8,128)}, f32[64,64,256]{2,1,0:T(8,128)}, u32[]{:S(2)}, u32[]{:S(2)}) collective-permute-start(f32[64,64,256]{2,1,0:T(8,128)} %get-tuple-element.178), channel_id=1, source_target_pairs={{0,3},{1,2},{2,1},{3,0},{4,7},{5,6},{6,5},{7,4}} | collective-permute-start | bytes 12582920 | tf_op jit(solution)/shard_map/ppermute | solution.py:627
  651.5 180.6 %collective-permute-start.17 = (f32[64,64,256]{2,1,0:T(8,128)S(1)}, f32[64,64,256]{2,1,0:T(8,128)}, u32[]{:S(2)}, u32[]{:S(2)}) collective-permute-start(f32[64,64,256]{2,1,0:T(8,128)S(1)} %get-tuple-element.177), channel_id=1, source_target_pairs={{0,1},{1,0},{2,3},{3,2},{4,5},{5,4},{6,7},{7,6}} | collective-permute-start | bytes 12582920 | tf_op jit(solution)/shard_map/ppermute | solution.py:627
  652.1 7.5 collective-permute-start.14
  659.7 262.9 %collective-permute-start.18 = (bf16[100,64,256]{2,1,0:T(8,128)(2,1)}, bf16[100,64,256]{2,1,0:T(8,128)(2,1)}, u32[]{:S(2)}, u32[]{:S(2)}) collective-permute-start(bf16[100,64,256]{2,1,0:T(8,128)(2,1)} %get-tuple-element.147), channel_id=1, source_target_pairs={{0,2},{1,3},{2,0},{3,1},{4,6},{5,7},{6,4},{7,5}} | collective-permute-start | bytes 9830408 | tf_op jit(solution)/shard_map/ppermute | solution.py:627
  659.9 328.6 %collective-permute-start.19 = (bf16[100,64,256]{2,1,0:T(8,128)(2,1)}, bf16[100,64,256]{2,1,0:T(8,128)(2,1)}, u32[]{:S(2)}, u32[]{:S(2)}) collective-permute-start(bf16[100,64,256]{2,1,0:T(8,128)(2,1)} %get-tuple-element.122), channel_id=1, source_target_pairs={{0,3},{1,2},{2,1},{3,0},{4,7},{5,6},{6,5},{7,4}} | collective-permute-start | bytes 9830408 | tf_op jit(solution)/shard_map/ppermute | solution.py:627
  919.3 88.5 %collective-permute-start.20 = (f32[64,64,256]{2,1,0:T(8,128)}, f32[64,64,256]{2,1,0:T(8,128)}, u32[]{:S(2)}, u32[]{:S(2)}) collective-permute-start(f32[64,64,256]{2,1,0:T(8,128)} %get-tuple-element.152), channel_id=1, source_target_pairs={{0,1},{1,0},{2,3},{3,2},{4,5},{5,4},{6,7},{7,6}} | collective-permute-start | bytes 12582920 | tf_op jit(solution)/shard_map/ppermute | solution.py:627
  921.2 182.4 %collective-permute-start.24 = (bf16[100,64,256]{2,1,0:T(8,128)(2,1)}, bf16[100,64,256]{2,1,0:T(8,128)(2,1)}, u32[]{:S(2)}, u32[]{:S(2)}) collective-permute-start(bf16[100,64,256]{2,1,0:T(8,128)(2,1)} %get-tuple-element.157), channel_id=1, source_target_pairs={{0,2},{1,3},{2,0},{3,1},{4,6},{5,7},{6,4},{7,5}} | collective-permute-start | bytes 9830408 | tf_op jit(solution)/shard_map/ppermute | solution.py:627
  921.2 193.2 %collective-permute-start.25 = (bf16[100,64,256]{2,1,0:T(8,128)(2,1)}, bf16[100,64,256]{2,1,0:T(8,128)(2,1)}, u32[]{:S(2)}, u32[]{:S(2)}) collective-permute-start(bf16[100,64,256]{2,1,0:T(8,128)(2,1)} %get-tuple-element.134), channel_id=1, source_target_pairs={{0,3},{1,2},{2,1},{3,0},{4,7},{5,6},{6,5},{7,4}} | collective-permute-start | bytes 9830408 | tf_op jit(solution)/shard_map/ppermute | solution.py:627
  922.6 270.9 %collective-permute-start.28 = (bf16[108,64,256]{2,1,0:T(8,128)(2,1)}, bf16[108,64,256]{2,1,0:T(8,128)(2,1)}, u32[]{:S(2)}, u32[]{:S(2)}) collective-permute-start(bf16[108,64,256]{2,1,0:T(8,128)(2,1)} %get-tuple-element.165), channel_id=1, source_target_pairs={{0,2},{1,3},{2,0},{3,1},{4,6},{5,7},{6,4},{7,5}} | collective-permute-start | bytes 10616840 | tf_op jit(solution)/shard_map/ppermute | solution.py:627
  923.4 51.3 %copy-start.4 = (f32[6,64,256]{2,1,0:T(8,128)S(1)}, f32[6,64,256]{2,1,0:T(8,128)}, u32[]{:S(2)}) copy-start(f32[6,64,256]{2,1,0:T(8,128)} %copy-done.3) | copy-start | bytes 1179652
  923.4 51.3 %copy-start.7 = (bf16[4,64,64]{2,1,0:T(8,128)(2,1)S(1)}, bf16[4,64,64]{2,1,0:T(8,128)(2,1)}, u32[]{:S(2)}) copy-start(bf16[4,64,64]{2,1,0:T(8,128)(2,1)} %pad_maximum_fusion.3.refs_12_.refs_11_.refs_2_.refs_1_) | copy-start | bytes 98308
  923.4 51.3 %copy-start.9 = (bf16[8,64]{1,0:T(8,128)(2,1)S(1)}, bf16[8,64]{1,0:T(8,128)(2,1)}, u32[]{:S(2)}) copy-start(bf16[8,64]{1,0:T(8,128)(2,1)} %concatenate.53.refs_13_.refs_12_.refs_3_.refs_2_) | copy-start | bytes 3076
  974.7 13.9 %copy-start.12 = (f32[8,64,256]{2,1,0:T(8,128)}, f32[8,64,256]{2,1,0:T(8,128)S(1)}, u32[]{:S(2)}) copy-start(f32[8,64,256]{2,1,0:T(8,128)S(1)} %get-tuple-element.145) | copy-start | bytes 1572868
  988.5 12.7 copy-start.21
  988.6 14.3 %copy-start.14 = (bf16[4,4,64,256]{3,2,1,0:T(8,128)(2,1)S(1)}, bf16[4,4,64,256]{3,2,1,0:T(8,128)(2,1)}, u32[]{:S(2)}) copy-start(bf16[4,4,64,256]{3,2,1,0:T(8,128)(2,1)} %get-tuple-element.144.refs_2_.refs_3_.refs_4_.refs_5_.refs_6_.refs_7_.refs_8_.refs_9_) | copy-start | bytes 1572868
  988.6 115.0 %slice-start = ((s8[6291456]{0:T(1024)(128)(4,1)}), s8[2097152]{0:T(1024)(128)(4,1)S(1)}, s32[]{:S(2)}) async-start(s8[6291456]{0:T(1024)(128)(4,1)} %bitcast.110), calls=%async_computation | async-start | bytes 4194304
  999.5 1.8 collective-permute-start.22
  1001.3 1.5 collective-permute-start.23
  1002.8 1.9 collective-permute-start.21
  1005.5 299.0 %collective-permute-start.34 = (f32[24,64,256]{2,1,0:T(8,128)}, f32[24,64,256]{2,1,0:T(8,128)}, u32[]{:S(2)}, u32[]{:S(2)}) collective-permute-start(f32[24,64,256]{2,1,0:T(8,128)} %get-tuple-element.176), channel_id=1, source_target_pairs={{0,3},{1,2},{2,1},{3,0},{4,7},{5,6},{6,5},{7,4}} | collective-permute-start | bytes 4718600 | tf_op jit(solution)/shard_map/ppermute | solution.py:627
  1008.4 95.2 %slice-start.1 = ((s8[6291456]{0:T(1024)(128)(4,1)}), s8[4194304]{0:T(1024)(128)(4,1)S(1)}, s32[]{:S(2)}) async-start(s8[6291456]{0:T(1024)(128)(4,1)} %bitcast.110), calls=%async_computation.1 | async-start | bytes 8388608
  1008.4 95.2 %copy-start.10 = (bf16[8,64]{1,0:T(8,128)(2,1)S(1)}, bf16[8,64]{1,0:T(8,128)(2,1)}, u32[]{:S(2)}) copy-start(bf16[8,64]{1,0:T(8,128)(2,1)} %concatenate.53.refs_13_.refs_12_.refs_3_.refs_2_) | copy-start | bytes 3076
  1114.4 10.9 copy-start.23
  1114.4 11.2 copy-start.57
  1114.4 12.5 copy-start.59
  1125.1 1.8 collective-permute-start.26
  1125.2 2.3 collective-permute-start.27
  1125.6 115.0 %collective-permute-start.30 = (bf16[16,64,256]{2,1,0:T(8,128)(2,1)S(1)}, bf16[16,64,256]{2,1,0:T(8,128)(2,1)S(1)}, u32[]{:S(2)}, u32[]{:S(2)}) collective-permute-start(bf16[16,64,256]{2,1,0:T(8,128)(2,1)S(1)} %copy-done.57), channel_id=1, source_target_pairs={{0,3},{1,2},{2,1},{3,0},{4,7},{5,6},{6,5},{7,4}} | collective-permute-start | bytes 1572872 | tf_op jit(solution)/shard_map/ppermute | solution.py:627
  1126.8 112.4 %collective-permute-start.29 = (bf16[16,64,128]{2,1,0:T(8,128)(2,1)S(1)}, bf16[16,64,128]{2,1,0:T(8,128)(2,1)S(1)}, u32[]{:S(2)}, u32[]{:S(2)}) collective-permute-start(bf16[16,64,128]{2,1,0:T(8,128)(2,1)S(1)} %copy-done.59), channel_id=1, source_target_pairs={{0,3},{1,2},{2,1},{3,0},{4,7},{5,6},{6,5},{7,4}} | collective-permute-start | bytes 786440 | tf_op jit(solution)/shard_map/ppermute | solution.py:627
  1193.4 11.1 copy-start.56
  1193.4 45.8 %copy-start.58 = (bf16[16,64,128]{2,1,0:T(8,128)(2,1)S(1)}, bf16[16,64,128]{2,1,0:T(8,128)(2,1)}, u32[]{:S(2)}) copy-start(bf16[16,64,128]{2,1,0:T(8,128)(2,1)} %get-tuple-element.173) | copy-start | bytes 786436
  1193.4 47.2 %copy-start.13 = (f32[8,64,256]{2,1,0:T(8,128)S(1)}, f32[8,64,256]{2,1,0:T(8,128)}, u32[]{:S(2)}) copy-start(f32[8,64,256]{2,1,0:T(8,128)} %copy-done.12) | copy-start | bytes 1572868
  1204.3 41.1 %collective-permute-start.31 = (bf16[4,4,64,256]{3,2,1,0:T(8,128)(2,1)}, bf16[4,4,64,256]{3,2,1,0:T(8,128)(2,1)S(1)}, u32[]{:S(2)}, u32[]{:S(2)}) collective-permute-start(bf16[4,4,64,256]{3,2,1,0:T(8,128)(2,1)} %get-tuple-element.166.refs_2_.refs_3_.refs_4_.refs_5_), channel_id=1, source_target_pairs={{0,1},{1,0},{2,3},{3,2},{4,5},{5,4},{6,7},{7,6}} | collective-permute-start | bytes 1572872 | tf_op jit(solution)/shard_map/ppermute | solution.py:627
  1204.5 84.2 %collective-permute-start.33 = (bf16[16,64,256]{2,1,0:T(8,128)(2,1)S(1)}, bf16[16,64,256]{2,1,0:T(8,128)(2,1)S(1)}, u32[]{:S(2)}, u32[]{:S(2)}) collective-permute-start(bf16[16,64,256]{2,1,0:T(8,128)(2,1)S(1)} %copy-done.56), channel_id=1, source_target_pairs={{0,3},{1,2},{2,1},{3,0},{4,7},{5,6},{6,5},{7,4}} | collective-permute-start | bytes 1572872 | tf_op jit(solution)/shard_map/ppermute | solution.py:627
  1239.3 49.5 %collective-permute-start.32 = (bf16[16,64,128]{2,1,0:T(8,128)(2,1)S(1)}, bf16[16,64,128]{2,1,0:T(8,128)(2,1)S(1)}, u32[]{:S(2)}, u32[]{:S(2)}) collective-permute-start(bf16[16,64,128]{2,1,0:T(8,128)(2,1)S(1)} %copy-done.58), channel_id=1, source_target_pairs={{0,3},{1,2},{2,1},{3,0},{4,7},{5,6},{6,5},{7,4}} | collective-permute-start | bytes 786440 | tf_op jit(solution)/shard_map/ppermute | solution.py:627
  1240.6 66.7 %collective-permute-start.35 = (f32[8,64,256]{2,1,0:T(8,128)S(1)}, f32[8,64,256]{2,1,0:T(8,128)S(1)}, u32[]{:S(2)}, u32[]{:S(2)}) collective-permute-start(f32[8,64,256]{2,1,0:T(8,128)S(1)} %copy-done.13), channel_id=1, source_target_pairs={{0,3},{1,2},{2,1},{3,0},{4,7},{5,6},{6,5},{7,4}} | collective-permute-start | bytes 1572872 | tf_op jit(solution)/shard_map/ppermute | solution.py:627
  (34 other events, 163.7 us)
where the time goes:
time: 1320 us; the launch traced here: 1310 us
  Pallas kernels  783 us (59%)
  waiting for transfers between devices  435 us (33%)
  local copies, waits for them, and re-layouts  59.6 us (5%)
  starting transfers between devices  26.1 us (2%)
    ppermute x36, waiting for transfers between devices, exchange(): return lax.ppermute(values, 'dap', [(i, i ^ r) for i in range(4)])  435 us
    pallas_call x7, Pallas kernels, attend(): pl.pallas_call(functools.partial(attention_kernel, static, fresh, away),...  396 us
    pallas_call x3, Pallas kernels, u_call(): pl.pallas_call(functools.partial(u_kernel, last, layout), out_shape=(ROW_...  262 us
    pallas_call x7, Pallas kernels, r_call(): pl.pallas_call(functools.partial(r_kernel, blocks), out_shape=[pltpu.HBM(...  62.3 us
    squeeze x6, local copies, waits for them, and re-layouts, local_block(): lax.dynamic_slice(lax.optimization_barrier((zt, *before))[0], where, (1,...  34.6 us
    pallas_call x1, Pallas kernels, l2_call(): pl.pallas_call(l2_kernel, grid=(n // 2,), out_shape=SDS((n, ROWS, CH, LAN...  33 us
    pallas_call x1, Pallas kernels, l1_call(): pl.pallas_call(l1_kernel, out_shape=(ab, ab), grid_spec=pltpu.PrefetchSca...  28.7 us
  transfers between devices with their start and end apart: 36, of which 14 were waited for; matrix products, arithmetic and copies ran while one was open for 3% of the time, Pallas kernels for 44%

commit v1 on v0

--- a/solution.py
+++ b/solution.py
@@ -98,7 +98,7 @@
 
 def u_kernel(last, layout, sc, *refs):
     z_refs = refs[:len(layout)]
-    n_far = 2 * CHUNKS + 1 if last else 1
+    n_far = 3 if last else 1
     (mask0, mask1, mask2, mask3, norms, xgs, w_ab, w_sq, w_bias, z2_own, z2_par, bias_out, far2, *far3) = refs[len(layout):][:13 + n_far]
     (z_s, a_s, b_s, x_s, mask, stats, tile_a, tile_b, tile_x, tile_c, tile_d, tile_z, in_sem, z_sem, x_sem) = refs[len(layout) + 13 + n_far:]
     me, sample = sc[0], sc[1]
@@ -147,11 +147,11 @@
         jobs = [(r == 2, narrow, far2.at[half, :, side])] if outgoing else [
             (r == 0, z_tile, z2_own.at[rows]), (r == 1, z_tile, z2_par.at[rows]), (r == 2, wide, far2.at[rows])]
         if last:
-            for n in range(CHUNKS):
-                jobs += [((r == 3) & (q == n), narrow, far3[2 * n + 1]) if outgoing else ((r == 3) & (q == n), wide, far3[2 * n])]
+            near_rows, away_rows = (pl.ds(pl.multiple_of(TILE * row, TILE), TILE)
+                                    for row in (jnp.minimum(q, CHUNKS - 1), jnp.maximum(q - CHUNKS, 0)))
+            jobs += [((r == 3) & (q < CHUNKS), *((narrow, far3[1].at[near_rows]) if outgoing else (wide, far3[0].at[near_rows])))]
             if not outgoing:
-                rest = pl.ds(pl.multiple_of(jnp.maximum(q - CHUNKS, 0) * TILE, TILE), TILE)
-                jobs += [((r == 3) & (q >= CHUNKS), z_tile, far3[-1].at[rest])]
+                jobs += [((r == 3) & (q >= CHUNKS), z_tile, far3[-1].at[away_rows])]
         else:
             jobs += [(r == 3, narrow, far3[0].at[half, :, side]) if outgoing else (r == 3, wide, far3[0].at[rows])]
         for when, src, dst in jobs:
@@ -264,10 +264,11 @@
 DMA2 = pltpu.SemaphoreType.DMA((2,))
 FAR_BIAS = ROWS + ROWS // 2
 FAR = SDS((FAR_BIAS + 4, CH, COLS), BF16)
-TILE_FULL = SDS((TILE, CH, COLS), BF16)
-TILE_HALF = SDS((TILE, CH, LANES), BF16)
 CHUNKS = 2
-AWAY = SDS((ROWS - CHUNKS * TILE, CH, COLS), F32)
+SOME = CHUNKS * TILE
+AWAY = SDS((ROWS - SOME, CH, COLS), F32)
+SOME_FULL = SDS((SOME, CH, COLS), BF16)
+SOME_HALF = SDS((SOME, CH, LANES), BF16)
 FAR_LAST = SDS((FAR_BIAS + 12, CH, COLS), BF16)
 ROW_WIDE = SDS((ROWS, CH, COLS), F32)
 SAMPLE_BF = pltpu.VMEM((CH, COLS, COLS), BF16)
@@ -276,9 +277,9 @@
 def u_call(last, layout, sc, z_parts, masks, norms, xgs, w_ab, w_sq, w_bias):
     return pl.pallas_call(
         functools.partial(u_kernel, last, layout),
-        out_shape=(ROW_WIDE, ROW_WIDE, SDS((4, 4, ROWS, COLS), BF16), *((FAR_LAST, *(TILE_FULL, TILE_HALF) * CHUNKS, AWAY) if last else (FAR, FAR))),
+        out_shape=(ROW_WIDE, ROW_WIDE, SDS((4, 4, ROWS, COLS), BF16), *((FAR_LAST, SOME_FULL, SOME_HALF, AWAY) if last else (FAR, FAR))),
         in_specs=[SM] + [HB] * len(layout) + [VM] * 9,
-        out_specs=(HB, HB, VM) + (HB,) * (2 * CHUNKS + 2 if last else 2),
+        out_specs=(HB, HB, VM) + (HB,) * (4 if last else 2),
         scratch_shapes=[
             pltpu.VMEM((COLS, CH, COLS), F32), SAMPLE_BF, SAMPLE_BF,
             pltpu.VMEM((CH, COLS, COLS), F32), pltpu.VMEM((COLS, COLS), F32), pltpu.VMEM((4, COLS, COLS), F32), AB_TILE, AB_TILE, pltpu.VMEM((CH, TILE, COLS), BF16), pltpu.VMEM((2, TILE, CH, COLS), BF16),
@@ -410,23 +411,20 @@
 
     @pl.when(step == steps - 1)
     def _():
-        @pl.when(steps > 1)
-        def _():
-            z_copy(step - 1).wait()
-
+        z_copy(step - 1).wait()
         z_copy(step).wait()
 
 
-def r_call(blocks, start, sc, zt, x_near, x_far, xi, norms, w_sq, w_bias):
-    steps = ROWS // TILE if blocks else 1
+def r_call(blocks, sc, zt, x_near, x_far, xi, norms, w_sq, w_bias):
+    steps = ROWS // TILE if blocks else CHUNKS
     far_map = (lambda i, sc: (ROWS // TILE + i % 2, 0, i // 2)) if blocks else (lambda i, sc: (i, 0, 0))
     return pl.pallas_call(
         functools.partial(r_kernel, blocks),
         out_shape=[pltpu.HBM((steps * TILE, CH, COLS), F32)] + [pltpu.HBM((blocks + 1, 4, ROWS, COLS), BF16)] * (blocks > 0),
         grid_spec=pltpu.PrefetchScalarGridSpec(
             num_scalar_prefetch=1, grid=(steps,),
-            in_specs=[pl.BlockSpec((1, TILE, CH, COLS), lambda i, sc: (sc[1], start + i, 0, 0)),
-                      pl.BlockSpec((1, TILE, CH, LANES), lambda i, sc: (sc[2], start + i, 0, 0)),
+            in_specs=[pl.BlockSpec((1, TILE, CH, COLS), lambda i, sc: (sc[1], i, 0, 0)),
+                      pl.BlockSpec((1, TILE, CH, LANES), lambda i, sc: (sc[2], i, 0, 0)),
                       pl.BlockSpec((TILE, CH, LANES), far_map), pl.BlockSpec((TILE, CH, COLS), lambda i, sc: (i, 0, 0)),
                       *[pl.BlockSpec((4 * blocks, CH, COLS), lambda i, sc: (FAR_BIAS // (4 * blocks), 0, 0))] * (blocks > 0),
                       VM, VM, VM],
@@ -707,17 +705,17 @@
             near = (n_own * (me ^ 1) + t, 0, exchange(z_par, 1), here(exchange(bias, 1)), 0)
             own = (n_own * me + t, 0, z_own, here(bias), 0)
             two = exchange(far2, 2)
-            three = [exchange(v, 3) for v in far3[:2 * CHUNKS]]
+            three = [exchange(v, 3) for v in far3[:2]]
             held.append((two, three))
             if last:
                 out, *away = attention([own, (0, 0, far3[-1], here(bias), 0)], out,
-                                       masks[3][t][None, CHUNKS * TILE:].astype(jnp.int32))
+                                       masks[3][t][None, SOME:].astype(jnp.int32))
                 away = [exchange(v, 3) for v in away]
             else:
                 out, = attention([own, near], out)
 
-        def rows_of(t, r, blocks, x_far, xi, start=0):
-            return ordered(functools.partial(r_call, blocks, start), [me, n_own * (me ^ r) + t, far.index((t, r))],
+        def rows_of(t, r, blocks, x_far, xi):
+            return ordered(functools.partial(r_call, blocks), [me, n_own * (me ^ r) + t, far.index((t, r))],
                            zt, x_near, x_far, xi, norms, w_sq, w_bias8)
 
         for t in range(n_own - 1):
@@ -731,13 +729,10 @@
         two, three = held[t + 1]
         z_two, mine = rows_of(t + 1, 2, 3, two, two)
         par = exchange(mine, 1)
-        jobs = [(n_own * (me ^ 2) + t + 1, me, z_two, [(mine, k) for k in (0, 3, 1, 2)], 0)]
-        for n in range(CHUNKS):
-            z_three, = rows_of(t + 1, 3, 0, three[2 * n + 1], three[2 * n], n)
-            jobs += [(n_own * (me ^ 3) + t + 1, me, z_three, [(par, k) for k in (3, 0, 2, 1)], n * TILE)]
-            out, = attention(jobs, out)
-            jobs = []
-        for v, start in zip(away, (CHUNKS * TILE, CHUNKS * TILE + AWAY_FIRST)):
+        out, = attention([(n_own * (me ^ 2) + t + 1, me, z_two, [(mine, k) for k in (0, 3, 1, 2)], 0)], out)
+        z_three, = rows_of(t + 1, 3, 0, three[1], three[0])
+        out, = attention([(n_own * (me ^ 3) + t + 1, me, z_three, [(par, k) for k in (3, 0, 2, 1)], 0)], out)
+        for v, start in zip(away, (SOME, SOME + AWAY_FIRST)):
             out = lax.dynamic_update_slice(out, v[None], (n_own * (me ^ 3) + n_own - 1, start, 0, 0))
         return jnp.transpose(out, (0, 1, 3, 2))
 

time: 1320 us -> 1300 us (0.985)
  waiting for transfers between devices: 435 us -> 417 us
    ppermute x36 -> x34, waiting for transfers between devices: 435 us -> 417 us  [exchange(): return lax.ppermute(values, 'dap', [(i, i ^ r) for i in range(4)])]
    pallas_call x7 -> x6, Pallas kernels: 62.3 us -> 59.9 us  [r_call(): pl.pallas_call(functools.partial(r_kernel, blocks), out_shape=[pltpu.HBM(...]
  transfers between devices with their start and end apart: 36 -> 34, of which waited for: 14 -> 14; matrix products, arithmetic and copies ran while one was open for 3% -> 3% of each run, Pallas kernels for 44% -> 45%
where the time goes in v1:
time: 1300 us; the launch traced here: 1290 us
  Pallas kernels  781 us (60%)
  waiting for transfers between devices  417 us (32%)
  local copies, waits for them, and re-layouts  59.5 us (5%)
  starting transfers between devices  24.6 us (2%)
    ppermute x34, waiting for transfers between devices, exchange(): return lax.ppermute(values, 'dap', [(i, i ^ r) for i in range(4)])  417 us
    pallas_call x7, Pallas kernels, attend(): pl.pallas_call(functools.partial(attention_kernel, static, fresh, away),...  397 us
    pallas_call x3, Pallas kernels, u_call(): pl.pallas_call(functools.partial(u_kernel, last, layout), out_shape=(ROW_...  262 us
    pallas_call x6, Pallas kernels, r_call(): pl.pallas_call(functools.partial(r_kernel, blocks), out_shape=[pltpu.HBM(...  59.9 us
    squeeze x6, local copies, waits for them, and re-layouts, local_block(): lax.dynamic_slice(lax.optimization_barrier((zt, *before))[0], where, (1,...  34.6 us
    pallas_call x1, Pallas kernels, l2_call(): pl.pallas_call(l2_kernel, grid=(n // 2,), out_shape=SDS((n, ROWS, CH, LAN...  33 us
    pallas_call x1, Pallas kernels, l1_call(): pl.pallas_call(l1_kernel, out_shape=(ab, ab), grid_spec=pltpu.PrefetchSca...  28.7 us
  transfers between devices with their start and end apart: 34, of which 14 were waited for; matrix products, arithmetic and copies ran while one was open for 3% of the time, Pallas kernels for 45%

profile of v1, /device:TPU:0, one launch (start us, length us, event | category | flops | bytes accessed | tf_op | source)
XLA Modules:
  0.0 1286.6 jit_solution(5710419985676551545)
XLA Ops:
  0.0 1.2 dynamic-slice_bitcast_fusion.9
  1.3 4.4 dynamic-slice_bitcast_fusion.8
  7.3 28.7 %near_projections.1 = (bf16[6,64,64,256]{3,2,1,0:T(8,128)(2,1)S(1)}, bf16[6,64,64,256]{3,2,1,0:T(8,128)(2,1)}) custom-call(s32[6]{0:T(128)S(1)} %stack.177.ids, f32[12,64,64,256]{3,2,1,0:T(8,128)} %bitcast.121, s32[12,64,256]{2,1,0:T(8,128)S(1)} %copy-done.2, f32[6,64,256]{2,1,0:T(8,128)S(1)} %broadcast_dynamic-update-slice_fusion.norms.refs_9_.refs_8_.refs_1_.refs_0_, ...), custom_call_target="tpu_custom_call" | custom-call | tf_op jit(solution)/shard_map/near_projections/pallas_call | solution.py:313
  36.1 4.6 copy-done.6
  40.7 0.8 collective-permute-start
  41.5 4.6 dynamic-slice_bitcast_fusion.7
  46.2 4.7 dynamic-slice_bitcast_fusion.6
  51.0 2.6 collective-permute-start.3
  54.0 1.5 collective-permute-start.7
  57.1 0.7 dynamic-slice_bitcast_fusion.10
  57.8 167.5 %collective-permute-done.7 = bf16[3,64,256]{2,1,0:T(8,128)(2,1)S(1)} collective-permute-done((bf16[3,64,256]{2,1,0:T(8,128)(2,1)S(1)}, bf16[3,64,256]{2,1,0:T(8,128)(2,1)S(1)}, u32[]{:S(2)}, u32[]{:S(2)}) %collective-permute-start.7) | collective-permute-done | bytes 98336 | tf_op jit(solution)/shard_map/ppermute | solution.py:625
  225.3 2.3 collective-permute-start.6
  228.2 2.4 collective-permute-done.6
  231.3 0.7 collective-permute-done.5
  232.0 1.7 collective-permute-start.1
  234.4 0.6 slice_bitcast_fusion.1
  235.6 33.0 %near_product.1.x_near = bf16[6,64,64,128]{3,2,1,0:T(8,128)(2,1)S(1)} custom-call(s32[1]{0:T(128)} %bitcast.1.sc, bf16[6,64,64,256]{3,2,1,0:T(8,128)(2,1)} %copy-done.6, bf16[6,64,64,256]{3,2,1,0:T(8,128)(2,1)} %get-tuple-element.103.b_own, bf16[6,64,64,256]{3,2,1,0:T(8,128)(2,1)} %collective-permute-done.b_par, ...), custom_call_target="tpu_custom_call" | custom-call | tf_op jit(solution)/shard_map/near_product/pallas_call | solution.py:349
  268.7 2.6 copy-done
  271.3 0.8 copy-done.27
  272.0 87.6 %pair_updates.3 = (f32[64,64,256]{2,1,0:T(8,128)}, f32[64,64,256]{2,1,0:T(8,128)}, bf16[4,4,64,256]{3,2,1,0:T(8,128)(2,1)}, bf16[100,64,256]{2,1,0:T(8,128)(2,1)}, bf16[100,64,256]{2,1,0:T(8,128)(2,1)}) custom-call(s32[2]{0:T(128)} %pad_add_fusion.14.sc, f32[12,64,64,256]{3,2,1,0:T(8,128)} %bitcast.124, f32[8,64,256]{2,1,0:T(8,128)} %copy-done.27, ...), custom_call_target="tpu_custom_call" | custom-call | tf_op jit(solution)/shard_map/pair_updates/pallas_call | solution.py:278
  359.8 9.8 dynamic-slice_bitcast_fusion.3
  369.6 1.8 collective-permute-start.11
  373.4 6.2 collective-permute-done.9.refs_6_.refs_7_.refs_8_.refs_9_
  379.5 0.8 copy-done.19
  380.3 65.2 %triangle_attention.7.refs_14_ = f32[12,64,64,256]{3,2,1,0:T(8,128)} custom-call(s32[4]{0:T(128)S(1)} %get-tuple-element.120.sc, f32[64,64,256]{2,1,0:T(8,128)} %get-tuple-element.121.refs_0_, f32[64,64,256]{2,1,0:T(8,128)} %collective-permute-done.8.refs_1_, bf16[4,4,64,256]{3,2,1,0:T(8,128)(2,1)} %get-tuple-element.123.refs_2_.refs_3_.refs_4_.refs_5_, ...), custom_call_target="tpu_custom_call" | custom-call | tf_op jit(solution)/shard_map/triangle_attention/pallas_call | solution.py:604
  445.5 17.9 %collective-permute-done.10.refs_1_ = f32[64,64,256]{2,1,0:T(8,128)} collective-permute-done((f32[64,64,256]{2,1,0:T(8,128)}, f32[64,64,256]{2,1,0:T(8,128)}, u32[]{:S(2)}, u32[]{:S(2)}) %collective-permute-start.10) | collective-permute-done | bytes 4194336 | tf_op jit(solution)/shard_map/ppermute | solution.py:625
  463.4 88.8 %collective-permute-done.11.refs_2_ = f32[64,64,256]{2,1,0:T(8,128)} collective-permute-done((f32[64,64,256]{2,1,0:T(8,128)}, f32[64,64,256]{2,1,0:T(8,128)}, u32[]{:S(2)}, u32[]{:S(2)}) %collective-permute-start.11) | collective-permute-done | bytes 4194336 | tf_op jit(solution)/shard_map/ppermute | solution.py:625
  552.2 87.6 %pair_updates.4 = (f32[64,64,256]{2,1,0:T(8,128)}, f32[64,64,256]{2,1,0:T(8,128)}, bf16[4,4,64,256]{3,2,1,0:T(8,128)(2,1)}, bf16[100,64,256]{2,1,0:T(8,128)(2,1)}, bf16[100,64,256]{2,1,0:T(8,128)(2,1)}) custom-call(s32[2]{0:T(128)} %pad_add_fusion.13.sc, f32[12,64,64,256]{3,2,1,0:T(8,128)} %bitcast.126, f32[64,64,256]{2,1,0:T(8,128)} %collective-permute-done.10.refs_1_, ...), custom_call_target="tpu_custom_call" | custom-call | tf_op jit(solution)/shard_map/pair_updates/pallas_call | solution.py:278
  640.2 9.8 dynamic-slice_bitcast_fusion
  650.1 1.5 collective-permute-start.16
  652.2 7.5 collective-permute-done.14.refs_6_.refs_7_.refs_8_.refs_9_
  660.0 1.5 collective-permute-start.19
  661.5 0.7 pad_add_fusion.12.sc
  662.1 65.2 %triangle_attention.8.refs_15_ = f32[12,64,64,256]{3,2,1,0:T(8,128)} custom-call(s32[4]{0:T(128)S(1)} %get-tuple-element.132.sc, f32[64,64,256]{2,1,0:T(8,128)} %get-tuple-element.133.refs_0_, f32[64,64,256]{2,1,0:T(8,128)} %collective-permute-done.13.refs_1_, ...), custom_call_target="tpu_custom_call", output_to_operand_aliasing={{}: (15, {})} | custom-call | tf_op jit(solution)/shard_map/triangle_attention/pallas_call | solution.py:604
  727.3 16.5 %collective-permute-done.15.refs_1_ = f32[64,64,256]{2,1,0:T(8,128)} collective-permute-done((f32[64,64,256]{2,1,0:T(8,128)}, f32[64,64,256]{2,1,0:T(8,128)}, u32[]{:S(2)}, u32[]{:S(2)}) %collective-permute-start.15) | collective-permute-done | bytes 4194336 | tf_op jit(solution)/shard_map/ppermute | solution.py:625
  743.8 88.3 %collective-permute-done.16.refs_2_ = f32[64,64,256]{2,1,0:T(8,128)} collective-permute-done((f32[64,64,256]{2,1,0:T(8,128)}, f32[64,64,256]{2,1,0:T(8,128)}, u32[]{:S(2)}, u32[]{:S(2)}) %collective-permute-start.16) | collective-permute-done | bytes 4194336 | tf_op jit(solution)/shard_map/ppermute | solution.py:625
  832.1 87.2 %pair_updates.5 = (f32[64,64,256]{2,1,0:T(8,128)}, f32[64,64,256]{2,1,0:T(8,128)}, bf16[4,4,64,256]{3,2,1,0:T(8,128)(2,1)}, bf16[108,64,256]{2,1,0:T(8,128)(2,1)...) custom-call(s32[2]{0:T(128)} %pad_add_fusion.12.sc, ...), custom_call_target="tpu_custom_call" | custom-call | tf_op jit(solution)/shard_map/pair_updates/pallas_call | solution.py:278
  919.3 2.0 collective-permute-start.20
  921.3 1.4 collective-permute-start.25
  922.6 0.6 collective-permute-start.28
  923.5 51.2 %triangle_attention.9 = (f32[12,64,64,256]{3,2,1,0:T(8,128)}, f32[24,64,256]{2,1,0:T(8,128)}, f32[8,64,256]{2,1,0:T(8,128)S(1)}) custom-call(s32[4]{0:T(128)S(1)} %get-tuple-element.139.sc, f32[64,64,256]{2,1,0:T(8,128)} %get-tuple-element.140.refs_0_, f32[32,64,256]{2,1,0:T(8,128)} %get-tuple-element.138.refs_1_, ...), custom_call_target="tpu_custom_call", output_to_operand_aliasing={{0}: (16, {})} | custom-call | tf_op jit(solution)/shard_map/triangle_attention/pallas_call | solution.py:604
  974.7 2.9 copy-done.1
  977.7 11.0 row_updates.6
  988.8 10.9 row_updates.7
  999.9 1.6 collective-permute-done.22.refs_8_.refs_10_
  1001.6 1.4 collective-permute-done.23.refs_12_.refs_14_
  1003.2 1.8 collective-permute-done.21.refs_3_.refs_4_.refs_5_.refs_6_
  1005.0 0.8 copy-done.18
  1005.8 1.5 collective-permute-start.32
  1008.9 95.2 %triangle_attention.10.refs_14_ = f32[12,64,64,256]{3,2,1,0:T(8,128)} custom-call(s32[6]{0:T(128)S(1)} %copy-done.11, f32[64,64,256]{2,1,0:T(8,128)} %collective-permute-done.20.refs_0_, f32[64,64,256]{2,1,0:T(8,128)} %get-tuple-element.150.refs_1_, f32[64,64,256]{2,1,0:T(8,128)} %get-tuple-element.151.refs_2_, ...), custom_call_target="tpu_custom_call", output_to_operand_aliasing={{}: (20, {})} | custom-call | tf_op jit(solution)/shard_map/triangle_attention/pallas_call | solution.py:604
  1104.1 10.7 row_updates.8
  1114.9 10.7 row_updates.9
  1126.2 1.1 collective-permute-done.26.refs_3_.refs_5_
  1127.3 1.5 collective-permute-start.29
  1128.8 0.7 copy-done.26
  1129.5 65.2 %triangle_attention.11.refs_9_ = f32[12,64,64,256]{3,2,1,0:T(8,128)} custom-call(s32[4]{0:T(128)S(1)} %pad_add_fusion.7.sc, f32[64,64,256]{2,1,0:T(8,128)} %get-tuple-element.159.refs_0_, f32[64,64,256]{2,1,0:T(8,128)} %get-tuple-element.160.refs_1_, bf16[2,4,64,256]{3,2,1,0:T(8,128)(2,1)} %get-tuple-element.155.refs_2_.refs_4_, ...), custom_call_target="tpu_custom_call", output_to_operand_aliasing={{}: (15, {})} | custom-call | tf_op jit(solution)/shard_map/triangle_attention/pallas_call | solution.py:604
  1194.7 10.9 row_updates.10
  1206.4 34.9 %triangle_attention.12.refs_9_ = f32[12,64,64,256]{3,2,1,0:T(8,128)} custom-call(s32[2]{0:T(128)S(1)} %pad_add_fusion.5.sc, f32[64,64,256]{2,1,0:T(8,128)} %get-tuple-element.165.refs_0_, bf16[4,4,64,256]{3,2,1,0:T(8,128)(2,1)} %get-tuple-element.163.refs_1_.refs_2_.refs_3_.refs_4_, ...), custom_call_target="tpu_custom_call", output_to_operand_aliasing={{}: (10, {})} | custom-call | tf_op jit(solution)/shard_map/triangle_attention/pallas_call | solution.py:604
  1241.3 14.8 %collective-permute-done.29.x_far = bf16[32,64,128]{2,1,0:T(8,128)(2,1)S(1)} collective-permute-done((bf16[32,64,128]{2,1,0:T(8,128)(2,1)S(1)}, bf16[32,64,128]{2,1,0:T(8,128)(2,1)S(1)}, u32[]{:S(2)}, u32[]{:S(2)}) %collective-permute-start.29) | collective-permute-done | bytes 524320 | tf_op jit(solution)/shard_map/ppermute | solution.py:625
  1256.1 5.7 row_updates.11.refs_0_
  1261.8 0.8 copy-done.17
  1262.6 20.2 %triangle_attention.13 = f32[12,64,64,256]{3,2,1,0:T(8,128)} custom-call(s32[2]{0:T(128)S(1)} %pad_add_fusion.3.sc, f32[32,64,256]{2,1,0:T(8,128)} %row_updates.11.refs_0_, bf16[4,4,64,256]{3,2,1,0:T(8,128)(2,1)} %copy-done.17, bf16[4,4,64,256]{3,2,1,0:T(8,128)(2,1)} %copy-done.17, ...), custom_call_target="tpu_custom_call", output_to_operand_aliasing={{}: (10, {})} | custom-call | tf_op jit(solution)/shard_map/triangle_attention/pallas_call | solution.py:604
  1282.8 2.7 bitcast_dynamic-update-slice_fusion
  1285.5 0.8 bitcast_dynamic-update-slice_fusion.1
  (211 shorter events, 12.9 us)
Async XLA Ops:
  6.9 29.2 %copy-start.8 = (bf16[2,256,64]{2,1,0:T(8,128)(2,1)}, bf16[2,256,64]{2,1,0:T(8,128)(2,1)S(1)}, u32[]{:S(2)}) copy-start(bf16[2,256,64]{2,1,0:T(8,128)(2,1)S(1)} %pad_maximum_fusion.1.w_ab.refs_11_.refs_10_) | copy-start | bytes 196612
  7.3 28.8 %copy-start.3 = (f32[6,64,256]{2,1,0:T(8,128)}, f32[6,64,256]{2,1,0:T(8,128)S(1)}, u32[]{:S(2)}) copy-start(f32[6,64,256]{2,1,0:T(8,128)S(1)} %broadcast_dynamic-update-slice_fusion.norms.refs_9_.refs_8_.refs_1_.refs_0_) | copy-start | bytes 1179652
  40.7 195.0 %collective-permute-start = (bf16[6,64,64,256]{3,2,1,0:T(8,128)(2,1)}, bf16[6,64,64,256]{3,2,1,0:T(8,128)(2,1)}, u32[]{:S(2)}, u32[]{:S(2)}) collective-permute-start(bf16[6,64,64,256]{3,2,1,0:T(8,128)(2,1)} %get-tuple-element.103.b_own), channel_id=1, source_target_pairs={{0,1},{1,0},{2,3},{3,2},{4,5},{5,4},{6,7},{7,6}} | collective-permute-start | bytes 37748744 | tf_op jit(solution)/shard_map/ppermute | solution.py:625
  46.2 9.4 copy-start.37
  46.2 9.5 copy-start.38
  46.2 9.6 copy-start.39
  46.2 9.7 copy-start.47
  46.2 10.3 copy-start.52
  46.2 10.4 copy-start.53
  46.2 10.5 copy-start.54
  46.2 10.6 copy-start.55
  51.0 220.3 %collective-permute-start.4 = (f32[64,64,256]{2,1,0:T(8,128)}, f32[64,64,256]{2,1,0:T(8,128)}, u32[]{:S(2)}, u32[]{:S(2)}) collective-permute-start(f32[64,64,256]{2,1,0:T(8,128)} %dynamic-slice_bitcast_fusion.6), channel_id=1, source_target_pairs={{0,1},{1,0},{2,3},{3,2},{4,5},{5,4},{6,7},{7,6}} | collective-permute-start | bytes 12582920 | tf_op jit(solution)/shard_map/ppermute | solution.py:625
  51.0 220.3 %collective-permute-start.3 = (f32[64,64,256]{2,1,0:T(8,128)}, f32[64,64,256]{2,1,0:T(8,128)}, u32[]{:S(2)}, u32[]{:S(2)}) collective-permute-start(f32[64,64,256]{2,1,0:T(8,128)} %dynamic-slice_bitcast_fusion.7), channel_id=1, source_target_pairs={{0,3},{1,2},{2,1},{3,0},{4,7},{5,6},{6,5},{7,4}} | collective-permute-start | bytes 12582920 | tf_op jit(solution)/shard_map/ppermute | solution.py:625
  53.6 217.7 %collective-permute-start.2 = (f32[56,64,256]{2,1,0:T(8,128)}, f32[56,64,256]{2,1,0:T(8,128)}, u32[]{:S(2)}, u32[]{:S(2)}) collective-permute-start(f32[56,64,256]{2,1,0:T(8,128)} %dynamic-slice_bitcast_fusion.8), channel_id=1, source_target_pairs={{0,2},{1,3},{2,0},{3,1},{4,6},{5,7},{6,4},{7,5}} | collective-permute-start | bytes 11010056 | tf_op jit(solution)/shard_map/ppermute | solution.py:625
  54.0 171.4 %collective-permute-start.7 = (bf16[3,64,256]{2,1,0:T(8,128)(2,1)S(1)}, bf16[3,64,256]{2,1,0:T(8,128)(2,1)S(1)}, u32[]{:S(2)}, u32[]{:S(2)}) collective-permute-start(bf16[3,64,256]{2,1,0:T(8,128)(2,1)S(1)} %get-tuple-element.180), channel_id=1, source_target_pairs={{0,3},{1,2},{2,1},{3,0},{4,7},{5,6},{6,5},{7,4}} | collective-permute-start | bytes 294920 | tf_op jit(solution)/shard_map/ppermute | solution.py:625
  57.1 211.6 %copy-start.5 = (f32[4,64,8,128]{3,2,1,0:T(8,128)}, f32[4,64,8,128]{3,2,1,0:T(8,128)S(1)}, u32[]{:S(2)}) copy-start(f32[4,64,8,128]{3,2,1,0:T(8,128)S(1)} %pad_maximum_fusion.xgs.refs_10_.refs_9_) | copy-start | bytes 3145732
  225.3 5.4 collective-permute-start.6
  230.7 1.3 collective-permute-start.5
  232.0 39.3 %collective-permute-start.1 = (f32[8,64,256]{2,1,0:T(8,128)S(1)}, f32[8,64,256]{2,1,0:T(8,128)S(1)}, u32[]{:S(2)}, u32[]{:S(2)}) collective-permute-start(f32[8,64,256]{2,1,0:T(8,128)S(1)} %dynamic-slice_bitcast_fusion.9), channel_id=1, source_target_pairs={{0,2},{1,3},{2,0},{3,1},{4,6},{5,7},{6,4},{7,5}} | collective-permute-start | bytes 1572872 | tf_op jit(solution)/shard_map/ppermute | solution.py:625
  359.7 12.1 copy-start.40
  359.7 12.1 copy-start.41
  359.7 12.2 copy-start.42
  359.7 12.3 copy-start.43
  359.7 12.4 copy-start.44
  359.8 12.6 copy-start.16
  359.8 19.8 %collective-permute-start.8 = (f32[64,64,256]{2,1,0:T(8,128)}, f32[64,64,256]{2,1,0:T(8,128)}, u32[]{:S(2)}, u32[]{:S(2)}) collective-permute-start(f32[64,64,256]{2,1,0:T(8,128)} %get-tuple-element.122), channel_id=1, source_target_pairs={{0,1},{1,0},{2,3},{3,2},{4,5},{5,4},{6,7},{7,6}} | collective-permute-start | bytes 12582920 | tf_op jit(solution)/shard_map/ppermute | solution.py:625
  369.6 93.8 %collective-permute-start.10 = (f32[64,64,256]{2,1,0:T(8,128)}, f32[64,64,256]{2,1,0:T(8,128)}, u32[]{:S(2)}, u32[]{:S(2)}) collective-permute-start(f32[64,64,256]{2,1,0:T(8,128)} %get-tuple-element.176), channel_id=1, source_target_pairs={{0,2},{1,3},{2,0},{3,1},{4,6},{5,7},{6,4},{7,5}} | collective-permute-start | bytes 12582920 | tf_op jit(solution)/shard_map/ppermute | solution.py:625
  369.6 182.6 %collective-permute-start.11 = (f32[64,64,256]{2,1,0:T(8,128)}, f32[64,64,256]{2,1,0:T(8,128)}, u32[]{:S(2)}, u32[]{:S(2)}) collective-permute-start(f32[64,64,256]{2,1,0:T(8,128)} %get-tuple-element.175), channel_id=1, source_target_pairs={{0,3},{1,2},{2,1},{3,0},{4,7},{5,6},{6,5},{7,4}} | collective-permute-start | bytes 12582920 | tf_op jit(solution)/shard_map/ppermute | solution.py:625
  371.4 180.8 %collective-permute-start.12 = (f32[64,64,256]{2,1,0:T(8,128)}, f32[64,64,256]{2,1,0:T(8,128)}, u32[]{:S(2)}, u32[]{:S(2)}) collective-permute-start(f32[64,64,256]{2,1,0:T(8,128)} %get-tuple-element.174), channel_id=1, source_target_pairs={{0,1},{1,0},{2,3},{3,2},{4,5},{5,4},{6,7},{7,6}} | collective-permute-start | bytes 12582920 | tf_op jit(solution)/shard_map/ppermute | solution.py:625
  372.4 7.2 collective-permute-start.9
  639.8 20.2 %collective-permute-start.13 = (f32[64,64,256]{2,1,0:T(8,128)}, f32[64,64,256]{2,1,0:T(8,128)}, u32[]{:S(2)}, u32[]{:S(2)}) collective-permute-start(f32[64,64,256]{2,1,0:T(8,128)} %get-tuple-element.134), channel_id=1, source_target_pairs={{0,1},{1,0},{2,3},{3,2},{4,5},{5,4},{6,7},{7,6}} | collective-permute-start | bytes 12582920 | tf_op jit(solution)/shard_map/ppermute | solution.py:625
  640.2 12.0 copy-start.15
  650.0 93.8 %collective-permute-start.15 = (f32[64,64,256]{2,1,0:T(8,128)}, f32[64,64,256]{2,1,0:T(8,128)}, u32[]{:S(2)}, u32[]{:S(2)}) collective-permute-start(f32[64,64,256]{2,1,0:T(8,128)} %get-tuple-element.173), channel_id=1, source_target_pairs={{0,2},{1,3},{2,0},{3,1},{4,6},{5,7},{6,4},{7,5}} | collective-permute-start | bytes 12582920 | tf_op jit(solution)/shard_map/ppermute | solution.py:625
  650.1 182.0 %collective-permute-start.16 = (f32[64,64,256]{2,1,0:T(8,128)}, f32[64,64,256]{2,1,0:T(8,128)}, u32[]{:S(2)}, u32[]{:S(2)}) collective-permute-start(f32[64,64,256]{2,1,0:T(8,128)} %get-tuple-element.172), channel_id=1, source_target_pairs={{0,3},{1,2},{2,1},{3,0},{4,7},{5,6},{6,5},{7,4}} | collective-permute-start | bytes 12582920 | tf_op jit(solution)/shard_map/ppermute | solution.py:625
  651.6 180.5 %collective-permute-start.17 = (f32[64,64,256]{2,1,0:T(8,128)S(1)}, f32[64,64,256]{2,1,0:T(8,128)}, u32[]{:S(2)}, u32[]{:S(2)}) collective-permute-start(f32[64,64,256]{2,1,0:T(8,128)S(1)} %get-tuple-element.171), channel_id=1, source_target_pairs={{0,1},{1,0},{2,3},{3,2},{4,5},{5,4},{6,7},{7,6}} | collective-permute-start | bytes 12582920 | tf_op jit(solution)/shard_map/ppermute | solution.py:625
  652.2 7.5 collective-permute-start.14
  659.7 262.9 %collective-permute-start.18 = (bf16[100,64,256]{2,1,0:T(8,128)(2,1)}, bf16[100,64,256]{2,1,0:T(8,128)(2,1)}, u32[]{:S(2)}, u32[]{:S(2)}) collective-permute-start(bf16[100,64,256]{2,1,0:T(8,128)(2,1)} %get-tuple-element.144), channel_id=1, source_target_pairs={{0,2},{1,3},{2,0},{3,1},{4,6},{5,7},{6,4},{7,5}} | collective-permute-start | bytes 9830408 | tf_op jit(solution)/shard_map/ppermute | solution.py:625
  660.0 328.8 %collective-permute-start.19 = (bf16[100,64,256]{2,1,0:T(8,128)(2,1)}, bf16[100,64,256]{2,1,0:T(8,128)(2,1)}, u32[]{:S(2)}, u32[]{:S(2)}) collective-permute-start(bf16[100,64,256]{2,1,0:T(8,128)(2,1)} %get-tuple-element.119), channel_id=1, source_target_pairs={{0,3},{1,2},{2,1},{3,0},{4,7},{5,6},{6,5},{7,4}} | collective-permute-start | bytes 9830408 | tf_op jit(solution)/shard_map/ppermute | solution.py:625
  919.3 88.0 %collective-permute-start.20 = (f32[64,64,256]{2,1,0:T(8,128)}, f32[64,64,256]{2,1,0:T(8,128)}, u32[]{:S(2)}, u32[]{:S(2)}) collective-permute-start(f32[64,64,256]{2,1,0:T(8,128)} %get-tuple-element.149), channel_id=1, source_target_pairs={{0,1},{1,0},{2,3},{3,2},{4,5},{5,4},{6,7},{7,6}} | collective-permute-start | bytes 12582920 | tf_op jit(solution)/shard_map/ppermute | solution.py:625
  921.2 182.8 %collective-permute-start.24 = (bf16[100,64,256]{2,1,0:T(8,128)(2,1)}, bf16[100,64,256]{2,1,0:T(8,128)(2,1)}, u32[]{:S(2)}, u32[]{:S(2)}) collective-permute-start(bf16[100,64,256]{2,1,0:T(8,128)(2,1)} %get-tuple-element.154), channel_id=1, source_target_pairs={{0,2},{1,3},{2,0},{3,1},{4,6},{5,7},{6,4},{7,5}} | collective-permute-start | bytes 9830408 | tf_op jit(solution)/shard_map/ppermute | solution.py:625
  921.3 193.6 %collective-permute-start.25 = (bf16[100,64,256]{2,1,0:T(8,128)(2,1)}, bf16[100,64,256]{2,1,0:T(8,128)(2,1)}, u32[]{:S(2)}, u32[]{:S(2)}) collective-permute-start(bf16[100,64,256]{2,1,0:T(8,128)(2,1)} %get-tuple-element.131), channel_id=1, source_target_pairs={{0,3},{1,2},{2,1},{3,0},{4,7},{5,6},{6,5},{7,4}} | collective-permute-start | bytes 9830408 | tf_op jit(solution)/shard_map/ppermute | solution.py:625
  922.6 272.0 %collective-permute-start.28 = (bf16[108,64,256]{2,1,0:T(8,128)(2,1)}, bf16[108,64,256]{2,1,0:T(8,128)(2,1)}, u32[]{:S(2)}, u32[]{:S(2)}) collective-permute-start(bf16[108,64,256]{2,1,0:T(8,128)(2,1)} %get-tuple-element.162), channel_id=1, source_target_pairs={{0,2},{1,3},{2,0},{3,1},{4,6},{5,7},{6,4},{7,5}} | collective-permute-start | bytes 10616840 | tf_op jit(solution)/shard_map/ppermute | solution.py:625
  923.4 51.3 %copy-start.4 = (f32[6,64,256]{2,1,0:T(8,128)S(1)}, f32[6,64,256]{2,1,0:T(8,128)}, u32[]{:S(2)}) copy-start(f32[6,64,256]{2,1,0:T(8,128)} %copy-done.3) | copy-start | bytes 1179652
  923.4 51.3 %copy-start.7 = (bf16[4,64,64]{2,1,0:T(8,128)(2,1)S(1)}, bf16[4,64,64]{2,1,0:T(8,128)(2,1)}, u32[]{:S(2)}) copy-start(bf16[4,64,64]{2,1,0:T(8,128)(2,1)} %pad_maximum_fusion.3.refs_12_.refs_11_.refs_2_.refs_1_) | copy-start | bytes 98308
  923.5 51.3 %copy-start.9 = (bf16[8,64]{1,0:T(8,128)(2,1)S(1)}, bf16[8,64]{1,0:T(8,128)(2,1)}, u32[]{:S(2)}) copy-start(bf16[8,64]{1,0:T(8,128)(2,1)} %concatenate.53.refs_13_.refs_12_.refs_3_.refs_2_) | copy-start | bytes 3076
  974.7 14.1 %copy-start.12 = (f32[8,64,256]{2,1,0:T(8,128)}, f32[8,64,256]{2,1,0:T(8,128)S(1)}, u32[]{:S(2)}) copy-start(f32[8,64,256]{2,1,0:T(8,128)S(1)} %get-tuple-element.142) | copy-start | bytes 1572868
  988.8 12.7 copy-start.21
  988.8 14.3 %copy-start.14 = (bf16[4,4,64,256]{3,2,1,0:T(8,128)(2,1)S(1)}, bf16[4,4,64,256]{3,2,1,0:T(8,128)(2,1)}, u32[]{:S(2)}) copy-start(bf16[4,4,64,256]{3,2,1,0:T(8,128)(2,1)} %get-tuple-element.141.refs_2_.refs_3_.refs_4_.refs_5_.refs_6_.refs_7_.refs_8_.refs_9_) | copy-start | bytes 1572868
  988.8 115.3 %slice-start = ((s8[6291456]{0:T(1024)(128)(4,1)}), s8[2097152]{0:T(1024)(128)(4,1)S(1)}, s32[]{:S(2)}) async-start(s8[6291456]{0:T(1024)(128)(4,1)} %bitcast.110), calls=%async_computation | async-start | bytes 4194304
  999.7 1.8 collective-permute-start.22
  1001.5 1.5 collective-permute-start.23
  1003.0 1.9 collective-permute-start.21
  1005.8 277.1 %collective-permute-start.32 = (f32[24,64,256]{2,1,0:T(8,128)}, f32[24,64,256]{2,1,0:T(8,128)}, u32[]{:S(2)}, u32[]{:S(2)}) collective-permute-start(f32[24,64,256]{2,1,0:T(8,128)} %get-tuple-element.170), channel_id=1, source_target_pairs={{0,3},{1,2},{2,1},{3,0},{4,7},{5,6},{6,5},{7,4}} | collective-permute-start | bytes 4718600 | tf_op jit(solution)/shard_map/ppermute | solution.py:625
  1007.2 248.9 %collective-permute-start.30 = (bf16[32,64,256]{2,1,0:T(8,128)(2,1)}, bf16[32,64,256]{2,1,0:T(8,128)(2,1)}, u32[]{:S(2)}, u32[]{:S(2)}) collective-permute-start(bf16[32,64,256]{2,1,0:T(8,128)(2,1)} %get-tuple-element.168), channel_id=1, source_target_pairs={{0,3},{1,2},{2,1},{3,0},{4,7},{5,6},{6,5},{7,4}} | collective-permute-start | bytes 3145736 | tf_op jit(solution)/shard_map/ppermute | solution.py:625
  1008.9 95.2 %slice-start.1 = ((s8[6291456]{0:T(1024)(128)(4,1)}), s8[4194304]{0:T(1024)(128)(4,1)S(1)}, s32[]{:S(2)}) async-start(s8[6291456]{0:T(1024)(128)(4,1)} %bitcast.110), calls=%async_computation.1 | async-start | bytes 8388608
  1008.9 95.2 %copy-start.10 = (bf16[8,64]{1,0:T(8,128)(2,1)S(1)}, bf16[8,64]{1,0:T(8,128)(2,1)}, u32[]{:S(2)}) copy-start(bf16[8,64]{1,0:T(8,128)(2,1)} %concatenate.53.refs_13_.refs_12_.refs_3_.refs_2_) | copy-start | bytes 3076
  1114.8 10.9 copy-start.24
  1114.9 12.5 copy-start.56
  1125.5 1.8 collective-permute-start.26
  1125.7 3.1 collective-permute-start.27
  1127.3 128.8 %collective-permute-start.29 = (bf16[32,64,128]{2,1,0:T(8,128)(2,1)S(1)}, bf16[32,64,128]{2,1,0:T(8,128)(2,1)S(1)}, u32[]{:S(2)}, u32[]{:S(2)}) collective-permute-start(bf16[32,64,128]{2,1,0:T(8,128)(2,1)S(1)} %copy-done.56), channel_id=1, source_target_pairs={{0,3},{1,2},{2,1},{3,0},{4,7},{5,6},{6,5},{7,4}} | collective-permute-start | bytes 1572872 | tf_op jit(solution)/shard_map/ppermute | solution.py:625
  1194.7 11.2 copy-start.13
  1205.6 56.2 %collective-permute-start.31 = (bf16[4,4,64,256]{3,2,1,0:T(8,128)(2,1)}, bf16[4,4,64,256]{3,2,1,0:T(8,128)(2,1)S(1)}, u32[]{:S(2)}, u32[]{:S(2)}) collective-permute-start(bf16[4,4,64,256]{3,2,1,0:T(8,128)(2,1)} %get-tuple-element.163.refs_1_.refs_2_.refs_3_.refs_4_), channel_id=1, source_target_pairs={{0,1},{1,0},{2,3},{3,2},{4,5},{5,4},{6,7},{7,6}} | collective-permute-start | bytes 1572872 | tf_op jit(solution)/shard_map/ppermute | solution.py:625
  1205.8 79.7 %collective-permute-start.33 = (f32[8,64,256]{2,1,0:T(8,128)S(1)}, f32[8,64,256]{2,1,0:T(8,128)S(1)}, u32[]{:S(2)}, u32[]{:S(2)}) collective-permute-start(f32[8,64,256]{2,1,0:T(8,128)S(1)} %copy-done.13), channel_id=1, source_target_pairs={{0,3},{1,2},{2,1},{3,0},{4,7},{5,6},{6,5},{7,4}} | collective-permute-start | bytes 1572872 | tf_op jit(solution)/shard_map/ppermute | solution.py:625
  (29 other events, 116.0 us)

commit v2 on v1

--- a/solution.py
+++ b/solution.py
@@ -442,6 +442,7 @@
 SLOTS = 2
 STEPS = 6
 AWAY_FIRST = 24
+HEAD_ROWS = 8
 
 
 def attention_kernel(parts, fresh, away, sc, *refs):
@@ -462,7 +463,12 @@
         return ref.at[sc[j], pl.ds(*parts[j][:2])]
 
     def z_copy(j):
-        return pltpu.make_async_copy(z_refs[j], z_in.at[rows_of(j)], z_sem.at[j])
+        start = 0 if j else HEAD_ROWS
+        size = parts[j][1] - start
+        return pltpu.make_async_copy(z_refs[j].at[pl.ds(start, size)], z_in.at[pl.ds(ROWS * j + start, size)], z_sem.at[j])
+
+    def head_copy():
+        return pltpu.make_async_copy(z_refs[0].at[pl.ds(0, HEAD_ROWS)], z_in.at[pl.ds(0, HEAD_ROWS)], z_sem.at[n])
 
     def m_copy(j):
         src = mask_away.at[0] if away and j == n - 1 else own(mask_in, j)
@@ -473,13 +479,17 @@
         return pltpu.make_async_copy(bias_refs[4 * j + r].at[parts[j][2][r]], bias_in.at[j, :, rows], b_sem.at[j])
 
     def o_copies(j):
-        if away and j == n - 1:
-            return [pltpu.make_async_copy(z_out.at[pl.ds(ROWS * j + start, ref.shape[0])], ref, o_sem.at[j])
-                    for ref, start in zip(out_away, (0, AWAY_FIRST))]
-        return [pltpu.make_async_copy(z_out.at[rows_of(j)], own(out, j), o_sem.at[j])]
+        first, size, _ = parts[j]
+        cuts = (0, size) if j < n - 1 else (0, AWAY_FIRST if away else size - TILE, size)
+        pieces = []
+        for k, (start, stop) in enumerate(zip(cuts, cuts[1:])):
+            dst = out_away[k] if away and j == n - 1 else out.at[sc[j], pl.ds(first + start, stop - start)]
+            src = z_out.at[pl.ds(ROWS * j + start, stop - start)]
+            pieces.append((ROWS * j + stop, pltpu.make_async_copy(src, dst, o_sem.at[j])))
+        return pieces
 
     starts = [f(j) for j in range(n) for f in (m_copy, *(functools.partial(b_copy, r=r) for r in range(4)))]
-    for copy in starts + [z_copy(j) for j in range(n)]:
+    for copy in starts + [head_copy()] + [z_copy(j) for j in range(n)]:
         copy.start()
     for copy in starts:
         copy.wait()
@@ -490,7 +500,7 @@
     def _(h):
         bias_t[h // HEADS, h % HEADS] = bias_in[h // HEADS, h % HEADS].astype(F32).T
 
-    z_copy(0).wait()
+    head_copy().wait()
 
     def project(row, slot):
         row = jnp.minimum(row, n_rows - 1)
@@ -573,20 +583,22 @@
                     v_s[1 - slot] = vn_s[1 - slot]
                     g_s[1 - slot] = gn_s[1 - slot]
             keep_mask(row + 2, slot)
-        for j in range(1, n):
-            @pl.when(it == (ROWS * j - 1) // STEPS - 1)
+        for j in range(n):
+            @pl.when(it == max((ROWS * j - 1) // STEPS - 1, 0))
             def _():
                 z_copy(j).wait()
 
-            @pl.when(it == (ROWS * j + 1) // STEPS)
-            def _():
-                for copy in o_copies(j - 1):
-                    copy.start()
-
-    for copy in o_copies(n - 1):
-        copy.start()
+            for stop, copy in o_copies(j):
+                if stop < n_rows:
+                    @pl.when(it == (stop + 1) // STEPS)
+                    def _():
+                        copy.start()
+
+    for stop, copy in o_copies(n - 1):
+        if stop == n_rows:
+            copy.start()
     for j in range(n):
-        for copy in o_copies(j):
+        for _, copy in o_copies(j):
             copy.wait()
 
 
@@ -600,7 +612,7 @@
     pair, wide, square, line = [pltpu.VMEM((SLOTS, *shape), dtype) for shape, dtype in (
         ((CH, COLS), BF16), ((CH, COLS), F32), ((COLS, COLS), F32), ((8, COLS), F32))]
     each = [pltpu.VMEM((n, HEADS, COLS, COLS), dtype) for dtype in (BF16, F32)]
-    sems = pltpu.SemaphoreType.DMA((n,))
+    sems, more = pltpu.SemaphoreType.DMA((n,)), pltpu.SemaphoreType.DMA((n + 1,))
     return pl.pallas_call(
         functools.partial(attention_kernel, static, fresh, away),
         out_shape=(whole, *aways),
@@ -610,7 +622,7 @@
             pltpu.VMEM((rows, CH, COLS), F32), pltpu.VMEM((rows + STEPS, CH, COLS), F32), pltpu.VMEM((rows, COLS), jnp.int32),
             pltpu.VMEM((rows, COLS), F32), *each, pltpu.VMEM((SLOTS, HEADS, CH, COLS), BF16),
             pltpu.VMEM((SLOTS, COLS, CH), BF16), pair, wide, pair, wide, pltpu.VMEM((SLOTS, COLS, LANES), F32),
-            square, square, pltpu.VMEM((COLS, COLS), BF16), line, line, wide, sems, sems, sems, sems,
+            square, square, pltpu.VMEM((COLS, COLS), BF16), line, line, wide, sems, more, sems, sems,
         ],
         compiler_params=pltpu.CompilerParams(vmem_limit_bytes=48 * MIB),
         input_output_aliases={} if fresh else {len(args) - 1: 0},

time: 1300 us -> 1300 us (level)
  transfers between devices with their start and end apart: 34 -> 34, of which waited for: 14 -> 14; matrix products, arithmetic and copies ran while one was open for 3% -> 3% of each run, Pallas kernels for 45% -> 44%
where the time goes in v2:
time: 1300 us; the launch traced here: 1290 us
  Pallas kernels  774 us (60%)
  waiting for transfers between devices  422 us (32%)
  local copies, waits for them, and re-layouts  59.5 us (5%)
  starting transfers between devices  24.6 us (2%)
    ppermute x34, waiting for transfers between devices, exchange(): return lax.ppermute(values, 'dap', [(i, i ^ r) for i in range(4)])  422 us
    pallas_call x7, Pallas kernels, attend(): pl.pallas_call(functools.partial(attention_kernel, static, fresh, away),...  390 us
    pallas_call x3, Pallas kernels, u_call(): pl.pallas_call(functools.partial(u_kernel, last, layout), out_shape=(ROW_...  262 us
    pallas_call x6, Pallas kernels, r_call(): pl.pallas_call(functools.partial(r_kernel, blocks), out_shape=[pltpu.HBM(...  59.9 us
    squeeze x6, local copies, waits for them, and re-layouts, local_block(): lax.dynamic_slice(lax.optimization_barrier((zt, *before))[0], where, (1,...  34.6 us
    pallas_call x1, Pallas kernels, l2_call(): pl.pallas_call(l2_kernel, grid=(n // 2,), out_shape=SDS((n, ROWS, CH, LAN...  33 us
    pallas_call x1, Pallas kernels, l1_call(): pl.pallas_call(l1_kernel, out_shape=(ab, ab), grid_spec=pltpu.PrefetchSca...  28.7 us
  transfers between devices with their start and end apart: 34, of which 14 were waited for; matrix products, arithmetic and copies ran while one was open for 3% of the time, Pallas kernels for 44%

profile of v2, /device:TPU:0, one launch (start us, length us, event | category | flops | bytes accessed | tf_op | source)
XLA Modules:
  0.0 1285.8 jit_solution(7525901297176373687)
XLA Ops:
  0.0 1.2 dynamic-slice_bitcast_fusion.9
  1.3 4.4 dynamic-slice_bitcast_fusion.8
  7.3 28.7 %near_projections.1 = (bf16[6,64,64,256]{3,2,1,0:T(8,128)(2,1)S(1)}, bf16[6,64,64,256]{3,2,1,0:T(8,128)(2,1)}) custom-call(s32[6]{0:T(128)S(1)} %stack.177.ids, f32[12,64,64,256]{3,2,1,0:T(8,128)} %bitcast.121, s32[12,64,256]{2,1,0:T(8,128)S(1)} %copy-done.2, f32[6,64,256]{2,1,0:T(8,128)S(1)} %broadcast_dynamic-update-slice_fusion.norms.refs_9_.refs_8_.refs_1_.refs_0_, ...), custom_call_target="tpu_custom_call" | custom-call | tf_op jit(solution)/shard_map/near_projections/pallas_call | solution.py:313
  36.1 4.6 copy-done.6
  40.7 0.8 collective-permute-start
  41.5 4.6 dynamic-slice_bitcast_fusion.7
  46.2 4.7 dynamic-slice_bitcast_fusion.6
  51.0 2.6 collective-permute-start.3
  54.0 1.5 collective-permute-start.7
  57.1 0.7 dynamic-slice_bitcast_fusion.10
  57.8 167.5 %collective-permute-done.7 = bf16[3,64,256]{2,1,0:T(8,128)(2,1)S(1)} collective-permute-done((bf16[3,64,256]{2,1,0:T(8,128)(2,1)S(1)}, bf16[3,64,256]{2,1,0:T(8,128)(2,1)S(1)}, u32[]{:S(2)}, u32[]{:S(2)}) %collective-permute-start.7) | collective-permute-done | bytes 98336 | tf_op jit(solution)/shard_map/ppermute | solution.py:637
  225.3 2.3 collective-permute-start.6
  228.2 2.4 collective-permute-done.6
  231.3 0.7 collective-permute-done.5
  232.0 1.7 collective-permute-start.1
  234.4 0.6 slice_bitcast_fusion.1
  235.6 33.0 %near_product.1.x_near = bf16[6,64,64,128]{3,2,1,0:T(8,128)(2,1)S(1)} custom-call(s32[1]{0:T(128)} %bitcast.1.sc, bf16[6,64,64,256]{3,2,1,0:T(8,128)(2,1)} %copy-done.6, bf16[6,64,64,256]{3,2,1,0:T(8,128)(2,1)} %get-tuple-element.103.b_own, bf16[6,64,64,256]{3,2,1,0:T(8,128)(2,1)} %collective-permute-done.b_par, ...), custom_call_target="tpu_custom_call" | custom-call | tf_op jit(solution)/shard_map/near_product/pallas_call | solution.py:349
  268.7 2.6 copy-done
  271.3 0.8 copy-done.27
  272.0 87.6 %pair_updates.3 = (f32[64,64,256]{2,1,0:T(8,128)}, f32[64,64,256]{2,1,0:T(8,128)}, bf16[4,4,64,256]{3,2,1,0:T(8,128)(2,1)}, bf16[100,64,256]{2,1,0:T(8,128)(2,1)}, bf16[100,64,256]{2,1,0:T(8,128)(2,1)}) custom-call(s32[2]{0:T(128)} %pad_add_fusion.14.sc, f32[12,64,64,256]{3,2,1,0:T(8,128)} %bitcast.124, f32[8,64,256]{2,1,0:T(8,128)} %copy-done.27, ...), custom_call_target="tpu_custom_call" | custom-call | tf_op jit(solution)/shard_map/pair_updates/pallas_call | solution.py:278
  359.8 9.8 dynamic-slice_bitcast_fusion.3
  369.6 1.8 collective-permute-start.11
  373.4 6.2 collective-permute-done.9.refs_6_.refs_7_.refs_8_.refs_9_
  379.5 0.8 copy-done.19
  380.3 64.1 %triangle_attention.7.refs_14_ = f32[12,64,64,256]{3,2,1,0:T(8,128)} custom-call(s32[4]{0:T(128)S(1)} %get-tuple-element.120.sc, f32[64,64,256]{2,1,0:T(8,128)} %get-tuple-element.121.refs_0_, f32[64,64,256]{2,1,0:T(8,128)} %collective-permute-done.8.refs_1_, bf16[4,4,64,256]{3,2,1,0:T(8,128)(2,1)} %get-tuple-element.123.refs_2_.refs_3_.refs_4_.refs_5_, ...), custom_call_target="tpu_custom_call" | custom-call | tf_op jit(solution)/shard_map/triangle_attention/pallas_call | solution.py:616
  444.4 19.0 %collective-permute-done.10.refs_1_ = f32[64,64,256]{2,1,0:T(8,128)} collective-permute-done((f32[64,64,256]{2,1,0:T(8,128)}, f32[64,64,256]{2,1,0:T(8,128)}, u32[]{:S(2)}, u32[]{:S(2)}) %collective-permute-start.10) | collective-permute-done | bytes 4194336 | tf_op jit(solution)/shard_map/ppermute | solution.py:637
  463.4 88.8 %collective-permute-done.11.refs_2_ = f32[64,64,256]{2,1,0:T(8,128)} collective-permute-done((f32[64,64,256]{2,1,0:T(8,128)}, f32[64,64,256]{2,1,0:T(8,128)}, u32[]{:S(2)}, u32[]{:S(2)}) %collective-permute-start.11) | collective-permute-done | bytes 4194336 | tf_op jit(solution)/shard_map/ppermute | solution.py:637
  552.2 87.6 %pair_updates.4 = (f32[64,64,256]{2,1,0:T(8,128)}, f32[64,64,256]{2,1,0:T(8,128)}, bf16[4,4,64,256]{3,2,1,0:T(8,128)(2,1)}, bf16[100,64,256]{2,1,0:T(8,128)(2,1)}, bf16[100,64,256]{2,1,0:T(8,128)(2,1)}) custom-call(s32[2]{0:T(128)} %pad_add_fusion.13.sc, f32[12,64,64,256]{3,2,1,0:T(8,128)} %bitcast.126, f32[64,64,256]{2,1,0:T(8,128)} %collective-permute-done.10.refs_1_, ...), custom_call_target="tpu_custom_call" | custom-call | tf_op jit(solution)/shard_map/pair_updates/pallas_call | solution.py:278
  640.2 9.8 dynamic-slice_bitcast_fusion
  650.1 1.5 collective-permute-start.16
  652.2 7.5 collective-permute-done.14.refs_6_.refs_7_.refs_8_.refs_9_
  660.0 1.5 collective-permute-start.19
  661.5 0.7 pad_add_fusion.12.sc
  662.1 64.1 %triangle_attention.8.refs_15_ = f32[12,64,64,256]{3,2,1,0:T(8,128)} custom-call(s32[4]{0:T(128)S(1)} %get-tuple-element.132.sc, f32[64,64,256]{2,1,0:T(8,128)} %get-tuple-element.133.refs_0_, f32[64,64,256]{2,1,0:T(8,128)} %collective-permute-done.13.refs_1_, ...), custom_call_target="tpu_custom_call", output_to_operand_aliasing={{}: (15, {})} | custom-call | tf_op jit(solution)/shard_map/triangle_attention/pallas_call | solution.py:616
  726.3 17.5 %collective-permute-done.15.refs_1_ = f32[64,64,256]{2,1,0:T(8,128)} collective-permute-done((f32[64,64,256]{2,1,0:T(8,128)}, f32[64,64,256]{2,1,0:T(8,128)}, u32[]{:S(2)}, u32[]{:S(2)}) %collective-permute-start.15) | collective-permute-done | bytes 4194336 | tf_op jit(solution)/shard_map/ppermute | solution.py:637
  743.8 88.3 %collective-permute-done.16.refs_2_ = f32[64,64,256]{2,1,0:T(8,128)} collective-permute-done((f32[64,64,256]{2,1,0:T(8,128)}, f32[64,64,256]{2,1,0:T(8,128)}, u32[]{:S(2)}, u32[]{:S(2)}) %collective-permute-start.16) | collective-permute-done | bytes 4194336 | tf_op jit(solution)/shard_map/ppermute | solution.py:637
  832.1 87.2 %pair_updates.5 = (f32[64,64,256]{2,1,0:T(8,128)}, f32[64,64,256]{2,1,0:T(8,128)}, bf16[4,4,64,256]{3,2,1,0:T(8,128)(2,1)}, bf16[108,64,256]{2,1,0:T(8,128)(2,1)...) custom-call(s32[2]{0:T(128)} %pad_add_fusion.12.sc, ...), custom_call_target="tpu_custom_call" | custom-call | tf_op jit(solution)/shard_map/pair_updates/pallas_call | solution.py:278
  919.3 2.0 collective-permute-start.20
  921.3 1.4 collective-permute-start.25
  922.6 0.6 collective-permute-start.28
  923.5 50.1 %triangle_attention.9 = (f32[12,64,64,256]{3,2,1,0:T(8,128)}, f32[24,64,256]{2,1,0:T(8,128)}, f32[8,64,256]{2,1,0:T(8,128)S(1)}) custom-call(s32[4]{0:T(128)S(1)} %get-tuple-element.139.sc, f32[64,64,256]{2,1,0:T(8,128)} %get-tuple-element.140.refs_0_, f32[32,64,256]{2,1,0:T(8,128)} %get-tuple-element.138.refs_1_, ...), custom_call_target="tpu_custom_call", output_to_operand_aliasing={{0}: (16, {})} | custom-call | tf_op jit(solution)/shard_map/triangle_attention/pallas_call | solution.py:616
  973.7 2.9 copy-done.1
  976.6 11.0 row_updates.6
  987.7 10.9 row_updates.7
  998.8 1.6 collective-permute-done.22.refs_8_.refs_10_
  1000.5 1.4 collective-permute-done.23.refs_12_.refs_14_
  1002.1 1.8 collective-permute-done.21.refs_3_.refs_4_.refs_5_.refs_6_
  1003.9 0.8 copy-done.18
  1004.7 1.5 collective-permute-start.32
  1007.8 95.5 %triangle_attention.10.refs_14_ = f32[12,64,64,256]{3,2,1,0:T(8,128)} custom-call(s32[6]{0:T(128)S(1)} %copy-done.11, f32[64,64,256]{2,1,0:T(8,128)} %collective-permute-done.20.refs_0_, f32[64,64,256]{2,1,0:T(8,128)} %get-tuple-element.150.refs_1_, f32[64,64,256]{2,1,0:T(8,128)} %get-tuple-element.151.refs_2_, ...), custom_call_target="tpu_custom_call", output_to_operand_aliasing={{}: (20, {})} | custom-call | tf_op jit(solution)/shard_map/triangle_attention/pallas_call | solution.py:616
  1103.4 10.7 row_updates.8
  1114.1 10.7 row_updates.9
  1125.5 1.1 collective-permute-done.26.refs_3_.refs_5_
  1126.5 1.5 collective-permute-start.29
  1128.0 0.7 copy-done.26
  1128.7 64.1 %triangle_attention.11.refs_9_ = f32[12,64,64,256]{3,2,1,0:T(8,128)} custom-call(s32[4]{0:T(128)S(1)} %pad_add_fusion.7.sc, f32[64,64,256]{2,1,0:T(8,128)} %get-tuple-element.159.refs_0_, f32[64,64,256]{2,1,0:T(8,128)} %get-tuple-element.160.refs_1_, bf16[2,4,64,256]{3,2,1,0:T(8,128)(2,1)} %get-tuple-element.155.refs_2_.refs_4_, ...), custom_call_target="tpu_custom_call", output_to_operand_aliasing={{}: (15, {})} | custom-call | tf_op jit(solution)/shard_map/triangle_attention/pallas_call | solution.py:616
  1192.8 10.9 row_updates.10
  1204.6 32.9 %triangle_attention.12.refs_9_ = f32[12,64,64,256]{3,2,1,0:T(8,128)} custom-call(s32[2]{0:T(128)S(1)} %pad_add_fusion.5.sc, f32[64,64,256]{2,1,0:T(8,128)} %get-tuple-element.165.refs_0_, bf16[4,4,64,256]{3,2,1,0:T(8,128)(2,1)} %get-tuple-element.163.refs_1_.refs_2_.refs_3_.refs_4_, ...), custom_call_target="tpu_custom_call", output_to_operand_aliasing={{}: (10, {})} | custom-call | tf_op jit(solution)/shard_map/triangle_attention/pallas_call | solution.py:616
  1237.5 18.6 %collective-permute-done.29.x_far = bf16[32,64,128]{2,1,0:T(8,128)(2,1)S(1)} collective-permute-done((bf16[32,64,128]{2,1,0:T(8,128)(2,1)S(1)}, bf16[32,64,128]{2,1,0:T(8,128)(2,1)S(1)}, u32[]{:S(2)}, u32[]{:S(2)}) %collective-permute-start.29) | collective-permute-done | bytes 524320 | tf_op jit(solution)/shard_map/ppermute | solution.py:637
  1256.1 5.7 row_updates.11.refs_0_
  1261.8 0.8 copy-done.17
  1262.6 19.5 %triangle_attention.13 = f32[12,64,64,256]{3,2,1,0:T(8,128)} custom-call(s32[2]{0:T(128)S(1)} %pad_add_fusion.3.sc, f32[32,64,256]{2,1,0:T(8,128)} %row_updates.11.refs_0_, bf16[4,4,64,256]{3,2,1,0:T(8,128)(2,1)} %copy-done.17, bf16[4,4,64,256]{3,2,1,0:T(8,128)(2,1)} %copy-done.17, ...), custom_call_target="tpu_custom_call", output_to_operand_aliasing={{}: (10, {})} | custom-call | tf_op jit(solution)/shard_map/triangle_attention/pallas_call | solution.py:616
  1282.1 2.7 bitcast_dynamic-update-slice_fusion
  1284.8 0.8 bitcast_dynamic-update-slice_fusion.1
  (211 shorter events, 13.0 us)
Async XLA Ops:
  6.9 29.2 %copy-start.8 = (bf16[2,256,64]{2,1,0:T(8,128)(2,1)}, bf16[2,256,64]{2,1,0:T(8,128)(2,1)S(1)}, u32[]{:S(2)}) copy-start(bf16[2,256,64]{2,1,0:T(8,128)(2,1)S(1)} %pad_maximum_fusion.1.w_ab.refs_11_.refs_10_) | copy-start | bytes 196612
  7.3 28.8 %copy-start.3 = (f32[6,64,256]{2,1,0:T(8,128)}, f32[6,64,256]{2,1,0:T(8,128)S(1)}, u32[]{:S(2)}) copy-start(f32[6,64,256]{2,1,0:T(8,128)S(1)} %broadcast_dynamic-update-slice_fusion.norms.refs_9_.refs_8_.refs_1_.refs_0_) | copy-start | bytes 1179652
  40.7 195.0 %collective-permute-start = (bf16[6,64,64,256]{3,2,1,0:T(8,128)(2,1)}, bf16[6,64,64,256]{3,2,1,0:T(8,128)(2,1)}, u32[]{:S(2)}, u32[]{:S(2)}) collective-permute-start(bf16[6,64,64,256]{3,2,1,0:T(8,128)(2,1)} %get-tuple-element.103.b_own), channel_id=1, source_target_pairs={{0,1},{1,0},{2,3},{3,2},{4,5},{5,4},{6,7},{7,6}} | collective-permute-start | bytes 37748744 | tf_op jit(solution)/shard_map/ppermute | solution.py:637
  46.2 9.4 copy-start.37
  46.2 9.5 copy-start.38
  46.2 9.6 copy-start.39
  46.2 9.7 copy-start.47
  46.2 10.3 copy-start.52
  46.2 10.4 copy-start.53
  46.2 10.5 copy-start.54
  46.2 10.6 copy-start.55
  51.0 220.3 %collective-permute-start.4 = (f32[64,64,256]{2,1,0:T(8,128)}, f32[64,64,256]{2,1,0:T(8,128)}, u32[]{:S(2)}, u32[]{:S(2)}) collective-permute-start(f32[64,64,256]{2,1,0:T(8,128)} %dynamic-slice_bitcast_fusion.6), channel_id=1, source_target_pairs={{0,1},{1,0},{2,3},{3,2},{4,5},{5,4},{6,7},{7,6}} | collective-permute-start | bytes 12582920 | tf_op jit(solution)/shard_map/ppermute | solution.py:637
  51.0 220.3 %collective-permute-start.3 = (f32[64,64,256]{2,1,0:T(8,128)}, f32[64,64,256]{2,1,0:T(8,128)}, u32[]{:S(2)}, u32[]{:S(2)}) collective-permute-start(f32[64,64,256]{2,1,0:T(8,128)} %dynamic-slice_bitcast_fusion.7), channel_id=1, source_target_pairs={{0,3},{1,2},{2,1},{3,0},{4,7},{5,6},{6,5},{7,4}} | collective-permute-start | bytes 12582920 | tf_op jit(solution)/shard_map/ppermute | solution.py:637
  53.6 217.7 %collective-permute-start.2 = (f32[56,64,256]{2,1,0:T(8,128)}, f32[56,64,256]{2,1,0:T(8,128)}, u32[]{:S(2)}, u32[]{:S(2)}) collective-permute-start(f32[56,64,256]{2,1,0:T(8,128)} %dynamic-slice_bitcast_fusion.8), channel_id=1, source_target_pairs={{0,2},{1,3},{2,0},{3,1},{4,6},{5,7},{6,4},{7,5}} | collective-permute-start | bytes 11010056 | tf_op jit(solution)/shard_map/ppermute | solution.py:637
  54.0 171.4 %collective-permute-start.7 = (bf16[3,64,256]{2,1,0:T(8,128)(2,1)S(1)}, bf16[3,64,256]{2,1,0:T(8,128)(2,1)S(1)}, u32[]{:S(2)}, u32[]{:S(2)}) collective-permute-start(bf16[3,64,256]{2,1,0:T(8,128)(2,1)S(1)} %get-tuple-element.180), channel_id=1, source_target_pairs={{0,3},{1,2},{2,1},{3,0},{4,7},{5,6},{6,5},{7,4}} | collective-permute-start | bytes 294920 | tf_op jit(solution)/shard_map/ppermute | solution.py:637
  57.1 211.6 %copy-start.5 = (f32[4,64,8,128]{3,2,1,0:T(8,128)}, f32[4,64,8,128]{3,2,1,0:T(8,128)S(1)}, u32[]{:S(2)}) copy-start(f32[4,64,8,128]{3,2,1,0:T(8,128)S(1)} %pad_maximum_fusion.xgs.refs_10_.refs_9_) | copy-start | bytes 3145732
  225.3 5.4 collective-permute-start.6
  230.7 1.3 collective-permute-start.5
  232.0 39.3 %collective-permute-start.1 = (f32[8,64,256]{2,1,0:T(8,128)S(1)}, f32[8,64,256]{2,1,0:T(8,128)S(1)}, u32[]{:S(2)}, u32[]{:S(2)}) collective-permute-start(f32[8,64,256]{2,1,0:T(8,128)S(1)} %dynamic-slice_bitcast_fusion.9), channel_id=1, source_target_pairs={{0,2},{1,3},{2,0},{3,1},{4,6},{5,7},{6,4},{7,5}} | collective-permute-start | bytes 1572872 | tf_op jit(solution)/shard_map/ppermute | solution.py:637
  359.7 12.1 copy-start.40
  359.7 12.1 copy-start.41
  359.7 12.2 copy-start.42
  359.7 12.3 copy-start.43
  359.7 12.4 copy-start.44
  359.8 12.6 copy-start.16
  359.8 19.8 %collective-permute-start.8 = (f32[64,64,256]{2,1,0:T(8,128)}, f32[64,64,256]{2,1,0:T(8,128)}, u32[]{:S(2)}, u32[]{:S(2)}) collective-permute-start(f32[64,64,256]{2,1,0:T(8,128)} %get-tuple-element.122), channel_id=1, source_target_pairs={{0,1},{1,0},{2,3},{3,2},{4,5},{5,4},{6,7},{7,6}} | collective-permute-start | bytes 12582920 | tf_op jit(solution)/shard_map/ppermute | solution.py:637
  369.6 93.8 %collective-permute-start.10 = (f32[64,64,256]{2,1,0:T(8,128)}, f32[64,64,256]{2,1,0:T(8,128)}, u32[]{:S(2)}, u32[]{:S(2)}) collective-permute-start(f32[64,64,256]{2,1,0:T(8,128)} %get-tuple-element.176), channel_id=1, source_target_pairs={{0,2},{1,3},{2,0},{3,1},{4,6},{5,7},{6,4},{7,5}} | collective-permute-start | bytes 12582920 | tf_op jit(solution)/shard_map/ppermute | solution.py:637
  369.6 182.6 %collective-permute-start.11 = (f32[64,64,256]{2,1,0:T(8,128)}, f32[64,64,256]{2,1,0:T(8,128)}, u32[]{:S(2)}, u32[]{:S(2)}) collective-permute-start(f32[64,64,256]{2,1,0:T(8,128)} %get-tuple-element.175), channel_id=1, source_target_pairs={{0,3},{1,2},{2,1},{3,0},{4,7},{5,6},{6,5},{7,4}} | collective-permute-start | bytes 12582920 | tf_op jit(solution)/shard_map/ppermute | solution.py:637
  371.4 180.8 %collective-permute-start.12 = (f32[64,64,256]{2,1,0:T(8,128)}, f32[64,64,256]{2,1,0:T(8,128)}, u32[]{:S(2)}, u32[]{:S(2)}) collective-permute-start(f32[64,64,256]{2,1,0:T(8,128)} %get-tuple-element.174), channel_id=1, source_target_pairs={{0,1},{1,0},{2,3},{3,2},{4,5},{5,4},{6,7},{7,6}} | collective-permute-start | bytes 12582920 | tf_op jit(solution)/shard_map/ppermute | solution.py:637
  372.4 7.2 collective-permute-start.9
  639.8 20.2 %collective-permute-start.13 = (f32[64,64,256]{2,1,0:T(8,128)}, f32[64,64,256]{2,1,0:T(8,128)}, u32[]{:S(2)}, u32[]{:S(2)}) collective-permute-start(f32[64,64,256]{2,1,0:T(8,128)} %get-tuple-element.134), channel_id=1, source_target_pairs={{0,1},{1,0},{2,3},{3,2},{4,5},{5,4},{6,7},{7,6}} | collective-permute-start | bytes 12582920 | tf_op jit(solution)/shard_map/ppermute | solution.py:637
  640.2 12.0 copy-start.15
  650.0 93.8 %collective-permute-start.15 = (f32[64,64,256]{2,1,0:T(8,128)}, f32[64,64,256]{2,1,0:T(8,128)}, u32[]{:S(2)}, u32[]{:S(2)}) collective-permute-start(f32[64,64,256]{2,1,0:T(8,128)} %get-tuple-element.173), channel_id=1, source_target_pairs={{0,2},{1,3},{2,0},{3,1},{4,6},{5,7},{6,4},{7,5}} | collective-permute-start | bytes 12582920 | tf_op jit(solution)/shard_map/ppermute | solution.py:637
  650.1 182.0 %collective-permute-start.16 = (f32[64,64,256]{2,1,0:T(8,128)}, f32[64,64,256]{2,1,0:T(8,128)}, u32[]{:S(2)}, u32[]{:S(2)}) collective-permute-start(f32[64,64,256]{2,1,0:T(8,128)} %get-tuple-element.172), channel_id=1, source_target_pairs={{0,3},{1,2},{2,1},{3,0},{4,7},{5,6},{6,5},{7,4}} | collective-permute-start | bytes 12582920 | tf_op jit(solution)/shard_map/ppermute | solution.py:637
  651.6 180.5 %collective-permute-start.17 = (f32[64,64,256]{2,1,0:T(8,128)S(1)}, f32[64,64,256]{2,1,0:T(8,128)}, u32[]{:S(2)}, u32[]{:S(2)}) collective-permute-start(f32[64,64,256]{2,1,0:T(8,128)S(1)} %get-tuple-element.171), channel_id=1, source_target_pairs={{0,1},{1,0},{2,3},{3,2},{4,5},{5,4},{6,7},{7,6}} | collective-permute-start | bytes 12582920 | tf_op jit(solution)/shard_map/ppermute | solution.py:637
  652.2 7.5 collective-permute-start.14
  659.7 262.9 %collective-permute-start.18 = (bf16[100,64,256]{2,1,0:T(8,128)(2,1)}, bf16[100,64,256]{2,1,0:T(8,128)(2,1)}, u32[]{:S(2)}, u32[]{:S(2)}) collective-permute-start(bf16[100,64,256]{2,1,0:T(8,128)(2,1)} %get-tuple-element.144), channel_id=1, source_target_pairs={{0,2},{1,3},{2,0},{3,1},{4,6},{5,7},{6,4},{7,5}} | collective-permute-start | bytes 9830408 | tf_op jit(solution)/shard_map/ppermute | solution.py:637
  660.0 327.7 %collective-permute-start.19 = (bf16[100,64,256]{2,1,0:T(8,128)(2,1)}, bf16[100,64,256]{2,1,0:T(8,128)(2,1)}, u32[]{:S(2)}, u32[]{:S(2)}) collective-permute-start(bf16[100,64,256]{2,1,0:T(8,128)(2,1)} %get-tuple-element.119), channel_id=1, source_target_pairs={{0,3},{1,2},{2,1},{3,0},{4,7},{5,6},{6,5},{7,4}} | collective-permute-start | bytes 9830408 | tf_op jit(solution)/shard_map/ppermute | solution.py:637
  919.3 86.9 %collective-permute-start.20 = (f32[64,64,256]{2,1,0:T(8,128)}, f32[64,64,256]{2,1,0:T(8,128)}, u32[]{:S(2)}, u32[]{:S(2)}) collective-permute-start(f32[64,64,256]{2,1,0:T(8,128)} %get-tuple-element.149), channel_id=1, source_target_pairs={{0,1},{1,0},{2,3},{3,2},{4,5},{5,4},{6,7},{7,6}} | collective-permute-start | bytes 12582920 | tf_op jit(solution)/shard_map/ppermute | solution.py:637
  921.2 182.1 %collective-permute-start.24 = (bf16[100,64,256]{2,1,0:T(8,128)(2,1)}, bf16[100,64,256]{2,1,0:T(8,128)(2,1)}, u32[]{:S(2)}, u32[]{:S(2)}) collective-permute-start(bf16[100,64,256]{2,1,0:T(8,128)(2,1)} %get-tuple-element.154), channel_id=1, source_target_pairs={{0,2},{1,3},{2,0},{3,1},{4,6},{5,7},{6,4},{7,5}} | collective-permute-start | bytes 9830408 | tf_op jit(solution)/shard_map/ppermute | solution.py:637
  921.3 192.8 %collective-permute-start.25 = (bf16[100,64,256]{2,1,0:T(8,128)(2,1)}, bf16[100,64,256]{2,1,0:T(8,128)(2,1)}, u32[]{:S(2)}, u32[]{:S(2)}) collective-permute-start(bf16[100,64,256]{2,1,0:T(8,128)(2,1)} %get-tuple-element.131), channel_id=1, source_target_pairs={{0,3},{1,2},{2,1},{3,0},{4,7},{5,6},{6,5},{7,4}} | collective-permute-start | bytes 9830408 | tf_op jit(solution)/shard_map/ppermute | solution.py:637
  922.6 270.2 %collective-permute-start.28 = (bf16[108,64,256]{2,1,0:T(8,128)(2,1)}, bf16[108,64,256]{2,1,0:T(8,128)(2,1)}, u32[]{:S(2)}, u32[]{:S(2)}) collective-permute-start(bf16[108,64,256]{2,1,0:T(8,128)(2,1)} %get-tuple-element.162), channel_id=1, source_target_pairs={{0,2},{1,3},{2,0},{3,1},{4,6},{5,7},{6,4},{7,5}} | collective-permute-start | bytes 10616840 | tf_op jit(solution)/shard_map/ppermute | solution.py:637
  923.4 50.2 %copy-start.4 = (f32[6,64,256]{2,1,0:T(8,128)S(1)}, f32[6,64,256]{2,1,0:T(8,128)}, u32[]{:S(2)}) copy-start(f32[6,64,256]{2,1,0:T(8,128)} %copy-done.3) | copy-start | bytes 1179652
  923.4 50.2 %copy-start.7 = (bf16[4,64,64]{2,1,0:T(8,128)(2,1)S(1)}, bf16[4,64,64]{2,1,0:T(8,128)(2,1)}, u32[]{:S(2)}) copy-start(bf16[4,64,64]{2,1,0:T(8,128)(2,1)} %pad_maximum_fusion.3.refs_12_.refs_11_.refs_2_.refs_1_) | copy-start | bytes 98308
  923.5 50.2 %copy-start.9 = (bf16[8,64]{1,0:T(8,128)(2,1)S(1)}, bf16[8,64]{1,0:T(8,128)(2,1)}, u32[]{:S(2)}) copy-start(bf16[8,64]{1,0:T(8,128)(2,1)} %concatenate.53.refs_13_.refs_12_.refs_3_.refs_2_) | copy-start | bytes 3076
  973.6 14.0 %copy-start.12 = (f32[8,64,256]{2,1,0:T(8,128)}, f32[8,64,256]{2,1,0:T(8,128)S(1)}, u32[]{:S(2)}) copy-start(f32[8,64,256]{2,1,0:T(8,128)S(1)} %get-tuple-element.142) | copy-start | bytes 1572868
  987.7 12.7 copy-start.21
  987.7 14.3 %copy-start.14 = (bf16[4,4,64,256]{3,2,1,0:T(8,128)(2,1)S(1)}, bf16[4,4,64,256]{3,2,1,0:T(8,128)(2,1)}, u32[]{:S(2)}) copy-start(bf16[4,4,64,256]{3,2,1,0:T(8,128)(2,1)} %get-tuple-element.141.refs_2_.refs_3_.refs_4_.refs_5_.refs_6_.refs_7_.refs_8_.refs_9_) | copy-start | bytes 1572868
  987.7 115.6 %slice-start = ((s8[6291456]{0:T(1024)(128)(4,1)}), s8[2097152]{0:T(1024)(128)(4,1)S(1)}, s32[]{:S(2)}) async-start(s8[6291456]{0:T(1024)(128)(4,1)} %bitcast.110), calls=%async_computation | async-start | bytes 4194304
  998.6 1.8 collective-permute-start.22
  1000.4 1.5 collective-permute-start.23
  1002.0 1.9 collective-permute-start.21
  1004.7 277.4 %collective-permute-start.32 = (f32[24,64,256]{2,1,0:T(8,128)}, f32[24,64,256]{2,1,0:T(8,128)}, u32[]{:S(2)}, u32[]{:S(2)}) collective-permute-start(f32[24,64,256]{2,1,0:T(8,128)} %get-tuple-element.170), channel_id=1, source_target_pairs={{0,3},{1,2},{2,1},{3,0},{4,7},{5,6},{6,5},{7,4}} | collective-permute-start | bytes 4718600 | tf_op jit(solution)/shard_map/ppermute | solution.py:637
  1006.1 250.0 %collective-permute-start.30 = (bf16[32,64,256]{2,1,0:T(8,128)(2,1)}, bf16[32,64,256]{2,1,0:T(8,128)(2,1)}, u32[]{:S(2)}, u32[]{:S(2)}) collective-permute-start(bf16[32,64,256]{2,1,0:T(8,128)(2,1)} %get-tuple-element.168), channel_id=1, source_target_pairs={{0,3},{1,2},{2,1},{3,0},{4,7},{5,6},{6,5},{7,4}} | collective-permute-start | bytes 3145736 | tf_op jit(solution)/shard_map/ppermute | solution.py:637
  1007.8 95.6 %slice-start.1 = ((s8[6291456]{0:T(1024)(128)(4,1)}), s8[4194304]{0:T(1024)(128)(4,1)S(1)}, s32[]{:S(2)}) async-start(s8[6291456]{0:T(1024)(128)(4,1)} %bitcast.110), calls=%async_computation.1 | async-start | bytes 8388608
  1007.8 95.6 %copy-start.10 = (bf16[8,64]{1,0:T(8,128)(2,1)S(1)}, bf16[8,64]{1,0:T(8,128)(2,1)}, u32[]{:S(2)}) copy-start(bf16[8,64]{1,0:T(8,128)(2,1)} %concatenate.53.refs_13_.refs_12_.refs_3_.refs_2_) | copy-start | bytes 3076
  1114.1 11.0 copy-start.24
  1114.1 12.5 copy-start.56
  1124.8 1.8 collective-permute-start.26
  1125.1 2.9 collective-permute-start.27
  1126.5 129.6 %collective-permute-start.29 = (bf16[32,64,128]{2,1,0:T(8,128)(2,1)S(1)}, bf16[32,64,128]{2,1,0:T(8,128)(2,1)S(1)}, u32[]{:S(2)}, u32[]{:S(2)}) collective-permute-start(bf16[32,64,128]{2,1,0:T(8,128)(2,1)S(1)} %copy-done.56), channel_id=1, source_target_pairs={{0,3},{1,2},{2,1},{3,0},{4,7},{5,6},{6,5},{7,4}} | collective-permute-start | bytes 1572872 | tf_op jit(solution)/shard_map/ppermute | solution.py:637
  1192.8 11.2 copy-start.13
  1203.8 58.0 %collective-permute-start.31 = (bf16[4,4,64,256]{3,2,1,0:T(8,128)(2,1)}, bf16[4,4,64,256]{3,2,1,0:T(8,128)(2,1)S(1)}, u32[]{:S(2)}, u32[]{:S(2)}) collective-permute-start(bf16[4,4,64,256]{3,2,1,0:T(8,128)(2,1)} %get-tuple-element.163.refs_1_.refs_2_.refs_3_.refs_4_), channel_id=1, source_target_pairs={{0,1},{1,0},{2,3},{3,2},{4,5},{5,4},{6,7},{7,6}} | collective-permute-start | bytes 1572872 | tf_op jit(solution)/shard_map/ppermute | solution.py:637
  1204.0 80.8 %collective-permute-start.33 = (f32[8,64,256]{2,1,0:T(8,128)S(1)}, f32[8,64,256]{2,1,0:T(8,128)S(1)}, u32[]{:S(2)}, u32[]{:S(2)}) collective-permute-start(f32[8,64,256]{2,1,0:T(8,128)S(1)} %copy-done.13), channel_id=1, source_target_pairs={{0,3},{1,2},{2,1},{3,0},{4,7},{5,6},{6,5},{7,4}} | collective-permute-start | bytes 1572872 | tf_op jit(solution)/shard_map/ppermute | solution.py:637
  (29 other events, 116.0 us)

commit v3 on v2

--- a/solution.py
+++ b/solution.py
@@ -110,7 +110,7 @@
 
     for ref, (r, start) in zip(z_refs, layout):
         src = ref if r else ref.at[sample]
-        rows = pl.ds(pl.multiple_of(ROWS * (me ^ r) + start, 8), src.shape[0])
+        rows = pl.ds(ROWS * (me ^ r) + start, src.shape[0])
         pltpu.make_async_copy(src, z_s.at[rows], in_sem.at[r]).start()
     for r, part in enumerate((mask0, mask1, mask2, mask3)):
         mask[pl.ds(pl.multiple_of(ROWS * (me ^ r), ROWS), ROWS), :] = part[:].astype(F32)
@@ -441,7 +441,7 @@
 CHUNK = 32
 SLOTS = 2
 STEPS = 6
-AWAY_FIRST = 24
+AWAY_FIRST = 28
 HEAD_ROWS = 8
 
 
@@ -630,7 +630,7 @@
     )(*args)
 
 
-FIRST = 8
+FIRST = 4
 
 
 def exchange(values, r):

time: 1300 us -> 1310 us (level)
  no operation moved by 1% of the time
where the time goes in v3:
time: 1310 us; the launch traced here: 1300 us
  Pallas kernels  774 us (59%)
  waiting for transfers between devices  433 us (33%)
  local copies, waits for them, and re-layouts  59.5 us (5%)
  starting transfers between devices  24.7 us (2%)
    ppermute x34, waiting for transfers between devices, exchange(): return lax.ppermute(values, 'dap', [(i, i ^ r) for i in range(4)])  433 us
    pallas_call x7, Pallas kernels, attend(): pl.pallas_call(functools.partial(attention_kernel, static, fresh, away),...  390 us
    pallas_call x3, Pallas kernels, u_call(): pl.pallas_call(functools.partial(u_kernel, last, layout), out_shape=(ROW_...  262 us
    pallas_call x6, Pallas kernels, r_call(): pl.pallas_call(functools.partial(r_kernel, blocks), out_shape=[pltpu.HBM(...  59.9 us
    squeeze x6, local copies, waits for them, and re-layouts, local_block(): lax.dynamic_slice(lax.optimization_barrier((zt, *before))[0], where, (1,...  34.7 us
    pallas_call x1, Pallas kernels, l2_call(): pl.pallas_call(l2_kernel, grid=(n // 2,), out_shape=SDS((n, ROWS, CH, LAN...  33 us
    pallas_call x1, Pallas kernels, l1_call(): pl.pallas_call(l1_kernel, out_shape=(ab, ab), grid_spec=pltpu.PrefetchSca...  28.7 us
  transfers between devices with their start and end apart: 34, of which 14 were waited for; matrix products, arithmetic and copies ran while one was open for 3% of the time, Pallas kernels for 44%

profile of v3, /device:TPU:0, one launch (start us, length us, event | category | flops | bytes accessed | tf_op | source)
XLA Modules:
  0.0 1296.5 jit_solution(15362582706195904022)
XLA Ops:
  0.0 1.0 dynamic-slice_bitcast_fusion.9
  1.2 4.6 dynamic-slice_bitcast_fusion.8
  7.4 28.7 %near_projections.1 = (bf16[6,64,64,256]{3,2,1,0:T(8,128)(2,1)S(1)}, bf16[6,64,64,256]{3,2,1,0:T(8,128)(2,1)}) custom-call(s32[6]{0:T(128)S(1)} %stack.177.ids, f32[12,64,64,256]{3,2,1,0:T(8,128)} %bitcast.121, s32[12,64,256]{2,1,0:T(8,128)S(1)} %copy-done.2, f32[6,64,256]{2,1,0:T(8,128)S(1)} %broadcast_dynamic-update-slice_fusion.norms.refs_9_.refs_8_.refs_1_.refs_0_, ...), custom_call_target="tpu_custom_call" | custom-call | tf_op jit(solution)/shard_map/near_projections/pallas_call | solution.py:313
  36.1 4.6 copy-done.6
  40.7 0.8 collective-permute-start
  41.6 4.6 dynamic-slice_bitcast_fusion.7
  46.3 4.7 dynamic-slice_bitcast_fusion.6
  51.0 2.6 collective-permute-start.3
  54.0 1.5 collective-permute-start.7
  57.8 0.7 pad_maximum_fusion.3.refs_12_.refs_11_.refs_2_.refs_1_
  58.5 172.5 %collective-permute-done.7 = bf16[3,64,256]{2,1,0:T(8,128)(2,1)S(1)} collective-permute-done((bf16[3,64,256]{2,1,0:T(8,128)(2,1)S(1)}, bf16[3,64,256]{2,1,0:T(8,128)(2,1)S(1)}, u32[]{:S(2)}, u32[]{:S(2)}) %collective-permute-start.7) | collective-permute-done | bytes 98336 | tf_op jit(solution)/shard_map/ppermute | solution.py:637
  231.0 2.3 collective-permute-start.6
  233.8 2.5 collective-permute-done.6
  237.0 0.7 collective-permute-done.5
  237.7 1.7 collective-permute-start.1
  240.7 33.0 %near_product.1.x_near = bf16[6,64,64,128]{3,2,1,0:T(8,128)(2,1)S(1)} custom-call(s32[1]{0:T(128)} %bitcast.1.sc, bf16[6,64,64,256]{3,2,1,0:T(8,128)(2,1)} %copy-done.6, bf16[6,64,64,256]{3,2,1,0:T(8,128)(2,1)} %get-tuple-element.103.b_own, bf16[6,64,64,256]{3,2,1,0:T(8,128)(2,1)} %collective-permute-done.b_par, ...), custom_call_target="tpu_custom_call" | custom-call | tf_op jit(solution)/shard_map/near_product/pallas_call | solution.py:349
  273.7 2.6 copy-done
  276.3 0.7 copy-done.27
  277.0 87.6 %pair_updates.3 = (f32[64,64,256]{2,1,0:T(8,128)}, f32[64,64,256]{2,1,0:T(8,128)}, bf16[4,4,64,256]{3,2,1,0:T(8,128)(2,1)}, bf16[100,64,256]{2,1,0:T(8,128)(2,1)}, bf16[100,64,256]{2,1,0:T(8,128)(2,1)}) custom-call(s32[2]{0:T(128)} %pad_add_fusion.14.sc, f32[12,64,64,256]{3,2,1,0:T(8,128)} %bitcast.124, f32[4,64,256]{2,1,0:T(8,128)} %copy-done.27, ...), custom_call_target="tpu_custom_call" | custom-call | tf_op jit(solution)/shard_map/pair_updates/pallas_call | solution.py:278
  364.7 9.8 dynamic-slice_bitcast_fusion.3
  374.5 1.8 collective-permute-start.11
  378.2 6.2 collective-permute-done.9.refs_6_.refs_7_.refs_8_.refs_9_
  384.5 0.8 copy-done.19
  385.2 64.1 %triangle_attention.7.refs_14_ = f32[12,64,64,256]{3,2,1,0:T(8,128)} custom-call(s32[4]{0:T(128)S(1)} %get-tuple-element.120.sc, f32[64,64,256]{2,1,0:T(8,128)} %get-tuple-element.121.refs_0_, f32[64,64,256]{2,1,0:T(8,128)} %collective-permute-done.8.refs_1_, bf16[4,4,64,256]{3,2,1,0:T(8,128)(2,1)} %get-tuple-element.123.refs_2_.refs_3_.refs_4_.refs_5_, ...), custom_call_target="tpu_custom_call" | custom-call | tf_op jit(solution)/shard_map/triangle_attention/pallas_call | solution.py:616
  449.3 18.9 %collective-permute-done.10.refs_1_ = f32[64,64,256]{2,1,0:T(8,128)} collective-permute-done((f32[64,64,256]{2,1,0:T(8,128)}, f32[64,64,256]{2,1,0:T(8,128)}, u32[]{:S(2)}, u32[]{:S(2)}) %collective-permute-start.10) | collective-permute-done | bytes 4194336 | tf_op jit(solution)/shard_map/ppermute | solution.py:637
  468.3 88.8 %collective-permute-done.11.refs_2_ = f32[64,64,256]{2,1,0:T(8,128)} collective-permute-done((f32[64,64,256]{2,1,0:T(8,128)}, f32[64,64,256]{2,1,0:T(8,128)}, u32[]{:S(2)}, u32[]{:S(2)}) %collective-permute-start.11) | collective-permute-done | bytes 4194336 | tf_op jit(solution)/shard_map/ppermute | solution.py:637
  557.1 87.6 %pair_updates.4 = (f32[64,64,256]{2,1,0:T(8,128)}, f32[64,64,256]{2,1,0:T(8,128)}, bf16[4,4,64,256]{3,2,1,0:T(8,128)(2,1)}, bf16[100,64,256]{2,1,0:T(8,128)(2,1)}, bf16[100,64,256]{2,1,0:T(8,128)(2,1)}) custom-call(s32[2]{0:T(128)} %pad_add_fusion.13.sc, f32[12,64,64,256]{3,2,1,0:T(8,128)} %bitcast.126, f32[64,64,256]{2,1,0:T(8,128)} %collective-permute-done.10.refs_1_, ...), custom_call_target="tpu_custom_call" | custom-call | tf_op jit(solution)/shard_map/pair_updates/pallas_call | solution.py:278
  645.1 9.8 dynamic-slice_bitcast_fusion
  655.0 1.5 collective-permute-start.16
  657.1 7.5 collective-permute-done.14.refs_6_.refs_7_.refs_8_.refs_9_
  664.9 1.5 collective-permute-start.19
  667.0 64.1 %triangle_attention.8.refs_15_ = f32[12,64,64,256]{3,2,1,0:T(8,128)} custom-call(s32[4]{0:T(128)S(1)} %get-tuple-element.132.sc, f32[64,64,256]{2,1,0:T(8,128)} %get-tuple-element.133.refs_0_, f32[64,64,256]{2,1,0:T(8,128)} %collective-permute-done.13.refs_1_, ...), custom_call_target="tpu_custom_call", output_to_operand_aliasing={{}: (15, {})} | custom-call | tf_op jit(solution)/shard_map/triangle_attention/pallas_call | solution.py:616
  731.1 17.6 %collective-permute-done.15.refs_1_ = f32[64,64,256]{2,1,0:T(8,128)} collective-permute-done((f32[64,64,256]{2,1,0:T(8,128)}, f32[64,64,256]{2,1,0:T(8,128)}, u32[]{:S(2)}, u32[]{:S(2)}) %collective-permute-start.15) | collective-permute-done | bytes 4194336 | tf_op jit(solution)/shard_map/ppermute | solution.py:637
  748.7 88.2 %collective-permute-done.16.refs_2_ = f32[64,64,256]{2,1,0:T(8,128)} collective-permute-done((f32[64,64,256]{2,1,0:T(8,128)}, f32[64,64,256]{2,1,0:T(8,128)}, u32[]{:S(2)}, u32[]{:S(2)}) %collective-permute-start.16) | collective-permute-done | bytes 4194336 | tf_op jit(solution)/shard_map/ppermute | solution.py:637
  837.0 87.2 %pair_updates.5 = (f32[64,64,256]{2,1,0:T(8,128)}, f32[64,64,256]{2,1,0:T(8,128)}, bf16[4,4,64,256]{3,2,1,0:T(8,128)(2,1)}, bf16[108,64,256]{2,1,0:T(8,128)(2,1)...) custom-call(s32[2]{0:T(128)} %pad_add_fusion.12.sc, ...), custom_call_target="tpu_custom_call" | custom-call | tf_op jit(solution)/shard_map/pair_updates/pallas_call | solution.py:278
  924.2 2.0 collective-permute-start.20
  926.2 1.4 collective-permute-start.25
  927.6 0.6 collective-permute-start.28
  928.4 50.1 %triangle_attention.9 = (f32[12,64,64,256]{3,2,1,0:T(8,128)}, f32[28,64,256]{2,1,0:T(8,128)}, f32[4,64,256]{2,1,0:T(8,128)S(1)}) custom-call(s32[4]{0:T(128)S(1)} %get-tuple-element.139.sc, f32[64,64,256]{2,1,0:T(8,128)} %get-tuple-element.140.refs_0_, f32[32,64,256]{2,1,0:T(8,128)} %get-tuple-element.138.refs_1_, ...), custom_call_target="tpu_custom_call", output_to_operand_aliasing={{0}: (16, {})} | custom-call | tf_op jit(solution)/shard_map/triangle_attention/pallas_call | solution.py:616
  978.6 2.9 copy-done.1
  981.4 11.0 row_updates.6
  992.5 10.9 row_updates.7
  1003.6 1.6 collective-permute-done.22.refs_8_.refs_10_
  1005.4 1.4 collective-permute-done.23.refs_12_.refs_14_
  1006.9 1.8 collective-permute-done.21.refs_3_.refs_4_.refs_5_.refs_6_
  1008.7 0.8 copy-done.18
  1009.5 1.5 collective-permute-start.32
  1011.2 0.7 stack.163.sc
  1012.0 0.7 copy-done.11
  1012.7 95.5 %triangle_attention.10.refs_14_ = f32[12,64,64,256]{3,2,1,0:T(8,128)} custom-call(s32[6]{0:T(128)S(1)} %copy-done.11, f32[64,64,256]{2,1,0:T(8,128)} %collective-permute-done.20.refs_0_, f32[64,64,256]{2,1,0:T(8,128)} %get-tuple-element.150.refs_1_, f32[64,64,256]{2,1,0:T(8,128)} %get-tuple-element.151.refs_2_, ...), custom_call_target="tpu_custom_call", output_to_operand_aliasing={{}: (20, {})} | custom-call | tf_op jit(solution)/shard_map/triangle_attention/pallas_call | solution.py:616
  1108.3 10.7 row_updates.8
  1119.0 10.7 row_updates.9
  1130.4 1.1 collective-permute-done.26.refs_3_.refs_5_
  1131.5 1.5 collective-permute-start.29
  1132.9 0.7 copy-done.26
  1133.6 64.1 %triangle_attention.11.refs_9_ = f32[12,64,64,256]{3,2,1,0:T(8,128)} custom-call(s32[4]{0:T(128)S(1)} %pad_add_fusion.7.sc, f32[64,64,256]{2,1,0:T(8,128)} %get-tuple-element.159.refs_0_, f32[64,64,256]{2,1,0:T(8,128)} %get-tuple-element.160.refs_1_, bf16[2,4,64,256]{3,2,1,0:T(8,128)(2,1)} %get-tuple-element.155.refs_2_.refs_4_, ...), custom_call_target="tpu_custom_call", output_to_operand_aliasing={{}: (15, {})} | custom-call | tf_op jit(solution)/shard_map/triangle_attention/pallas_call | solution.py:616
  1197.8 10.9 row_updates.10
  1209.5 32.9 %triangle_attention.12.refs_9_ = f32[12,64,64,256]{3,2,1,0:T(8,128)} custom-call(s32[2]{0:T(128)S(1)} %pad_add_fusion.5.sc, f32[64,64,256]{2,1,0:T(8,128)} %get-tuple-element.165.refs_0_, bf16[4,4,64,256]{3,2,1,0:T(8,128)(2,1)} %get-tuple-element.163.refs_1_.refs_2_.refs_3_.refs_4_, ...), custom_call_target="tpu_custom_call", output_to_operand_aliasing={{}: (10, {})} | custom-call | tf_op jit(solution)/shard_map/triangle_attention/pallas_call | solution.py:616
  1242.4 24.2 %collective-permute-done.29.x_far = bf16[32,64,128]{2,1,0:T(8,128)(2,1)S(1)} collective-permute-done((bf16[32,64,128]{2,1,0:T(8,128)(2,1)S(1)}, bf16[32,64,128]{2,1,0:T(8,128)(2,1)S(1)}, u32[]{:S(2)}, u32[]{:S(2)}) %collective-permute-start.29) | collective-permute-done | bytes 524320 | tf_op jit(solution)/shard_map/ppermute | solution.py:637
  1266.6 5.7 row_updates.11.refs_0_
  1272.3 0.8 copy-done.17
  1273.1 19.5 %triangle_attention.13 = f32[12,64,64,256]{3,2,1,0:T(8,128)} custom-call(s32[2]{0:T(128)S(1)} %pad_add_fusion.3.sc, f32[32,64,256]{2,1,0:T(8,128)} %row_updates.11.refs_0_, bf16[4,4,64,256]{3,2,1,0:T(8,128)(2,1)} %copy-done.17, bf16[4,4,64,256]{3,2,1,0:T(8,128)(2,1)} %copy-done.17, ...), custom_call_target="tpu_custom_call", output_to_operand_aliasing={{}: (10, {})} | custom-call | tf_op jit(solution)/shard_map/triangle_attention/pallas_call | solution.py:616
  1292.6 2.9 bitcast_dynamic-update-slice_fusion
  1295.6 0.7 bitcast_dynamic-update-slice_fusion.1
  (211 shorter events, 12.9 us)
Async XLA Ops:
  6.9 29.2 %copy-start.8 = (bf16[2,256,64]{2,1,0:T(8,128)(2,1)}, bf16[2,256,64]{2,1,0:T(8,128)(2,1)S(1)}, u32[]{:S(2)}) copy-start(bf16[2,256,64]{2,1,0:T(8,128)(2,1)S(1)} %pad_maximum_fusion.1.w_ab.refs_11_.refs_10_) | copy-start | bytes 196612
  7.3 28.8 %copy-start.3 = (f32[6,64,256]{2,1,0:T(8,128)}, f32[6,64,256]{2,1,0:T(8,128)S(1)}, u32[]{:S(2)}) copy-start(f32[6,64,256]{2,1,0:T(8,128)S(1)} %broadcast_dynamic-update-slice_fusion.norms.refs_9_.refs_8_.refs_1_.refs_0_) | copy-start | bytes 1179652
  40.7 199.9 %collective-permute-start = (bf16[6,64,64,256]{3,2,1,0:T(8,128)(2,1)}, bf16[6,64,64,256]{3,2,1,0:T(8,128)(2,1)}, u32[]{:S(2)}, u32[]{:S(2)}) collective-permute-start(bf16[6,64,64,256]{3,2,1,0:T(8,128)(2,1)} %get-tuple-element.103.b_own), channel_id=1, source_target_pairs={{0,1},{1,0},{2,3},{3,2},{4,5},{5,4},{6,7},{7,6}} | collective-permute-start | bytes 37748744 | tf_op jit(solution)/shard_map/ppermute | solution.py:637
  46.2 9.3 copy-start.37
  46.2 9.4 copy-start.38
  46.2 9.6 copy-start.39
  46.3 9.7 copy-start.47
  46.3 10.9 copy-start.52
  46.3 11.0 copy-start.53
  46.3 11.1 copy-start.54
  46.3 11.2 copy-start.55
  51.0 225.3 %collective-permute-start.4 = (f32[64,64,256]{2,1,0:T(8,128)}, f32[64,64,256]{2,1,0:T(8,128)}, u32[]{:S(2)}, u32[]{:S(2)}) collective-permute-start(f32[64,64,256]{2,1,0:T(8,128)} %dynamic-slice_bitcast_fusion.6), channel_id=1, source_target_pairs={{0,1},{1,0},{2,3},{3,2},{4,5},{5,4},{6,7},{7,6}} | collective-permute-start | bytes 12582920 | tf_op jit(solution)/shard_map/ppermute | solution.py:637
  51.0 225.3 %collective-permute-start.3 = (f32[64,64,256]{2,1,0:T(8,128)}, f32[64,64,256]{2,1,0:T(8,128)}, u32[]{:S(2)}, u32[]{:S(2)}) collective-permute-start(f32[64,64,256]{2,1,0:T(8,128)} %dynamic-slice_bitcast_fusion.7), channel_id=1, source_target_pairs={{0,3},{1,2},{2,1},{3,0},{4,7},{5,6},{6,5},{7,4}} | collective-permute-start | bytes 12582920 | tf_op jit(solution)/shard_map/ppermute | solution.py:637
  53.6 222.7 %collective-permute-start.2 = (f32[60,64,256]{2,1,0:T(8,128)}, f32[60,64,256]{2,1,0:T(8,128)}, u32[]{:S(2)}, u32[]{:S(2)}) collective-permute-start(f32[60,64,256]{2,1,0:T(8,128)} %dynamic-slice_bitcast_fusion.8), channel_id=1, source_target_pairs={{0,2},{1,3},{2,0},{3,1},{4,6},{5,7},{6,4},{7,5}} | collective-permute-start | bytes 11796488 | tf_op jit(solution)/shard_map/ppermute | solution.py:637
  54.0 177.0 %collective-permute-start.7 = (bf16[3,64,256]{2,1,0:T(8,128)(2,1)S(1)}, bf16[3,64,256]{2,1,0:T(8,128)(2,1)S(1)}, u32[]{:S(2)}, u32[]{:S(2)}) collective-permute-start(bf16[3,64,256]{2,1,0:T(8,128)(2,1)S(1)} %get-tuple-element.180), channel_id=1, source_target_pairs={{0,3},{1,2},{2,1},{3,0},{4,7},{5,6},{6,5},{7,4}} | collective-permute-start | bytes 294920 | tf_op jit(solution)/shard_map/ppermute | solution.py:637
  57.8 216.0 %copy-start.5 = (f32[4,64,8,128]{3,2,1,0:T(8,128)}, f32[4,64,8,128]{3,2,1,0:T(8,128)S(1)}, u32[]{:S(2)}) copy-start(f32[4,64,8,128]{3,2,1,0:T(8,128)S(1)} %pad_maximum_fusion.xgs.refs_10_.refs_9_) | copy-start | bytes 3145732
  231.0 5.4 collective-permute-start.6
  236.4 1.3 collective-permute-start.5
  237.7 38.6 %collective-permute-start.1 = (f32[4,64,256]{2,1,0:T(8,128)S(1)}, f32[4,64,256]{2,1,0:T(8,128)S(1)}, u32[]{:S(2)}, u32[]{:S(2)}) collective-permute-start(f32[4,64,256]{2,1,0:T(8,128)S(1)} %dynamic-slice_bitcast_fusion.9), channel_id=1, source_target_pairs={{0,2},{1,3},{2,0},{3,1},{4,6},{5,7},{6,4},{7,5}} | collective-permute-start | bytes 786440 | tf_op jit(solution)/shard_map/ppermute | solution.py:637
  364.6 12.1 copy-start.40
  364.6 12.1 copy-start.41
  364.6 12.2 copy-start.42
  364.7 12.3 copy-start.43
  364.7 12.4 copy-start.44
  364.7 12.6 copy-start.16
  364.7 19.8 %collective-permute-start.8 = (f32[64,64,256]{2,1,0:T(8,128)}, f32[64,64,256]{2,1,0:T(8,128)}, u32[]{:S(2)}, u32[]{:S(2)}) collective-permute-start(f32[64,64,256]{2,1,0:T(8,128)} %get-tuple-element.122), channel_id=1, source_target_pairs={{0,1},{1,0},{2,3},{3,2},{4,5},{5,4},{6,7},{7,6}} | collective-permute-start | bytes 12582920 | tf_op jit(solution)/shard_map/ppermute | solution.py:637
  374.5 93.8 %collective-permute-start.10 = (f32[64,64,256]{2,1,0:T(8,128)}, f32[64,64,256]{2,1,0:T(8,128)}, u32[]{:S(2)}, u32[]{:S(2)}) collective-permute-start(f32[64,64,256]{2,1,0:T(8,128)} %get-tuple-element.176), channel_id=1, source_target_pairs={{0,2},{1,3},{2,0},{3,1},{4,6},{5,7},{6,4},{7,5}} | collective-permute-start | bytes 12582920 | tf_op jit(solution)/shard_map/ppermute | solution.py:637
  374.5 182.6 %collective-permute-start.11 = (f32[64,64,256]{2,1,0:T(8,128)}, f32[64,64,256]{2,1,0:T(8,128)}, u32[]{:S(2)}, u32[]{:S(2)}) collective-permute-start(f32[64,64,256]{2,1,0:T(8,128)} %get-tuple-element.175), channel_id=1, source_target_pairs={{0,3},{1,2},{2,1},{3,0},{4,7},{5,6},{6,5},{7,4}} | collective-permute-start | bytes 12582920 | tf_op jit(solution)/shard_map/ppermute | solution.py:637
  376.3 180.8 %collective-permute-start.12 = (f32[64,64,256]{2,1,0:T(8,128)}, f32[64,64,256]{2,1,0:T(8,128)}, u32[]{:S(2)}, u32[]{:S(2)}) collective-permute-start(f32[64,64,256]{2,1,0:T(8,128)} %get-tuple-element.174), channel_id=1, source_target_pairs={{0,1},{1,0},{2,3},{3,2},{4,5},{5,4},{6,7},{7,6}} | collective-permute-start | bytes 12582920 | tf_op jit(solution)/shard_map/ppermute | solution.py:637
  377.3 7.2 collective-permute-start.9
  644.7 20.2 %collective-permute-start.13 = (f32[64,64,256]{2,1,0:T(8,128)}, f32[64,64,256]{2,1,0:T(8,128)}, u32[]{:S(2)}, u32[]{:S(2)}) collective-permute-start(f32[64,64,256]{2,1,0:T(8,128)} %get-tuple-element.134), channel_id=1, source_target_pairs={{0,1},{1,0},{2,3},{3,2},{4,5},{5,4},{6,7},{7,6}} | collective-permute-start | bytes 12582920 | tf_op jit(solution)/shard_map/ppermute | solution.py:637
  645.1 12.0 copy-start.15
  655.0 93.8 %collective-permute-start.15 = (f32[64,64,256]{2,1,0:T(8,128)}, f32[64,64,256]{2,1,0:T(8,128)}, u32[]{:S(2)}, u32[]{:S(2)}) collective-permute-start(f32[64,64,256]{2,1,0:T(8,128)} %get-tuple-element.173), channel_id=1, source_target_pairs={{0,2},{1,3},{2,0},{3,1},{4,6},{5,7},{6,4},{7,5}} | collective-permute-start | bytes 12582920 | tf_op jit(solution)/shard_map/ppermute | solution.py:637
  655.0 182.0 %collective-permute-start.16 = (f32[64,64,256]{2,1,0:T(8,128)}, f32[64,64,256]{2,1,0:T(8,128)}, u32[]{:S(2)}, u32[]{:S(2)}) collective-permute-start(f32[64,64,256]{2,1,0:T(8,128)} %get-tuple-element.172), channel_id=1, source_target_pairs={{0,3},{1,2},{2,1},{3,0},{4,7},{5,6},{6,5},{7,4}} | collective-permute-start | bytes 12582920 | tf_op jit(solution)/shard_map/ppermute | solution.py:637
  656.5 180.5 %collective-permute-start.17 = (f32[64,64,256]{2,1,0:T(8,128)S(1)}, f32[64,64,256]{2,1,0:T(8,128)}, u32[]{:S(2)}, u32[]{:S(2)}) collective-permute-start(f32[64,64,256]{2,1,0:T(8,128)S(1)} %get-tuple-element.171), channel_id=1, source_target_pairs={{0,1},{1,0},{2,3},{3,2},{4,5},{5,4},{6,7},{7,6}} | collective-permute-start | bytes 12582920 | tf_op jit(solution)/shard_map/ppermute | solution.py:637
  657.1 7.5 collective-permute-start.14
  664.6 262.9 %collective-permute-start.18 = (bf16[100,64,256]{2,1,0:T(8,128)(2,1)}, bf16[100,64,256]{2,1,0:T(8,128)(2,1)}, u32[]{:S(2)}, u32[]{:S(2)}) collective-permute-start(bf16[100,64,256]{2,1,0:T(8,128)(2,1)} %get-tuple-element.144), channel_id=1, source_target_pairs={{0,2},{1,3},{2,0},{3,1},{4,6},{5,7},{6,4},{7,5}} | collective-permute-start | bytes 9830408 | tf_op jit(solution)/shard_map/ppermute | solution.py:637
  664.9 327.6 %collective-permute-start.19 = (bf16[100,64,256]{2,1,0:T(8,128)(2,1)}, bf16[100,64,256]{2,1,0:T(8,128)(2,1)}, u32[]{:S(2)}, u32[]{:S(2)}) collective-permute-start(bf16[100,64,256]{2,1,0:T(8,128)(2,1)} %get-tuple-element.119), channel_id=1, source_target_pairs={{0,3},{1,2},{2,1},{3,0},{4,7},{5,6},{6,5},{7,4}} | collective-permute-start | bytes 9830408 | tf_op jit(solution)/shard_map/ppermute | solution.py:637
  924.2 86.8 %collective-permute-start.20 = (f32[64,64,256]{2,1,0:T(8,128)}, f32[64,64,256]{2,1,0:T(8,128)}, u32[]{:S(2)}, u32[]{:S(2)}) collective-permute-start(f32[64,64,256]{2,1,0:T(8,128)} %get-tuple-element.149), channel_id=1, source_target_pairs={{0,1},{1,0},{2,3},{3,2},{4,5},{5,4},{6,7},{7,6}} | collective-permute-start | bytes 12582920 | tf_op jit(solution)/shard_map/ppermute | solution.py:637
  926.2 182.1 %collective-permute-start.24 = (bf16[100,64,256]{2,1,0:T(8,128)(2,1)}, bf16[100,64,256]{2,1,0:T(8,128)(2,1)}, u32[]{:S(2)}, u32[]{:S(2)}) collective-permute-start(bf16[100,64,256]{2,1,0:T(8,128)(2,1)} %get-tuple-element.154), channel_id=1, source_target_pairs={{0,2},{1,3},{2,0},{3,1},{4,6},{5,7},{6,4},{7,5}} | collective-permute-start | bytes 9830408 | tf_op jit(solution)/shard_map/ppermute | solution.py:637
  926.2 192.8 %collective-permute-start.25 = (bf16[100,64,256]{2,1,0:T(8,128)(2,1)}, bf16[100,64,256]{2,1,0:T(8,128)(2,1)}, u32[]{:S(2)}, u32[]{:S(2)}) collective-permute-start(bf16[100,64,256]{2,1,0:T(8,128)(2,1)} %get-tuple-element.131), channel_id=1, source_target_pairs={{0,3},{1,2},{2,1},{3,0},{4,7},{5,6},{6,5},{7,4}} | collective-permute-start | bytes 9830408 | tf_op jit(solution)/shard_map/ppermute | solution.py:637
  927.6 270.2 %collective-permute-start.28 = (bf16[108,64,256]{2,1,0:T(8,128)(2,1)}, bf16[108,64,256]{2,1,0:T(8,128)(2,1)}, u32[]{:S(2)}, u32[]{:S(2)}) collective-permute-start(bf16[108,64,256]{2,1,0:T(8,128)(2,1)} %get-tuple-element.162), channel_id=1, source_target_pairs={{0,2},{1,3},{2,0},{3,1},{4,6},{5,7},{6,4},{7,5}} | collective-permute-start | bytes 10616840 | tf_op jit(solution)/shard_map/ppermute | solution.py:637
  928.4 50.2 %copy-start.4 = (f32[6,64,256]{2,1,0:T(8,128)S(1)}, f32[6,64,256]{2,1,0:T(8,128)}, u32[]{:S(2)}) copy-start(f32[6,64,256]{2,1,0:T(8,128)} %copy-done.3) | copy-start | bytes 1179652
  928.4 50.2 %copy-start.7 = (bf16[4,64,64]{2,1,0:T(8,128)(2,1)S(1)}, bf16[4,64,64]{2,1,0:T(8,128)(2,1)}, u32[]{:S(2)}) copy-start(bf16[4,64,64]{2,1,0:T(8,128)(2,1)} %pad_maximum_fusion.3.refs_12_.refs_11_.refs_2_.refs_1_) | copy-start | bytes 98308
  928.4 50.2 %copy-start.9 = (bf16[8,64]{1,0:T(8,128)(2,1)S(1)}, bf16[8,64]{1,0:T(8,128)(2,1)}, u32[]{:S(2)}) copy-start(bf16[8,64]{1,0:T(8,128)(2,1)} %concatenate.53.refs_13_.refs_12_.refs_3_.refs_2_) | copy-start | bytes 3076
  978.5 14.0 %copy-start.12 = (f32[4,64,256]{2,1,0:T(8,128)}, f32[4,64,256]{2,1,0:T(8,128)S(1)}, u32[]{:S(2)}) copy-start(f32[4,64,256]{2,1,0:T(8,128)S(1)} %get-tuple-element.142) | copy-start | bytes 786436
  992.5 12.7 copy-start.21
  992.5 14.3 %copy-start.14 = (bf16[4,4,64,256]{3,2,1,0:T(8,128)(2,1)S(1)}, bf16[4,4,64,256]{3,2,1,0:T(8,128)(2,1)}, u32[]{:S(2)}) copy-start(bf16[4,4,64,256]{3,2,1,0:T(8,128)(2,1)} %get-tuple-element.141.refs_2_.refs_3_.refs_4_.refs_5_.refs_6_.refs_7_.refs_8_.refs_9_) | copy-start | bytes 1572868
  992.5 115.7 %slice-start = ((s8[6291456]{0:T(1024)(128)(4,1)}), s8[2097152]{0:T(1024)(128)(4,1)S(1)}, s32[]{:S(2)}) async-start(s8[6291456]{0:T(1024)(128)(4,1)} %bitcast.110), calls=%async_computation | async-start | bytes 4194304
  1003.5 1.8 collective-permute-start.22
  1005.2 1.5 collective-permute-start.23
  1006.8 1.9 collective-permute-start.21
  1009.5 283.1 %collective-permute-start.32 = (f32[28,64,256]{2,1,0:T(8,128)}, f32[28,64,256]{2,1,0:T(8,128)}, u32[]{:S(2)}, u32[]{:S(2)}) collective-permute-start(f32[28,64,256]{2,1,0:T(8,128)} %get-tuple-element.170), channel_id=1, source_target_pairs={{0,3},{1,2},{2,1},{3,0},{4,7},{5,6},{6,5},{7,4}} | collective-permute-start | bytes 5505032 | tf_op jit(solution)/shard_map/ppermute | solution.py:637
  1010.9 255.7 %collective-permute-start.30 = (bf16[32,64,256]{2,1,0:T(8,128)(2,1)}, bf16[32,64,256]{2,1,0:T(8,128)(2,1)}, u32[]{:S(2)}, u32[]{:S(2)}) collective-permute-start(bf16[32,64,256]{2,1,0:T(8,128)(2,1)} %get-tuple-element.168), channel_id=1, source_target_pairs={{0,3},{1,2},{2,1},{3,0},{4,7},{5,6},{6,5},{7,4}} | collective-permute-start | bytes 3145736 | tf_op jit(solution)/shard_map/ppermute | solution.py:637
  1012.7 95.6 %slice-start.1 = ((s8[6291456]{0:T(1024)(128)(4,1)}), s8[4194304]{0:T(1024)(128)(4,1)S(1)}, s32[]{:S(2)}) async-start(s8[6291456]{0:T(1024)(128)(4,1)} %bitcast.110), calls=%async_computation.1 | async-start | bytes 8388608
  1012.7 95.6 %copy-start.10 = (bf16[8,64]{1,0:T(8,128)(2,1)S(1)}, bf16[8,64]{1,0:T(8,128)(2,1)}, u32[]{:S(2)}) copy-start(bf16[8,64]{1,0:T(8,128)(2,1)} %concatenate.53.refs_13_.refs_12_.refs_3_.refs_2_) | copy-start | bytes 3076
  1119.0 11.0 copy-start.24
  1119.0 12.5 copy-start.56
  1129.7 1.8 collective-permute-start.26
  1130.0 2.9 collective-permute-start.27
  1131.5 135.1 %collective-permute-start.29 = (bf16[32,64,128]{2,1,0:T(8,128)(2,1)S(1)}, bf16[32,64,128]{2,1,0:T(8,128)(2,1)S(1)}, u32[]{:S(2)}, u32[]{:S(2)}) collective-permute-start(bf16[32,64,128]{2,1,0:T(8,128)(2,1)S(1)} %copy-done.56), channel_id=1, source_target_pairs={{0,3},{1,2},{2,1},{3,0},{4,7},{5,6},{6,5},{7,4}} | collective-permute-start | bytes 1572872 | tf_op jit(solution)/shard_map/ppermute | solution.py:637
  1197.7 11.3 copy-start.13
  1208.7 63.6 %collective-permute-start.31 = (bf16[4,4,64,256]{3,2,1,0:T(8,128)(2,1)}, bf16[4,4,64,256]{3,2,1,0:T(8,128)(2,1)S(1)}, u32[]{:S(2)}, u32[]{:S(2)}) collective-permute-start(bf16[4,4,64,256]{3,2,1,0:T(8,128)(2,1)} %get-tuple-element.163.refs_1_.refs_2_.refs_3_.refs_4_), channel_id=1, source_target_pairs={{0,1},{1,0},{2,3},{3,2},{4,5},{5,4},{6,7},{7,6}} | collective-permute-start | bytes 1572872 | tf_op jit(solution)/shard_map/ppermute | solution.py:637
  1209.1 86.5 %collective-permute-start.33 = (f32[4,64,256]{2,1,0:T(8,128)S(1)}, f32[4,64,256]{2,1,0:T(8,128)S(1)}, u32[]{:S(2)}, u32[]{:S(2)}) collective-permute-start(f32[4,64,256]{2,1,0:T(8,128)S(1)} %copy-done.13), channel_id=1, source_target_pairs={{0,3},{1,2},{2,1},{3,0},{4,7},{5,6},{6,5},{7,4}} | collective-permute-start | bytes 786440 | tf_op jit(solution)/shard_map/ppermute | solution.py:637
  (29 other events, 118.6 us)

commit v4 on v3

--- a/solution.py
+++ b/solution.py
@@ -12,6 +12,7 @@
 F32, BF16 = jnp.float32, jnp.bfloat16
 ROWS, CH, COLS = 64, 64, 256
 TILE = 16
+SUB = 8
 MIB = 1 << 20
 OUT, IN, ATT = range(3)
 
@@ -147,11 +148,14 @@
         jobs = [(r == 2, narrow, far2.at[half, :, side])] if outgoing else [
             (r == 0, z_tile, z2_own.at[rows]), (r == 1, z_tile, z2_par.at[rows]), (r == 2, wide, far2.at[rows])]
         if last:
-            near_rows, away_rows = (pl.ds(pl.multiple_of(TILE * row, TILE), TILE)
-                                    for row in (jnp.minimum(q, CHUNKS - 1), jnp.maximum(q - CHUNKS, 0)))
-            jobs += [((r == 3) & (q < CHUNKS), *((narrow, far3[1].at[near_rows]) if outgoing else (wide, far3[0].at[near_rows])))]
+            whole = pl.ds(pl.multiple_of(TILE * jnp.minimum(q, CHUNKS - 1), TILE), TILE)
+            src, dst = (narrow, far3[1]) if outgoing else (wide, far3[0])
+            jobs += [((r == 3) & (q < CHUNKS), src, dst.at[whole]),
+                     ((r == 3) & (q == CHUNKS), src.at[pl.ds(0, SPLIT)], dst.at[pl.ds(CHUNKS * TILE, SPLIT)])]
             if not outgoing:
-                jobs += [((r == 3) & (q >= CHUNKS), z_tile, far3[-1].at[away_rows])]
+                rest = TILE - SPLIT
+                jobs += [((r == 3) & (q == CHUNKS), z_tile.at[pl.ds(SPLIT, rest)], far3[-1].at[pl.ds(0, rest)]),
+                         ((r == 3) & (q > CHUNKS), z_tile, far3[-1].at[pl.ds(rest, TILE)])]
         else:
             jobs += [(r == 3, narrow, far3[0].at[half, :, side]) if outgoing else (r == 3, wide, far3[0].at[rows])]
         for when, src, dst in jobs:
@@ -265,7 +269,8 @@
 FAR_BIAS = ROWS + ROWS // 2
 FAR = SDS((FAR_BIAS + 4, CH, COLS), BF16)
 CHUNKS = 2
-SOME = CHUNKS * TILE
+SOME = 34
+SPLIT = SOME - CHUNKS * TILE
 AWAY = SDS((ROWS - SOME, CH, COLS), F32)
 SOME_FULL = SDS((SOME, CH, COLS), BF16)
 SOME_HALF = SDS((SOME, CH, LANES), BF16)
@@ -363,12 +368,12 @@
     norms, w_sq, w_bias, z_out, *refs = refs
     swap, refs = (refs[0], refs[1:]) if blocks else (None, refs)
     tile_d, tile_z, z_buf, sem = refs
-    step, steps = pl.program_id(0), pl.num_programs(0)
+    step, steps, tile = pl.program_id(0), pl.num_programs(0), xi.shape[0]
     first = sc[0] < 2
     out_norm, in_norm, att_norm = [norm_of(norms, place) for place in (OUT, IN, ATT)]
 
     def z_copy(n):
-        return pltpu.make_async_copy(z_buf.at[n % 2], z_out.at[pl.ds(pl.multiple_of(n * TILE, TILE), TILE)], sem.at[n % 2])
+        return pltpu.make_async_copy(z_buf.at[n % 2], z_out.at[pl.ds(n * tile, tile)], sem.at[n % 2])
 
     @pl.when(step >= 2)
     def _():
@@ -399,7 +404,7 @@
     def bias_row(i, normed):
         tile_d[i] = mm(w_bias[:], normed)
 
-    staggered(TILE, outgoing, norm_one, incoming, norm_two, *([bias_row] if blocks else []))
+    staggered(tile, outgoing, norm_one, incoming, norm_two, *([bias_row] if blocks else []))
     z_copy(step).start()
     if blocks:
         swap[0, :, pl.ds(pl.multiple_of(step * TILE, TILE), TILE), :] = swap_major(tile_d[:])[:4].astype(BF16)
@@ -417,20 +422,21 @@
 
 def r_call(blocks, sc, zt, x_near, x_far, xi, norms, w_sq, w_bias):
     steps = ROWS // TILE if blocks else CHUNKS
+    tile = TILE if blocks else SOME // steps
     far_map = (lambda i, sc: (ROWS // TILE + i % 2, 0, i // 2)) if blocks else (lambda i, sc: (i, 0, 0))
     return pl.pallas_call(
         functools.partial(r_kernel, blocks),
-        out_shape=[pltpu.HBM((steps * TILE, CH, COLS), F32)] + [pltpu.HBM((blocks + 1, 4, ROWS, COLS), BF16)] * (blocks > 0),
+        out_shape=[pltpu.HBM((steps * tile, CH, COLS), F32)] + [pltpu.HBM((blocks + 1, 4, ROWS, COLS), BF16)] * (blocks > 0),
         grid_spec=pltpu.PrefetchScalarGridSpec(
             num_scalar_prefetch=1, grid=(steps,),
-            in_specs=[pl.BlockSpec((1, TILE, CH, COLS), lambda i, sc: (sc[1], i, 0, 0)),
-                      pl.BlockSpec((1, TILE, CH, LANES), lambda i, sc: (sc[2], i, 0, 0)),
-                      pl.BlockSpec((TILE, CH, LANES), far_map), pl.BlockSpec((TILE, CH, COLS), lambda i, sc: (i, 0, 0)),
+            in_specs=[pl.BlockSpec((1, tile, CH, COLS), lambda i, sc: (sc[1], i, 0, 0)),
+                      pl.BlockSpec((1, tile, CH, LANES), lambda i, sc: (sc[2], i, 0, 0)),
+                      pl.BlockSpec((tile, CH, LANES), far_map), pl.BlockSpec((tile, CH, COLS), lambda i, sc: (i, 0, 0)),
                       *[pl.BlockSpec((4 * blocks, CH, COLS), lambda i, sc: (FAR_BIAS // (4 * blocks), 0, 0))] * (blocks > 0),
                       VM, VM, VM],
             out_specs=[HB] + [pl.BlockSpec((blocks + 1, 4, ROWS, COLS), lambda i, sc: (0, 0, 0, 0))] * (blocks > 0),
-            scratch_shapes=[pltpu.VMEM((TILE, 8, COLS), F32), pltpu.VMEM((TILE, CH, COLS), F32),
-                            pltpu.VMEM((2, TILE, CH, COLS), F32), DMA2]),
+            scratch_shapes=[pltpu.VMEM((tile, 8, COLS), F32), pltpu.VMEM((tile, CH, COLS), F32),
+                            pltpu.VMEM((2, tile, CH, COLS), F32), DMA2]),
         compiler_params=PARAMS,
         name="row_updates",
     )(sc, zt, x_near, x_far, xi, *[xi] * (blocks > 0), norms, w_sq, w_bias)
@@ -441,8 +447,12 @@
 CHUNK = 32
 SLOTS = 2
 STEPS = 6
-AWAY_FIRST = 28
+AWAY_FIRST = 26
 HEAD_ROWS = 8
+
+
+def mask_rows(size):
+    return pl.cdiv(size, SUB) * SUB
 
 
 def attention_kernel(parts, fresh, away, sc, *refs):
@@ -456,12 +466,6 @@
     n_rows = sum(size for _, size, _ in parts)
     att_norm = norm_of(norms, 0)
 
-    def rows_of(j):
-        return pl.ds(ROWS * j, parts[j][1])
-
-    def own(ref, j):
-        return ref.at[sc[j], pl.ds(*parts[j][:2])]
-
     def z_copy(j):
         start = 0 if j else HEAD_ROWS
         size = parts[j][1] - start
@@ -471,8 +475,9 @@
         return pltpu.make_async_copy(z_refs[0].at[pl.ds(0, HEAD_ROWS)], z_in.at[pl.ds(0, HEAD_ROWS)], z_sem.at[n])
 
     def m_copy(j):
-        src = mask_away.at[0] if away and j == n - 1 else own(mask_in, j)
-        return pltpu.make_async_copy(src, mask_i.at[rows_of(j)], m_sem.at[j])
+        size = mask_rows(parts[j][1])
+        src = mask_away.at[0] if away and j == n - 1 else mask_in.at[sc[j], pl.ds(parts[j][0], size)]
+        return pltpu.make_async_copy(src, mask_i.at[pl.ds(ROWS * j, size)], m_sem.at[j])
 
     def b_copy(j, r):
         rows = pl.ds(pl.multiple_of(ROWS * (sc[n + j] ^ r), ROWS), ROWS)
@@ -518,12 +523,12 @@
         keep_s[slot] = jnp.broadcast_to(mask[pl.ds(row, 1), :], (LANES, COLS)).T
 
     def tall(line):
-        return jnp.concatenate([line] * (CHUNK // 8))
+        return jnp.concatenate([line] * (CHUNK // SUB))
 
     def fold(part, op):
-        out = part[:8]
-        for n in range(1, part.shape[0] // 8):
-            out = op(out, part[8 * n:8 * n + 8])
+        out = part[:SUB]
+        for n in range(1, part.shape[0] // SUB):
+            out = op(out, part[SUB * n:SUB * n + SUB])
         return out
 
     def scores(slot, h):
@@ -550,8 +555,8 @@
             s_buf[buf, rows] = vals
             part = fold(vals, jnp.maximum)
             top = part if top is None else jnp.maximum(top, part)
-        top_s[buf] = jnp.broadcast_to(jnp.max(top, axis=0, keepdims=True), (8, COLS))
-        inv_s[prev] = jnp.broadcast_to(1.0 / jnp.sum(total, axis=0, keepdims=True), (8, COLS))
+        top_s[buf] = jnp.broadcast_to(jnp.max(top, axis=0, keepdims=True), (SUB, COLS))
+        inv_s[prev] = jnp.broadcast_to(1.0 / jnp.sum(total, axis=0, keepdims=True), (SUB, COLS))
         if defer:
             p_s[:] = jnp.concatenate(probs)
         else:
@@ -610,7 +615,7 @@
     aways = [SDS((k, CH, COLS), F32) for k in (AWAY_FIRST, AWAY.shape[0] - AWAY_FIRST)] * away
     rows = sum(z.shape[0] for z in z_parts)
     pair, wide, square, line = [pltpu.VMEM((SLOTS, *shape), dtype) for shape, dtype in (
-        ((CH, COLS), BF16), ((CH, COLS), F32), ((COLS, COLS), F32), ((8, COLS), F32))]
+        ((CH, COLS), BF16), ((CH, COLS), F32), ((COLS, COLS), F32), ((SUB, COLS), F32))]
     each = [pltpu.VMEM((n, HEADS, COLS, COLS), dtype) for dtype in (BF16, F32)]
     sems, more = pltpu.SemaphoreType.DMA((n,)), pltpu.SemaphoreType.DMA((n + 1,))
     return pl.pallas_call(
@@ -619,8 +624,8 @@
         in_specs=[SM] + [HB] * (5 * n + 1) + [VM] * 3 + [HB] * (away + (not fresh)),
         out_specs=(HB,) * (1 + len(aways)),
         scratch_shapes=[
-            pltpu.VMEM((rows, CH, COLS), F32), pltpu.VMEM((rows + STEPS, CH, COLS), F32), pltpu.VMEM((rows, COLS), jnp.int32),
-            pltpu.VMEM((rows, COLS), F32), *each, pltpu.VMEM((SLOTS, HEADS, CH, COLS), BF16),
+            pltpu.VMEM((rows, CH, COLS), F32), pltpu.VMEM((rows + STEPS, CH, COLS), F32), pltpu.VMEM((mask_rows(rows), COLS), jnp.int32),
+            pltpu.VMEM((mask_rows(rows), COLS), F32), *each, pltpu.VMEM((SLOTS, HEADS, CH, COLS), BF16),
             pltpu.VMEM((SLOTS, COLS, CH), BF16), pair, wide, pair, wide, pltpu.VMEM((SLOTS, COLS, LANES), F32),
             square, square, pltpu.VMEM((COLS, COLS), BF16), line, line, wide, sems, more, sems, sems,
         ],
@@ -721,7 +726,7 @@
             held.append((two, three))
             if last:
                 out, *away = attention([own, (0, 0, far3[-1], here(bias), 0)], out,
-                                       masks[3][t][None, SOME:].astype(jnp.int32))
+                                       jnp.roll(masks[3][t], -SOME, axis=0)[None, :mask_rows(ROWS - SOME)].astype(jnp.int32))
                 away = [exchange(v, 3) for v in away]
             else:
                 out, = attention([own, near], out)

time: 1310 us -> 1310 us (level)
  transfers between devices with their start and end apart: 34 -> 34, of which waited for: 14 -> 16; matrix products, arithmetic and copies ran while one was open for 3% -> 3% of each run, Pallas kernels for 44% -> 44%
where the time goes in v4:
time: 1310 us; the launch traced here: 1300 us
  Pallas kernels  773 us (59%)
  waiting for transfers between devices  433 us (33%)
  local copies, waits for them, and re-layouts  59.3 us (5%)
  starting transfers between devices  25.5 us (2%)
    ppermute x34, waiting for transfers between devices, exchange(): return lax.ppermute(values, 'dap', [(i, i ^ r) for i in range(4)])  433 us
    pallas_call x7, Pallas kernels, attend(): pl.pallas_call(functools.partial(attention_kernel, static, fresh, away),...  389 us
    pallas_call x3, Pallas kernels, u_call(): pl.pallas_call(functools.partial(u_kernel, last, layout), out_shape=(ROW_...  262 us
    pallas_call x6, Pallas kernels, r_call(): pl.pallas_call(functools.partial(r_kernel, blocks), out_shape=[pltpu.HBM(...  60.1 us
    squeeze x6, local copies, waits for them, and re-layouts, local_block(): lax.dynamic_slice(lax.optimization_barrier((zt, *before))[0], where, (1,...  34.7 us
    pallas_call x1, Pallas kernels, l2_call(): pl.pallas_call(l2_kernel, grid=(n // 2,), out_shape=SDS((n, ROWS, CH, LAN...  33 us
    pallas_call x1, Pallas kernels, l1_call(): pl.pallas_call(l1_kernel, out_shape=(ab, ab), grid_spec=pltpu.PrefetchSca...  28.7 us
  transfers between devices with their start and end apart: 34, of which 16 were waited for; matrix products, arithmetic and copies ran while one was open for 3% of the time, Pallas kernels for 44%

profile of v4, /device:TPU:0, one launch (start us, length us, event | category | flops | bytes accessed | tf_op | source)
XLA Modules:
  0.0 1295.9 jit_solution(3766960424713107067)
XLA Ops:
  0.0 1.0 dynamic-slice_bitcast_fusion.9
  1.2 4.6 dynamic-slice_bitcast_fusion.8
  7.4 28.7 %near_projections.1 = (bf16[6,64,64,256]{3,2,1,0:T(8,128)(2,1)S(1)}, bf16[6,64,64,256]{3,2,1,0:T(8,128)(2,1)}) custom-call(s32[6]{0:T(128)S(1)} %stack.177.ids, f32[12,64,64,256]{3,2,1,0:T(8,128)} %bitcast.130, s32[12,64,256]{2,1,0:T(8,128)S(1)} %copy-done.2, f32[6,64,256]{2,1,0:T(8,128)S(1)} %broadcast_dynamic-update-slice_fusion.norms.refs_9_.refs_8_.refs_1_.refs_0_, ...), custom_call_target="tpu_custom_call" | custom-call | tf_op jit(solution)/shard_map/near_projections/pallas_call | solution.py:318
  36.1 4.6 copy-done.6
  40.7 0.8 collective-permute-start
  41.6 4.6 dynamic-slice_bitcast_fusion.7
  46.3 4.7 dynamic-slice_bitcast_fusion.6
  51.0 2.6 collective-permute-start.3
  54.0 1.5 collective-permute-start.7
  57.8 0.7 pad_maximum_fusion.3.refs_12_.refs_11_.refs_2_.refs_1_
  58.5 172.5 %collective-permute-done.7 = bf16[3,64,256]{2,1,0:T(8,128)(2,1)S(1)} collective-permute-done((bf16[3,64,256]{2,1,0:T(8,128)(2,1)S(1)}, bf16[3,64,256]{2,1,0:T(8,128)(2,1)S(1)}, u32[]{:S(2)}, u32[]{:S(2)}) %collective-permute-start.7) | collective-permute-done | bytes 98336 | tf_op jit(solution)/shard_map/ppermute | solution.py:642
  231.0 2.3 collective-permute-start.6
  233.8 2.5 collective-permute-done.6
  236.4 0.6 slice_bitcast_fusion
  237.0 0.7 collective-permute-done.5
  237.7 1.7 collective-permute-start.1
  240.7 33.0 %near_product.1.x_near = bf16[6,64,64,128]{3,2,1,0:T(8,128)(2,1)S(1)} custom-call(s32[1]{0:T(128)} %bitcast.1.sc, bf16[6,64,64,256]{3,2,1,0:T(8,128)(2,1)} %copy-done.6, bf16[6,64,64,256]{3,2,1,0:T(8,128)(2,1)} %get-tuple-element.103.b_own, bf16[6,64,64,256]{3,2,1,0:T(8,128)(2,1)} %collective-permute-done.b_par, ...), custom_call_target="tpu_custom_call" | custom-call | tf_op jit(solution)/shard_map/near_product/pallas_call | solution.py:354
  273.7 2.6 copy-done
  276.3 0.7 copy-done.27
  277.0 87.6 %pair_updates.3 = (f32[64,64,256]{2,1,0:T(8,128)}, f32[64,64,256]{2,1,0:T(8,128)}, bf16[4,4,64,256]{3,2,1,0:T(8,128)(2,1)}, bf16[100,64,256]{2,1,0:T(8,128)(2,1)}, bf16[100,64,256]{2,1,0:T(8,128)(2,1)}) custom-call(s32[2]{0:T(128)} %pad_add_fusion.14.sc, f32[12,64,64,256]{3,2,1,0:T(8,128)} %bitcast.133, f32[4,64,256]{2,1,0:T(8,128)} %copy-done.27, ...), custom_call_target="tpu_custom_call" | custom-call | tf_op jit(solution)/shard_map/pair_updates/pallas_call | solution.py:283
  364.7 9.8 dynamic-slice_bitcast_fusion.3
  374.5 1.8 collective-permute-start.11
  378.2 6.2 collective-permute-done.9.refs_6_.refs_7_.refs_8_.refs_9_
  384.5 0.8 copy-done.19
  385.2 64.1 %triangle_attention.7.refs_14_ = f32[12,64,64,256]{3,2,1,0:T(8,128)} custom-call(s32[4]{0:T(128)S(1)} %get-tuple-element.120.sc, f32[64,64,256]{2,1,0:T(8,128)} %get-tuple-element.121.refs_0_, f32[64,64,256]{2,1,0:T(8,128)} %collective-permute-done.8.refs_1_, bf16[4,4,64,256]{3,2,1,0:T(8,128)(2,1)} %get-tuple-element.123.refs_2_.refs_3_.refs_4_.refs_5_, ...), custom_call_target="tpu_custom_call" | custom-call | tf_op jit(solution)/shard_map/triangle_attention/pallas_call | solution.py:621
  449.3 18.9 %collective-permute-done.10.refs_1_ = f32[64,64,256]{2,1,0:T(8,128)} collective-permute-done((f32[64,64,256]{2,1,0:T(8,128)}, f32[64,64,256]{2,1,0:T(8,128)}, u32[]{:S(2)}, u32[]{:S(2)}) %collective-permute-start.10) | collective-permute-done | bytes 4194336 | tf_op jit(solution)/shard_map/ppermute | solution.py:642
  468.3 88.8 %collective-permute-done.11.refs_2_ = f32[64,64,256]{2,1,0:T(8,128)} collective-permute-done((f32[64,64,256]{2,1,0:T(8,128)}, f32[64,64,256]{2,1,0:T(8,128)}, u32[]{:S(2)}, u32[]{:S(2)}) %collective-permute-start.11) | collective-permute-done | bytes 4194336 | tf_op jit(solution)/shard_map/ppermute | solution.py:642
  557.1 87.6 %pair_updates.4 = (f32[64,64,256]{2,1,0:T(8,128)}, f32[64,64,256]{2,1,0:T(8,128)}, bf16[4,4,64,256]{3,2,1,0:T(8,128)(2,1)}, bf16[100,64,256]{2,1,0:T(8,128)(2,1)}, bf16[100,64,256]{2,1,0:T(8,128)(2,1)}) custom-call(s32[2]{0:T(128)} %pad_add_fusion.13.sc, f32[12,64,64,256]{3,2,1,0:T(8,128)} %bitcast.135, f32[64,64,256]{2,1,0:T(8,128)} %collective-permute-done.10.refs_1_, ...), custom_call_target="tpu_custom_call" | custom-call | tf_op jit(solution)/shard_map/pair_updates/pallas_call | solution.py:283
  645.1 9.8 dynamic-slice_bitcast_fusion
  655.0 1.5 collective-permute-start.16
  656.5 0.6 collective-permute-start.17
  657.1 7.5 collective-permute-done.14.refs_6_.refs_7_.refs_8_.refs_9_
  664.9 1.5 collective-permute-start.19
  667.0 64.1 %triangle_attention.8.refs_15_ = f32[12,64,64,256]{3,2,1,0:T(8,128)} custom-call(s32[4]{0:T(128)S(1)} %get-tuple-element.132.sc, f32[64,64,256]{2,1,0:T(8,128)} %get-tuple-element.133.refs_0_, f32[64,64,256]{2,1,0:T(8,128)} %collective-permute-done.13.refs_1_, ...), custom_call_target="tpu_custom_call", output_to_operand_aliasing={{}: (15, {})} | custom-call | tf_op jit(solution)/shard_map/triangle_attention/pallas_call | solution.py:621
  731.1 17.6 %collective-permute-done.15.refs_1_ = f32[64,64,256]{2,1,0:T(8,128)} collective-permute-done((f32[64,64,256]{2,1,0:T(8,128)}, f32[64,64,256]{2,1,0:T(8,128)}, u32[]{:S(2)}, u32[]{:S(2)}) %collective-permute-start.15) | collective-permute-done | bytes 4194336 | tf_op jit(solution)/shard_map/ppermute | solution.py:642
  748.7 88.2 %collective-permute-done.16.refs_2_ = f32[64,64,256]{2,1,0:T(8,128)} collective-permute-done((f32[64,64,256]{2,1,0:T(8,128)}, f32[64,64,256]{2,1,0:T(8,128)}, u32[]{:S(2)}, u32[]{:S(2)}) %collective-permute-start.16) | collective-permute-done | bytes 4194336 | tf_op jit(solution)/shard_map/ppermute | solution.py:642
  837.0 87.2 %pair_updates.5 = (f32[64,64,256]{2,1,0:T(8,128)}, f32[64,64,256]{2,1,0:T(8,128)}, bf16[4,4,64,256]{3,2,1,0:T(8,128)(2,1)}, bf16[108,64,256]{2,1,0:T(8,128)(2,1)...) custom-call(s32[2]{0:T(128)} %pad_add_fusion.12.sc, ...), custom_call_target="tpu_custom_call" | custom-call | tf_op jit(solution)/shard_map/pair_updates/pallas_call | solution.py:283
  924.2 2.0 collective-permute-start.20
  926.2 1.4 collective-permute-start.25
  927.6 0.6 collective-permute-start.28
  928.5 48.5 %triangle_attention.9 = (f32[12,64,64,256]{3,2,1,0:T(8,128)}, f32[26,64,256]{2,1,0:T(8,128)}, f32[4,64,256]{2,1,0:T(8,128)S(1)}) custom-call(s32[4]{0:T(128)S(1)} %get-tuple-element.139.sc, f32[64,64,256]{2,1,0:T(8,128)} %get-tuple-element.140.refs_0_, f32[30,64,256]{2,1,0:T(8,128)} %get-tuple-element.138.refs_1_, ...), custom_call_target="tpu_custom_call", output_to_operand_aliasing={{0}: (16, {})} | custom-call | tf_op jit(solution)/shard_map/triangle_attention/pallas_call | solution.py:621
  977.1 2.9 copy-done.1
  979.9 11.0 row_updates.6
  991.0 10.9 row_updates.7
  1002.1 1.6 collective-permute-done.22.refs_8_.refs_10_
  1003.9 1.4 collective-permute-done.23.refs_12_.refs_14_
  1005.4 1.8 collective-permute-done.21.refs_3_.refs_4_.refs_5_.refs_6_
  1007.2 0.8 copy-done.18
  1008.0 1.5 collective-permute-start.32
  1011.1 95.5 %triangle_attention.10.refs_14_ = f32[12,64,64,256]{3,2,1,0:T(8,128)} custom-call(s32[6]{0:T(128)S(1)} %copy-done.11, f32[64,64,256]{2,1,0:T(8,128)} %collective-permute-done.20.refs_0_, f32[64,64,256]{2,1,0:T(8,128)} %get-tuple-element.150.refs_1_, f32[64,64,256]{2,1,0:T(8,128)} %get-tuple-element.151.refs_2_, ...), custom_call_target="tpu_custom_call", output_to_operand_aliasing={{}: (20, {})} | custom-call | tf_op jit(solution)/shard_map/triangle_attention/pallas_call | solution.py:621
  1106.7 10.7 row_updates.8
  1117.9 10.6 row_updates.9
  1128.5 1.5 collective-permute-start.26
  1130.1 1.3 collective-permute-done.26.refs_3_.refs_5_
  1132.4 64.1 %triangle_attention.11.refs_9_ = f32[12,64,64,256]{3,2,1,0:T(8,128)} custom-call(s32[4]{0:T(128)S(1)} %pad_add_fusion.7.sc, f32[64,64,256]{2,1,0:T(8,128)} %get-tuple-element.159.refs_0_, f32[64,64,256]{2,1,0:T(8,128)} %get-tuple-element.160.refs_1_, bf16[2,4,64,256]{3,2,1,0:T(8,128)(2,1)} %get-tuple-element.155.refs_2_.refs_4_, ...), custom_call_target="tpu_custom_call", output_to_operand_aliasing={{}: (15, {})} | custom-call | tf_op jit(solution)/shard_map/triangle_attention/pallas_call | solution.py:621
  1196.6 10.9 row_updates.10
  1208.1 1.4 collective-permute-start.33
  1209.6 32.9 %triangle_attention.12.refs_9_ = f32[12,64,64,256]{3,2,1,0:T(8,128)} custom-call(s32[2]{0:T(128)S(1)} %pad_add_fusion.5.sc, f32[64,64,256]{2,1,0:T(8,128)} %get-tuple-element.165.refs_0_, bf16[4,4,64,256]{3,2,1,0:T(8,128)(2,1)} %get-tuple-element.163.refs_1_.refs_2_.refs_3_.refs_4_, ...), custom_call_target="tpu_custom_call", output_to_operand_aliasing={{}: (10, {})} | custom-call | tf_op jit(solution)/shard_map/triangle_attention/pallas_call | solution.py:621
  1242.5 23.4 %collective-permute-done.29.x_far = bf16[34,64,128]{2,1,0:T(8,128)(2,1)S(1)} collective-permute-done((bf16[34,64,128]{2,1,0:T(8,128)(2,1)S(1)}, bf16[34,64,128]{2,1,0:T(8,128)(2,1)S(1)}, u32[]{:S(2)}, u32[]{:S(2)}) %collective-permute-start.29) | collective-permute-done | bytes 557088 | tf_op jit(solution)/shard_map/ppermute | solution.py:642
  1265.9 5.9 row_updates.11.refs_0_
  1271.9 0.8 copy-done.17
  1272.7 19.5 %triangle_attention.13 = f32[12,64,64,256]{3,2,1,0:T(8,128)} custom-call(s32[2]{0:T(128)S(1)} %pad_add_fusion.3.sc, f32[34,64,256]{2,1,0:T(8,128)} %row_updates.11.refs_0_, bf16[4,4,64,256]{3,2,1,0:T(8,128)(2,1)} %copy-done.17, bf16[4,4,64,256]{3,2,1,0:T(8,128)(2,1)} %copy-done.17, ...), custom_call_target="tpu_custom_call", output_to_operand_aliasing={{}: (10, {})} | custom-call | tf_op jit(solution)/shard_map/triangle_attention/pallas_call | solution.py:621
  1292.2 2.8 bitcast_dynamic-update-slice_fusion
  1295.0 0.7 bitcast_dynamic-update-slice_fusion.1
  (213 shorter events, 13.7 us)
Async XLA Ops:
  6.9 29.2 %copy-start.8 = (bf16[2,256,64]{2,1,0:T(8,128)(2,1)}, bf16[2,256,64]{2,1,0:T(8,128)(2,1)S(1)}, u32[]{:S(2)}) copy-start(bf16[2,256,64]{2,1,0:T(8,128)(2,1)S(1)} %pad_maximum_fusion.1.w_ab.refs_11_.refs_10_) | copy-start | bytes 196612
  7.3 28.8 %copy-start.3 = (f32[6,64,256]{2,1,0:T(8,128)}, f32[6,64,256]{2,1,0:T(8,128)S(1)}, u32[]{:S(2)}) copy-start(f32[6,64,256]{2,1,0:T(8,128)S(1)} %broadcast_dynamic-update-slice_fusion.norms.refs_9_.refs_8_.refs_1_.refs_0_) | copy-start | bytes 1179652
  40.7 199.9 %collective-permute-start = (bf16[6,64,64,256]{3,2,1,0:T(8,128)(2,1)}, bf16[6,64,64,256]{3,2,1,0:T(8,128)(2,1)}, u32[]{:S(2)}, u32[]{:S(2)}) collective-permute-start(bf16[6,64,64,256]{3,2,1,0:T(8,128)(2,1)} %get-tuple-element.103.b_own), channel_id=1, source_target_pairs={{0,1},{1,0},{2,3},{3,2},{4,5},{5,4},{6,7},{7,6}} | collective-permute-start | bytes 37748744 | tf_op jit(solution)/shard_map/ppermute | solution.py:642
  46.2 9.3 copy-start.37
  46.2 9.4 copy-start.38
  46.2 9.6 copy-start.39
  46.3 9.7 copy-start.47
  46.3 10.9 copy-start.52
  46.3 11.0 copy-start.53
  46.3 11.1 copy-start.54
  46.3 11.2 copy-start.55
  51.0 225.3 %collective-permute-start.4 = (f32[64,64,256]{2,1,0:T(8,128)}, f32[64,64,256]{2,1,0:T(8,128)}, u32[]{:S(2)}, u32[]{:S(2)}) collective-permute-start(f32[64,64,256]{2,1,0:T(8,128)} %dynamic-slice_bitcast_fusion.6), channel_id=1, source_target_pairs={{0,1},{1,0},{2,3},{3,2},{4,5},{5,4},{6,7},{7,6}} | collective-permute-start | bytes 12582920 | tf_op jit(solution)/shard_map/ppermute | solution.py:642
  51.0 225.3 %collective-permute-start.3 = (f32[64,64,256]{2,1,0:T(8,128)}, f32[64,64,256]{2,1,0:T(8,128)}, u32[]{:S(2)}, u32[]{:S(2)}) collective-permute-start(f32[64,64,256]{2,1,0:T(8,128)} %dynamic-slice_bitcast_fusion.7), channel_id=1, source_target_pairs={{0,3},{1,2},{2,1},{3,0},{4,7},{5,6},{6,5},{7,4}} | collective-permute-start | bytes 12582920 | tf_op jit(solution)/shard_map/ppermute | solution.py:642
  53.6 222.7 %collective-permute-start.2 = (f32[60,64,256]{2,1,0:T(8,128)}, f32[60,64,256]{2,1,0:T(8,128)}, u32[]{:S(2)}, u32[]{:S(2)}) collective-permute-start(f32[60,64,256]{2,1,0:T(8,128)} %dynamic-slice_bitcast_fusion.8), channel_id=1, source_target_pairs={{0,2},{1,3},{2,0},{3,1},{4,6},{5,7},{6,4},{7,5}} | collective-permute-start | bytes 11796488 | tf_op jit(solution)/shard_map/ppermute | solution.py:642
  54.0 177.0 %collective-permute-start.7 = (bf16[3,64,256]{2,1,0:T(8,128)(2,1)S(1)}, bf16[3,64,256]{2,1,0:T(8,128)(2,1)S(1)}, u32[]{:S(2)}, u32[]{:S(2)}) collective-permute-start(bf16[3,64,256]{2,1,0:T(8,128)(2,1)S(1)} %get-tuple-element.180), channel_id=1, source_target_pairs={{0,3},{1,2},{2,1},{3,0},{4,7},{5,6},{6,5},{7,4}} | collective-permute-start | bytes 294920 | tf_op jit(solution)/shard_map/ppermute | solution.py:642
  57.8 216.0 %copy-start.5 = (f32[4,64,8,128]{3,2,1,0:T(8,128)}, f32[4,64,8,128]{3,2,1,0:T(8,128)S(1)}, u32[]{:S(2)}) copy-start(f32[4,64,8,128]{3,2,1,0:T(8,128)S(1)} %pad_maximum_fusion.xgs.refs_10_.refs_9_) | copy-start | bytes 3145732
  231.0 5.4 collective-permute-start.6
  236.4 1.3 collective-permute-start.5
  237.7 38.6 %collective-permute-start.1 = (f32[4,64,256]{2,1,0:T(8,128)S(1)}, f32[4,64,256]{2,1,0:T(8,128)S(1)}, u32[]{:S(2)}, u32[]{:S(2)}) collective-permute-start(f32[4,64,256]{2,1,0:T(8,128)S(1)} %dynamic-slice_bitcast_fusion.9), channel_id=1, source_target_pairs={{0,2},{1,3},{2,0},{3,1},{4,6},{5,7},{6,4},{7,5}} | collective-permute-start | bytes 786440 | tf_op jit(solution)/shard_map/ppermute | solution.py:642
  364.6 12.1 copy-start.40
  364.6 12.1 copy-start.41
  364.6 12.2 copy-start.42
  364.7 12.3 copy-start.43
  364.7 12.4 copy-start.44
  364.7 12.6 copy-start.16
  364.7 19.8 %collective-permute-start.8 = (f32[64,64,256]{2,1,0:T(8,128)}, f32[64,64,256]{2,1,0:T(8,128)}, u32[]{:S(2)}, u32[]{:S(2)}) collective-permute-start(f32[64,64,256]{2,1,0:T(8,128)} %get-tuple-element.122), channel_id=1, source_target_pairs={{0,1},{1,0},{2,3},{3,2},{4,5},{5,4},{6,7},{7,6}} | collective-permute-start | bytes 12582920 | tf_op jit(solution)/shard_map/ppermute | solution.py:642
  374.5 93.8 %collective-permute-start.10 = (f32[64,64,256]{2,1,0:T(8,128)}, f32[64,64,256]{2,1,0:T(8,128)}, u32[]{:S(2)}, u32[]{:S(2)}) collective-permute-start(f32[64,64,256]{2,1,0:T(8,128)} %get-tuple-element.176), channel_id=1, source_target_pairs={{0,2},{1,3},{2,0},{3,1},{4,6},{5,7},{6,4},{7,5}} | collective-permute-start | bytes 12582920 | tf_op jit(solution)/shard_map/ppermute | solution.py:642
  374.5 182.6 %collective-permute-start.11 = (f32[64,64,256]{2,1,0:T(8,128)}, f32[64,64,256]{2,1,0:T(8,128)}, u32[]{:S(2)}, u32[]{:S(2)}) collective-permute-start(f32[64,64,256]{2,1,0:T(8,128)} %get-tuple-element.175), channel_id=1, source_target_pairs={{0,3},{1,2},{2,1},{3,0},{4,7},{5,6},{6,5},{7,4}} | collective-permute-start | bytes 12582920 | tf_op jit(solution)/shard_map/ppermute | solution.py:642
  376.3 180.8 %collective-permute-start.12 = (f32[64,64,256]{2,1,0:T(8,128)}, f32[64,64,256]{2,1,0:T(8,128)}, u32[]{:S(2)}, u32[]{:S(2)}) collective-permute-start(f32[64,64,256]{2,1,0:T(8,128)} %get-tuple-element.174), channel_id=1, source_target_pairs={{0,1},{1,0},{2,3},{3,2},{4,5},{5,4},{6,7},{7,6}} | collective-permute-start | bytes 12582920 | tf_op jit(solution)/shard_map/ppermute | solution.py:642
  377.3 7.2 collective-permute-start.9
  644.7 20.2 %collective-permute-start.13 = (f32[64,64,256]{2,1,0:T(8,128)}, f32[64,64,256]{2,1,0:T(8,128)}, u32[]{:S(2)}, u32[]{:S(2)}) collective-permute-start(f32[64,64,256]{2,1,0:T(8,128)} %get-tuple-element.134), channel_id=1, source_target_pairs={{0,1},{1,0},{2,3},{3,2},{4,5},{5,4},{6,7},{7,6}} | collective-permute-start | bytes 12582920 | tf_op jit(solution)/shard_map/ppermute | solution.py:642
  645.1 12.0 copy-start.15
  655.0 93.8 %collective-permute-start.15 = (f32[64,64,256]{2,1,0:T(8,128)}, f32[64,64,256]{2,1,0:T(8,128)}, u32[]{:S(2)}, u32[]{:S(2)}) collective-permute-start(f32[64,64,256]{2,1,0:T(8,128)} %get-tuple-element.173), channel_id=1, source_target_pairs={{0,2},{1,3},{2,0},{3,1},{4,6},{5,7},{6,4},{7,5}} | collective-permute-start | bytes 12582920 | tf_op jit(solution)/shard_map/ppermute | solution.py:642
  655.0 182.0 %collective-permute-start.16 = (f32[64,64,256]{2,1,0:T(8,128)}, f32[64,64,256]{2,1,0:T(8,128)}, u32[]{:S(2)}, u32[]{:S(2)}) collective-permute-start(f32[64,64,256]{2,1,0:T(8,128)} %get-tuple-element.172), channel_id=1, source_target_pairs={{0,3},{1,2},{2,1},{3,0},{4,7},{5,6},{6,5},{7,4}} | collective-permute-start | bytes 12582920 | tf_op jit(solution)/shard_map/ppermute | solution.py:642
  656.5 180.5 %collective-permute-start.17 = (f32[64,64,256]{2,1,0:T(8,128)S(1)}, f32[64,64,256]{2,1,0:T(8,128)}, u32[]{:S(2)}, u32[]{:S(2)}) collective-permute-start(f32[64,64,256]{2,1,0:T(8,128)S(1)} %get-tuple-element.171), channel_id=1, source_target_pairs={{0,1},{1,0},{2,3},{3,2},{4,5},{5,4},{6,7},{7,6}} | collective-permute-start | bytes 12582920 | tf_op jit(solution)/shard_map/ppermute | solution.py:642
  657.1 7.5 collective-permute-start.14
  664.6 263.0 %collective-permute-start.18 = (bf16[100,64,256]{2,1,0:T(8,128)(2,1)}, bf16[100,64,256]{2,1,0:T(8,128)(2,1)}, u32[]{:S(2)}, u32[]{:S(2)}) collective-permute-start(bf16[100,64,256]{2,1,0:T(8,128)(2,1)} %get-tuple-element.144), channel_id=1, source_target_pairs={{0,2},{1,3},{2,0},{3,1},{4,6},{5,7},{6,4},{7,5}} | collective-permute-start | bytes 9830408 | tf_op jit(solution)/shard_map/ppermute | solution.py:642
  664.9 326.1 %collective-permute-start.19 = (bf16[100,64,256]{2,1,0:T(8,128)(2,1)}, bf16[100,64,256]{2,1,0:T(8,128)(2,1)}, u32[]{:S(2)}, u32[]{:S(2)}) collective-permute-start(bf16[100,64,256]{2,1,0:T(8,128)(2,1)} %get-tuple-element.119), channel_id=1, source_target_pairs={{0,3},{1,2},{2,1},{3,0},{4,7},{5,6},{6,5},{7,4}} | collective-permute-start | bytes 9830408 | tf_op jit(solution)/shard_map/ppermute | solution.py:642
  924.2 85.8 %collective-permute-start.20 = (f32[64,64,256]{2,1,0:T(8,128)}, f32[64,64,256]{2,1,0:T(8,128)}, u32[]{:S(2)}, u32[]{:S(2)}) collective-permute-start(f32[64,64,256]{2,1,0:T(8,128)} %get-tuple-element.149), channel_id=1, source_target_pairs={{0,1},{1,0},{2,3},{3,2},{4,5},{5,4},{6,7},{7,6}} | collective-permute-start | bytes 12582920 | tf_op jit(solution)/shard_map/ppermute | solution.py:642
  926.2 180.4 %collective-permute-start.24 = (bf16[100,64,256]{2,1,0:T(8,128)(2,1)}, bf16[100,64,256]{2,1,0:T(8,128)(2,1)}, u32[]{:S(2)}, u32[]{:S(2)}) collective-permute-start(bf16[100,64,256]{2,1,0:T(8,128)(2,1)} %get-tuple-element.154), channel_id=1, source_target_pairs={{0,2},{1,3},{2,0},{3,1},{4,6},{5,7},{6,4},{7,5}} | collective-permute-start | bytes 9830408 | tf_op jit(solution)/shard_map/ppermute | solution.py:642
  926.2 191.6 %collective-permute-start.25 = (bf16[100,64,256]{2,1,0:T(8,128)(2,1)}, bf16[100,64,256]{2,1,0:T(8,128)(2,1)}, u32[]{:S(2)}, u32[]{:S(2)}) collective-permute-start(bf16[100,64,256]{2,1,0:T(8,128)(2,1)} %get-tuple-element.131), channel_id=1, source_target_pairs={{0,3},{1,2},{2,1},{3,0},{4,7},{5,6},{6,5},{7,4}} | collective-permute-start | bytes 9830408 | tf_op jit(solution)/shard_map/ppermute | solution.py:642
  927.6 268.9 %collective-permute-start.28 = (bf16[108,64,256]{2,1,0:T(8,128)(2,1)}, bf16[108,64,256]{2,1,0:T(8,128)(2,1)}, u32[]{:S(2)}, u32[]{:S(2)}) collective-permute-start(bf16[108,64,256]{2,1,0:T(8,128)(2,1)} %get-tuple-element.162), channel_id=1, source_target_pairs={{0,2},{1,3},{2,0},{3,1},{4,6},{5,7},{6,4},{7,5}} | collective-permute-start | bytes 10616840 | tf_op jit(solution)/shard_map/ppermute | solution.py:642
  928.4 48.6 %copy-start.4 = (f32[6,64,256]{2,1,0:T(8,128)S(1)}, f32[6,64,256]{2,1,0:T(8,128)}, u32[]{:S(2)}) copy-start(f32[6,64,256]{2,1,0:T(8,128)} %copy-done.3) | copy-start | bytes 1179652
  928.5 48.6 %copy-start.7 = (bf16[4,64,64]{2,1,0:T(8,128)(2,1)S(1)}, bf16[4,64,64]{2,1,0:T(8,128)(2,1)}, u32[]{:S(2)}) copy-start(bf16[4,64,64]{2,1,0:T(8,128)(2,1)} %pad_maximum_fusion.3.refs_12_.refs_11_.refs_2_.refs_1_) | copy-start | bytes 98308
  928.5 48.6 %copy-start.9 = (bf16[8,64]{1,0:T(8,128)(2,1)S(1)}, bf16[8,64]{1,0:T(8,128)(2,1)}, u32[]{:S(2)}) copy-start(bf16[8,64]{1,0:T(8,128)(2,1)} %concatenate.57.refs_13_.refs_12_.refs_3_.refs_2_) | copy-start | bytes 3076
  977.0 14.0 %copy-start.12 = (f32[4,64,256]{2,1,0:T(8,128)}, f32[4,64,256]{2,1,0:T(8,128)S(1)}, u32[]{:S(2)}) copy-start(f32[4,64,256]{2,1,0:T(8,128)S(1)} %get-tuple-element.142) | copy-start | bytes 786436
  991.0 12.7 copy-start.21
  991.0 14.3 %copy-start.14 = (bf16[4,4,64,256]{3,2,1,0:T(8,128)(2,1)S(1)}, bf16[4,4,64,256]{3,2,1,0:T(8,128)(2,1)}, u32[]{:S(2)}) copy-start(bf16[4,4,64,256]{3,2,1,0:T(8,128)(2,1)} %get-tuple-element.141.refs_2_.refs_3_.refs_4_.refs_5_.refs_6_.refs_7_.refs_8_.refs_9_) | copy-start | bytes 1572868
  991.0 115.6 %slice-start = ((s8[6291456]{0:T(1024)(128)(4,1)}), s8[2097152]{0:T(1024)(128)(4,1)S(1)}, s32[]{:S(2)}) async-start(s8[6291456]{0:T(1024)(128)(4,1)} %bitcast.119), calls=%async_computation | async-start | bytes 4194304
  1002.0 1.8 collective-permute-start.22
  1003.7 1.5 collective-permute-start.23
  1005.3 1.9 collective-permute-start.21
  1008.0 284.2 %collective-permute-start.32 = (f32[26,64,256]{2,1,0:T(8,128)}, f32[26,64,256]{2,1,0:T(8,128)}, u32[]{:S(2)}, u32[]{:S(2)}) collective-permute-start(f32[26,64,256]{2,1,0:T(8,128)} %get-tuple-element.170), channel_id=1, source_target_pairs={{0,3},{1,2},{2,1},{3,0},{4,7},{5,6},{6,5},{7,4}} | collective-permute-start | bytes 5111816 | tf_op jit(solution)/shard_map/ppermute | solution.py:642
  1010.1 255.9 %collective-permute-start.30 = (bf16[34,64,256]{2,1,0:T(8,128)(2,1)}, bf16[34,64,256]{2,1,0:T(8,128)(2,1)}, u32[]{:S(2)}, u32[]{:S(2)}) collective-permute-start(bf16[34,64,256]{2,1,0:T(8,128)(2,1)} %get-tuple-element.168), channel_id=1, source_target_pairs={{0,3},{1,2},{2,1},{3,0},{4,7},{5,6},{6,5},{7,4}} | collective-permute-start | bytes 3342344 | tf_op jit(solution)/shard_map/ppermute | solution.py:642
  1011.1 95.6 %slice-start.1 = ((s8[6291456]{0:T(1024)(128)(4,1)}), s8[4194304]{0:T(1024)(128)(4,1)S(1)}, s32[]{:S(2)}) async-start(s8[6291456]{0:T(1024)(128)(4,1)} %bitcast.119), calls=%async_computation.1 | async-start | bytes 8388608
  1011.1 95.6 %copy-start.10 = (bf16[8,64]{1,0:T(8,128)(2,1)S(1)}, bf16[8,64]{1,0:T(8,128)(2,1)}, u32[]{:S(2)}) copy-start(bf16[8,64]{1,0:T(8,128)(2,1)} %concatenate.57.refs_13_.refs_12_.refs_3_.refs_2_) | copy-start | bytes 3076
  1117.4 12.6 copy-start.24
  1117.4 14.0 %copy-start.56 = (bf16[34,64,128]{2,1,0:T(8,128)(2,1)S(1)}, bf16[34,64,128]{2,1,0:T(8,128)(2,1)}, u32[]{:S(2)}) copy-start(bf16[34,64,128]{2,1,0:T(8,128)(2,1)} %get-tuple-element.167) | copy-start | bytes 1671172
  1128.5 2.9 collective-permute-start.26
  1130.0 1.7 collective-permute-start.27
  1131.4 134.6 %collective-permute-start.29 = (bf16[34,64,128]{2,1,0:T(8,128)(2,1)S(1)}, bf16[34,64,128]{2,1,0:T(8,128)(2,1)S(1)}, u32[]{:S(2)}, u32[]{:S(2)}) collective-permute-start(bf16[34,64,128]{2,1,0:T(8,128)(2,1)S(1)} %copy-done.56), channel_id=1, source_target_pairs={{0,3},{1,2},{2,1},{3,0},{4,7},{5,6},{6,5},{7,4}} | collective-permute-start | bytes 1671176 | tf_op jit(solution)/shard_map/ppermute | solution.py:642
  1196.5 11.6 copy-start.13
  1207.5 64.4 %collective-permute-start.31 = (bf16[4,4,64,256]{3,2,1,0:T(8,128)(2,1)}, bf16[4,4,64,256]{3,2,1,0:T(8,128)(2,1)S(1)}, u32[]{:S(2)}, u32[]{:S(2)}) collective-permute-start(bf16[4,4,64,256]{3,2,1,0:T(8,128)(2,1)} %get-tuple-element.163.refs_1_.refs_2_.refs_3_.refs_4_), channel_id=1, source_target_pairs={{0,1},{1,0},{2,3},{3,2},{4,5},{5,4},{6,7},{7,6}} | collective-permute-start | bytes 1572872 | tf_op jit(solution)/shard_map/ppermute | solution.py:642
  1208.1 86.9 %collective-permute-start.33 = (f32[4,64,256]{2,1,0:T(8,128)S(1)}, f32[4,64,256]{2,1,0:T(8,128)S(1)}, u32[]{:S(2)}, u32[]{:S(2)}) collective-permute-start(f32[4,64,256]{2,1,0:T(8,128)S(1)} %copy-done.13), channel_id=1, source_target_pairs={{0,3},{1,2},{2,1},{3,0},{4,7},{5,6},{6,5},{7,4}} | collective-permute-start | bytes 786440 | tf_op jit(solution)/shard_map/ppermute | solution.py:642
  (29 other events, 117.8 us)
